TPU v7x, 256 devices: a whole 4x4x8 slice. The times are simulated.
256 devices in a mesh: seq: 64 (over z_lo, x, y), tp: 4 (over z_hi, core).
Axes of the slice: x: 4, y: 4, z: 8 (z_hi: 2, z_lo: 4; z = z_hi * 4 + z_lo), core: 2. Of those that a mesh axis runs over, the one named last changes fastest.
Arguments:
- states: bfloat16 [64, 128, 2048], P('seq', None, 'tp'), may hold values from -60 to 60, as said below
- cotangent: bfloat16 [64, 128, 2048], P('seq', None, 'tp'), may hold values from -12 to 12, as said below
- wq: bfloat16 [2048, 2048], P(None, 'tp'), may hold values from -0.125 to 0.125
- wk: bfloat16 [2048, 512], P(None, 'tp'), may hold values from -0.125 to 0.125
- wv: bfloat16 [2048, 512], P(None, 'tp'), may hold values from -0.125 to 0.125
- wo: bfloat16 [2048, 2048], P('tp'), may hold values from -0.125 to 0.125
Outputs:
- gram: float32 [64, 64], P('seq')
Inputs may be any that keep to these rules, and one draw needn't show every extreme that they name: `states`: finite values. `cotangent`: finite values.
All inputs are finite; a program needn't handle non-finite values.
Results may differ from a plain program's by a relative error of at most 0.0025.
Values may be sent and summed in bfloat16 or wider, within the bound.
No kernel may reach another device: no remote copies, remote signals or barrier semaphores. Data moves between devices by JAX's collectives and lax.ppermute only.
A program may use at most 64 MiB of HBM per device.

v0:
```python
import jax
import jax.numpy as jnp
from jax import lax
from jax.sharding import Mesh
from jax.sharding import PartitionSpec as P

HEADS = 32
KV_HEADS = 8
HEAD_DIM = 64
TP = ("tp_0", "tp_1")


theta_base = 500000.0


def from_behind(block, axis, distance):
    devices = range(lax.axis_size(axis))
    route = [((i - distance) % len(devices), i) for i in devices]
    return lax.ppermute(block, axis, route)


def cut_along(value, dim, size):
    before, after = (value.shape[:dim], value.shape[dim + 1 :])
    return jnp.moveaxis(value.reshape(*before, size, -1, *after), dim, 0)


def joined_along(blocks, dim):
    blocks = jnp.moveaxis(blocks, 0, dim)
    dims = blocks.shape
    return blocks.reshape(*dims[:dim], dims[dim] * dims[dim + 1], *dims[dim + 2 :])


def moved_by_axis(blocks, axes, order):
    dims = [lax.axis_size(a) for a in axes]
    blocks = blocks.reshape(*dims, *blocks.shape[1:])
    for k in order:
        blocks = lax.all_to_all(blocks, axes[k], split_axis=k, concat_axis=k, tiled=True)
    return blocks.reshape(-1, *blocks.shape[len(axes) :])


def exchange_by_chip(value, groups, order, split_dim, concat_dim):
    size = lax.axis_size(groups[0]) * lax.axis_size(groups[1])
    blocks = cut_along(value, split_dim, size)
    return joined_along(moved_by_axis(blocks, groups, order), concat_dim)


def copy_for_each(value, axis):
    size = lax.axis_size(axis)
    return lax.all_to_all(
        jnp.broadcast_to(value[None], (size, *value.shape)), axis, 0, 0, tiled=True
    )


def of_everyone(value, axis):
    everything = copy_for_each(value, axis)
    return jnp.sum(everything, axis=0)


def in_one(arrays, axis):
    ends = [0]
    for a in arrays:
        ends.append(ends[-1] + a.size)
    total = of_everyone(jnp.concatenate([a.ravel() for a in arrays]), axis)
    return tuple((total[b:e].reshape(a.shape) for a, b, e in zip(arrays, ends, ends[1:])))


def collect(value, axis, dim):
    blocks = copy_for_each(value, axis)
    return joined_along(blocks, dim)


def rope_tables(length, head_dim):
    half_dim = head_dim // 2
    freqs_k = theta_base ** (-(jnp.arange(half_dim, dtype=jnp.float32) * 2.0 / head_dim))
    angles = jnp.arange(length, dtype=jnp.float32)[:, None] * freqs_k[None, :]
    angles = jnp.concatenate([angles, angles], axis=1)
    return (jnp.cos(angles)[:, None, :], jnp.sin(angles)[:, None, :])


def rotate(values_in, cos_table, sine_table):
    half_dim = values_in.shape[-1] // 2
    turned = jnp.concatenate([-values_in[..., half_dim:], values_in[..., :half_dim]], axis=-1)
    return values_in * cos_table + turned * sine_table


def attention_factors(states, cotangent, wq, wk, wv, wo):
    seq_dev, length, part_width = states.shape
    full_states, full_cot = (
        lax.all_gather(states, TP, axis=2, tiled=True),
        lax.all_gather(cotangent, TP, axis=2, tiled=True),
    )
    model_width = full_states.shape[2]
    tok_rows = seq_dev * length
    kv_local = wk.shape[1] // HEAD_DIM
    group_size = HEADS // KV_HEADS
    cos_table, sine_table = rope_tables(length, HEAD_DIM)
    flat_states = full_states.reshape(tok_rows, model_width)
    query_heads = jnp.dot(flat_states, wq, preferred_element_type=jnp.float32).reshape(
        seq_dev, length, kv_local * group_size, HEAD_DIM
    )
    query_heads = (
        rotate(query_heads, cos_table, sine_table)
        .astype(jnp.bfloat16)
        .reshape(seq_dev, length, kv_local, group_size, HEAD_DIM)
    )
    key_heads = jnp.dot(flat_states, wk, preferred_element_type=jnp.float32).reshape(
        seq_dev, length, kv_local, HEAD_DIM
    )
    key_heads = rotate(key_heads, cos_table, sine_table).astype(jnp.bfloat16)
    value_heads = (
        jnp.dot(flat_states, wv, preferred_element_type=jnp.float32)
        .astype(jnp.bfloat16)
        .reshape(seq_dev, length, kv_local, HEAD_DIM)
    )
    scores = jnp.einsum(
        "sqkgd,stkd->skgqt", query_heads, key_heads, preferred_element_type=jnp.float32
    ) * HEAD_DIM ** (-0.5)
    causal = jnp.arange(length)[:, None] >= jnp.arange(length)[None, :]
    scores = jnp.where(causal, scores, -jnp.inf)
    weights_bf = jax.nn.softmax(scores, axis=-1).astype(jnp.bfloat16)
    attended = (
        jnp.einsum("skgqt,stkd->sqkgd", weights_bf, value_heads, preferred_element_type=jnp.float32)
        .astype(jnp.bfloat16)
        .reshape(tok_rows, part_width)
    )
    grad_attended = (
        lax.dot_general(
            full_cot.reshape(tok_rows, model_width),
            wo,
            (((1,), (1,)), ((), ())),
            preferred_element_type=jnp.float32,
        )
        .astype(jnp.bfloat16)
        .reshape(seq_dev, length, kv_local, group_size, HEAD_DIM)
    )
    value_gradient = (
        jnp.einsum(
            "skgqt,sqkgd->stkd", weights_bf, grad_attended, preferred_element_type=jnp.float32
        )
        .astype(jnp.bfloat16)
        .reshape(tok_rows, kv_local * HEAD_DIM)
    )
    return jnp.concatenate(
        [
            states.reshape(tok_rows, part_width),
            attended,
            cotangent.reshape(tok_rows, part_width),
            value_gradient,
        ],
        axis=1,
    )


def whole_tile(left_whole, right_whole, begin_col, end_col):
    return lax.dot_general(
        left_whole[:, :, begin_col:end_col],
        right_whole[:, :, begin_col:end_col],
        (((0, 2), (0, 2)), ((), ())),
        preferred_element_type=jnp.float32,
    )


def entire_block(own_whole, visitor_whole, part_width, seq_dev, length):
    full_width = own_whole.shape[2]
    states_tile = whole_tile(own_whole, visitor_whole, 0, part_width)
    attended_tile = whole_tile(own_whole, visitor_whole, part_width, 2 * part_width)
    cot_tile = whole_tile(own_whole, visitor_whole, 2 * part_width, 3 * part_width)
    values_tile = whole_tile(own_whole, visitor_whole, 3 * part_width, full_width)
    product = states_tile * values_tile + attended_tile * cot_tile
    return product.reshape(seq_dev, length, seq_dev, length).sum(axis=(1, 3))


def record(totals, block, distance, me_index, n_seq, half_rotation):
    row_acc, col_acc = totals
    seq_dev = block.shape[0]
    distance = jnp.asarray(distance, jnp.int32)
    offset = (me_index + distance) % n_seq * seq_dev
    zero_at = jnp.zeros((), jnp.int32)
    row_on = jnp.where(distance < half_rotation, 1.0, 0.0).astype(jnp.float32)
    row_acc = lax.dynamic_update_slice(row_acc, block * row_on, (zero_at, offset))
    mirror_on = jnp.where((distance > 0) & (distance <= half_rotation), 1.0, 0.0).astype(
        jnp.float32
    )
    col_acc = lax.dynamic_update_slice(col_acc, block.T * mirror_on, (offset, zero_at))
    return (row_acc, col_acc)


def on_device(states, cotangent, wq, wk, wv, wo):
    seq_dev, length, part_width = states.shape
    own_rows = attention_factors(states, cotangent, wq, wk, wv, wo)
    n_seq = lax.axis_size("seq")
    half_rotation = n_seq // 2
    me_index = lax.axis_index("seq")
    totals = (
        jnp.zeros((seq_dev, n_seq * seq_dev), jnp.float32),
        jnp.zeros((n_seq * seq_dev, seq_dev), jnp.float32),
    )
    n_tp = lax.axis_size(TP)
    tp_index = lax.axis_index(TP)
    own_whole = lax.all_gather(own_rows[None], TP, axis=0, tiled=True)
    shifted_parts = [own_rows] + [
        from_behind(own_rows, "seq", -offset) for offset in range(1, n_tp)
    ]
    visitor = exchange_by_chip(jnp.stack(shifted_parts), ("tp_0", "tp_1"), (1, 0), 0, 0)
    turn_count = half_rotation // n_tp + 1

    def measure_whole(totals_in, visitor_rows, distance):
        in_range = jnp.where(distance <= half_rotation, 1.0, 0.0).astype(jnp.float32)
        block = entire_block(own_whole, visitor_rows, part_width, seq_dev, length) * in_range
        return record(totals_in, block, distance, me_index, n_seq, half_rotation)

    totals = measure_whole(totals, visitor, tp_index)

    def stride_turn(step_index, carried):
        visitor_rows, totals_in = carried
        visitor_rows = from_behind(visitor_rows, "seq", -n_tp)
        return (
            visitor_rows,
            measure_whole(totals_in, visitor_rows, tp_index + (step_index + 1) * n_tp),
        )

    visitor, totals = lax.fori_loop(0, turn_count - 1, stride_turn, (visitor, totals))
    row_acc, col_acc = in_one((totals[0], totals[1]), TP)
    mirrored = lax.all_to_all(col_acc, "seq", split_axis=0, concat_axis=1, tiled=True)
    kernel = row_acc + mirrored
    own_block = lax.dynamic_slice_in_dim(kernel, me_index * seq_dev, seq_dev, 1)
    own_diag = jnp.diagonal(own_block)
    all_diag = collect(own_diag, "seq", 0)
    return kernel / jnp.sqrt(own_diag[:, None] * all_diag[None, :])


def solution(mesh):
    split = Mesh(mesh.devices.reshape(mesh.shape["seq"], 2, 2), ("seq", "tp_0", "tp_1"))
    placed = (
        P("seq", None, TP),
        P("seq", None, TP),
        P(None, TP),
        P(None, TP),
        P(None, TP),
        P(TP, None),
    )
    return jax.shard_map(
        on_device, mesh=split, in_specs=placed, out_specs=P("seq", None), check_vma=False
    )
```

profile of v0, /device:TPU:1, one launch (start us, length us, event | category | flops | bytes accessed | tf_op | source)
XLA Modules:
  0.0 601.5 jit_solution(8476827043644769787)
XLA Ops:
  6.6 14.6 %all_gather.9 = bf16[1,128,2048]{2,1,0:T(8,128)(2,1)S(1)} all-gather(bf16[1,128,512]{2,1,0:T(8,128)(2,1)} %param.8), channel_id=1, replica_groups=mesh['seq'=64,'tp_0'=2,'tp_1'=2] {'tp_0','tp_1'}, dimensions={2}, use_global_device_ids=true | all-gather | bytes 655360 | tf_op jit(solution)/shard_map/all_gather | solution.py:89
  24.3 11.3 %all_gather.10 = bf16[1,128,2048]{2,1,0:T(8,128)(2,1)S(1)} all-gather(bf16[1,128,512]{2,1,0:T(8,128)(2,1)S(1)} %copy-done.1), channel_id=1, replica_groups=mesh['seq'=64,'tp_0'=2,'tp_1'=2] {'tp_0','tp_1'}, dimensions={2}, use_global_device_ids=true | all-gather | bytes 655360 | tf_op jit(solution)/shard_map/all_gather | solution.py:90
  39.4 6.9 %collective-permute-start.1 = (bf16[128,1664]{1,0:T(8,128)(2,1)}, bf16[128,1664]{1,0:T(8,128)(2,1)S(1)}, u32[]{:S(2)}, u32[]{:S(2)}) collective-permute-start(bf16[128,1664]{1,0:T(8,128)(2,1)} %get-tuple-element.200), channel_id=1, source_target_pairs={{4,0},{8,4},{12,8},{16,12},{20,16},{24,20},{28,24},{32,28},{36,32}... | collective-permute-start | bytes 1277960 | tf_op jit(solution)/shard_map/ppermute | solution.py:19
  47.6 10.6 %collective-permute-done.1 = bf16[128,1664]{1,0:T(8,128)(2,1)S(1)} collective-permute-done((bf16[128,1664]{1,0:T(8,128)(2,1)}, bf16[128,1664]{1,0:T(8,128)(2,1)S(1)}, u32[]{:S(2)}, u32[]{:S(2)}) %collective-permute-start.1) | collective-permute-done | bytes 426016 | tf_op jit(solution)/shard_map/ppermute | solution.py:19
  58.2 25.2 %collective-permute-done.2 = bf16[128,1664]{1,0:T(8,128)(2,1)S(1)} collective-permute-done((bf16[128,1664]{1,0:T(8,128)(2,1)}, bf16[128,1664]{1,0:T(8,128)(2,1)S(1)}, u32[]{:S(2)}, u32[]{:S(2)}) %collective-permute-start.2) | collective-permute-done | bytes 426016 | tf_op jit(solution)/shard_map/ppermute | solution.py:19
  83.4 12.2 %collective-permute-done.3 = bf16[128,1664]{1,0:T(8,128)(2,1)S(1)} collective-permute-done((bf16[128,1664]{1,0:T(8,128)(2,1)}, bf16[128,1664]{1,0:T(8,128)(2,1)S(1)}, u32[]{:S(2)}, u32[]{:S(2)}) %collective-permute-start.3) | collective-permute-done | bytes 426016 | tf_op jit(solution)/shard_map/ppermute | solution.py:19
  103.1 7.2 %all-to-all-start.1 = ((bf16[2,2,1,128,1664]{4,3,1,2,0:T(8,128)(2,1)}), bf16[2,2,1,128,1664]{4,3,1,2,0:T(8,128)(2,1)}, u32[]{:S(2)}, u32[]{:S(2)}) async-start(bf16[2,2,1,128,1664]{4,3,1,2,0:T(8,128)(2,1)} %copy.59), calls=%async_computation.1 | async-start | bytes 3407872 | tf_op jit(solution)/shard_map/all_to_all | solution.py:37
  110.3 24.3 %all-to-all-done.1 = bf16[2,2,1,128,1664]{4,3,1,2,0:T(8,128)(2,1)} async-done(((bf16[2,2,1,128,1664]{4,3,1,2,0:T(8,128)(2,1)}), bf16[2,2,1,128,1664]{4,3,1,2,0:T(8,128)(2,1)}, u32[]{:S(2)}, u32[]{:S(2)}) %all-to-all-start.1) | async-done | bytes 1703968 | tf_op jit(solution)/shard_map/all_to_all | solution.py:37
  141.9 386.1 %while.19 = (s32[]{:T(128)}, bf16[4,128,1664]{2,1,0:T(8,128)(2,1)}, f32[1,64]{1,0:T(1,128)S(1)}, f32[64,1]{0,1:T(1,128)S(1)}, bf16[4,128,1664]{2,1,0:T(8,128)(2,...) while((s32[]{:T(128)}, bf16[4,128,1664]{2,1,0:T(8,128)(2,1)}, ...), condition=%wide.region_5.6_spmd, body=%wide.region_3.5_spmd.sunk | while | flops 218169344 | bytes 14025197 | solution.py:222
  142.1 37.0 %collective-permute-done = bf16[4,128,1664]{2,1,0:T(8,128)(2,1)} collective-permute-done((bf16[4,128,1664]{2,1,0:T(8,128)(2,1)}, bf16[4,128,1664]{2,1,0:T(8,128)(2,1)}, u32[]{:S(2)}, u32[]{:S(2)}) %collective-permute-start) | collective-permute-done | bytes 1703968 | tf_op jit(solution)/shard_map/while/body/eval_jaxpr/ppermute | solution.py:19
  189.1 6.1 %collective-permute-start = (bf16[4,128,1664]{2,1,0:T(8,128)(2,1)}, bf16[4,128,1664]{2,1,0:T(8,128)(2,1)}, u32[]{:S(2)}, u32[]{:S(2)}) collective-permute-start(bf16[4,128,1664]{2,1,0:T(8,128)(2,1)} %get-tuple-element.268), channel_id=1, source_target_pairs={{16,0},{20,4},{24,8},{28,12},{32,16},{36,20},{40,24},{44,28},{48,3... | collective-permute-start | bytes 5111816 | tf_op jit(solution)/shard_map/while/body/eval_jaxpr/ppermute | solution.py:19
  195.2 26.5 %collective-permute-done = bf16[4,128,1664]{2,1,0:T(8,128)(2,1)} collective-permute-done((bf16[4,128,1664]{2,1,0:T(8,128)(2,1)}, bf16[4,128,1664]{2,1,0:T(8,128)(2,1)}, u32[]{:S(2)}, u32[]{:S(2)}) %collective-permute-start) | collective-permute-done | bytes 1703968 | tf_op jit(solution)/shard_map/while/body/eval_jaxpr/ppermute | solution.py:19
  237.8 25.7 %collective-permute-done = bf16[4,128,1664]{2,1,0:T(8,128)(2,1)} collective-permute-done((bf16[4,128,1664]{2,1,0:T(8,128)(2,1)}, bf16[4,128,1664]{2,1,0:T(8,128)(2,1)}, u32[]{:S(2)}, u32[]{:S(2)}) %collective-permute-start) | collective-permute-done | bytes 1703968 | tf_op jit(solution)/shard_map/while/body/eval_jaxpr/ppermute | solution.py:19
  273.5 24.3 %collective-permute-start = (bf16[4,128,1664]{2,1,0:T(8,128)(2,1)}, bf16[4,128,1664]{2,1,0:T(8,128)(2,1)}, u32[]{:S(2)}, u32[]{:S(2)}) collective-permute-start(bf16[4,128,1664]{2,1,0:T(8,128)(2,1)} %get-tuple-element.268), channel_id=1, source_target_pairs={{16,0},{20,4},{24,8},{28,12},{32,16},{36,20},{40,24},{44,28},{48,3... | collective-permute-start | bytes 5111816 | tf_op jit(solution)/shard_map/while/body/eval_jaxpr/ppermute | solution.py:19
  297.9 36.0 %collective-permute-done = bf16[4,128,1664]{2,1,0:T(8,128)(2,1)} collective-permute-done((bf16[4,128,1664]{2,1,0:T(8,128)(2,1)}, bf16[4,128,1664]{2,1,0:T(8,128)(2,1)}, u32[]{:S(2)}, u32[]{:S(2)}) %collective-permute-start) | collective-permute-done | bytes 1703968 | tf_op jit(solution)/shard_map/while/body/eval_jaxpr/ppermute | solution.py:19
  346.8 33.5 %collective-permute-done = bf16[4,128,1664]{2,1,0:T(8,128)(2,1)} collective-permute-done((bf16[4,128,1664]{2,1,0:T(8,128)(2,1)}, bf16[4,128,1664]{2,1,0:T(8,128)(2,1)}, u32[]{:S(2)}, u32[]{:S(2)}) %collective-permute-start) | collective-permute-done | bytes 1703968 | tf_op jit(solution)/shard_map/while/body/eval_jaxpr/ppermute | solution.py:19
  395.0 31.1 %collective-permute-done = bf16[4,128,1664]{2,1,0:T(8,128)(2,1)} collective-permute-done((bf16[4,128,1664]{2,1,0:T(8,128)(2,1)}, bf16[4,128,1664]{2,1,0:T(8,128)(2,1)}, u32[]{:S(2)}, u32[]{:S(2)}) %collective-permute-start) | collective-permute-done | bytes 1703968 | tf_op jit(solution)/shard_map/while/body/eval_jaxpr/ppermute | solution.py:19
  436.1 6.1 %collective-permute-start = (bf16[4,128,1664]{2,1,0:T(8,128)(2,1)}, bf16[4,128,1664]{2,1,0:T(8,128)(2,1)}, u32[]{:S(2)}, u32[]{:S(2)}) collective-permute-start(bf16[4,128,1664]{2,1,0:T(8,128)(2,1)} %get-tuple-element.268), channel_id=1, source_target_pairs={{16,0},{20,4},{24,8},{28,12},{32,16},{36,20},{40,24},{44,28},{48,3... | collective-permute-start | bytes 5111816 | tf_op jit(solution)/shard_map/while/body/eval_jaxpr/ppermute | solution.py:19
  442.2 30.3 %collective-permute-done = bf16[4,128,1664]{2,1,0:T(8,128)(2,1)} collective-permute-done((bf16[4,128,1664]{2,1,0:T(8,128)(2,1)}, bf16[4,128,1664]{2,1,0:T(8,128)(2,1)}, u32[]{:S(2)}, u32[]{:S(2)}) %collective-permute-start) | collective-permute-done | bytes 1703968 | tf_op jit(solution)/shard_map/while/body/eval_jaxpr/ppermute | solution.py:19
  488.6 29.4 %collective-permute-done = bf16[4,128,1664]{2,1,0:T(8,128)(2,1)} collective-permute-done((bf16[4,128,1664]{2,1,0:T(8,128)(2,1)}, bf16[4,128,1664]{2,1,0:T(8,128)(2,1)}, u32[]{:S(2)}, u32[]{:S(2)}) %collective-permute-start) | collective-permute-done | bytes 1703968 | tf_op jit(solution)/shard_map/while/body/eval_jaxpr/ppermute | solution.py:19
  528.2 18.4 %all_to_all.39 = f32[4,1,128]{2,1,0:T(1,128)S(1)} all-to-all(f32[4,1,128]{2,1,0:T(1,128)S(1)} %broadcast_in_dim.18), channel_id=1, replica_groups=mesh['seq'=64,'tp_0'=2,'tp_1'=2] {'tp_0','tp_1'}, dimensions={0} | all-to-all | bytes 4096 | tf_op jit(solution)/shard_map/all_to_all | solution.py:49
  547.3 22.0 %all-to-all-start.3 = ((f32[64,1,1]{2,1,0:T(1,128)}), f32[64,1,1]{2,1,0:T(1,128)S(1)}, u32[]{:S(2)}, u32[]{:S(2)}) async-start(f32[64,1,1]{2,1,0:T(1,128)} %copy.61), calls=%async_computation.3 | async-start | bytes 65536 | tf_op jit(solution)/shard_map/all_to_all | solution.py:224
  569.3 9.0 %all-to-all-done.3 = f32[64,1,1]{2,1,0:T(1,128)S(1)} async-done(((f32[64,1,1]{2,1,0:T(1,128)}), f32[64,1,1]{2,1,0:T(1,128)S(1)}, u32[]{:S(2)}, u32[]{:S(2)}) %all-to-all-start.3) | async-done | bytes 288 | tf_op jit(solution)/shard_map/all_to_all | solution.py:224
  580.1 12.8 %all_to_all.40 = f32[64,1,1]{2,1,0:T(1,128)S(1)} all-to-all(f32[64,1,1]{2,1,0:T(1,128)S(1)} %mul.237), channel_id=1, replica_groups=mesh['seq'=64,'tp_0'=2,'tp_1'=2] {'seq'}, dimensions={0} | all-to-all | bytes 512 | tf_op jit(solution)/shard_map/all_to_all | solution.py:49
  (118 shorter events, 120.9 us)
Async XLA Ops:
  6.5 14.7 %copy-start = (bf16[2048,512]{1,0:T(8,128)(2,1)S(1)}, bf16[2048,512]{1,0:T(8,128)(2,1)}, u32[]{:S(2)}) copy-start(bf16[2048,512]{1,0:T(8,128)(2,1)} %param.10) | copy-start | bytes 6291460
  6.5 128.1 %all-gather.3.cloned.1.call-start = ((), (), s32[]{:S(2)}) async-start(), calls=%async_computation.5 | async-start | bytes 2129920 | tf_op jit(solution)/shard_map/all_gather | solution.py:200
  21.2 1.0 copy-start.3
  22.6 1.0 copy-start.4
  23.1 1.2 copy-start.1
  35.6 2.9 copy-start.2
  39.4 18.8 %collective-permute-start.1 = (bf16[128,1664]{1,0:T(8,128)(2,1)}, bf16[128,1664]{1,0:T(8,128)(2,1)S(1)}, u32[]{:S(2)}, u32[]{:S(2)}) collective-permute-start(bf16[128,1664]{1,0:T(8,128)(2,1)} %get-tuple-element.200), channel_id=1, source_target_pairs={{4,0},{8,4},{12,8},{16,12},{20,16},{24,20},{28,24},{32,28},{36,32}... | collective-permute-start | bytes 1277960 | tf_op jit(solution)/shard_map/ppermute | solution.py:19
  46.3 37.1 %collective-permute-start.2 = (bf16[128,1664]{1,0:T(8,128)(2,1)}, bf16[128,1664]{1,0:T(8,128)(2,1)S(1)}, u32[]{:S(2)}, u32[]{:S(2)}) collective-permute-start(bf16[128,1664]{1,0:T(8,128)(2,1)} %get-tuple-element.200), channel_id=1, source_target_pairs={{8,0},{12,4},{16,8},{20,12},{24,16},{28,20},{32,24},{36,28},{40,32... | collective-permute-start | bytes 1277960 | tf_op jit(solution)/shard_map/ppermute | solution.py:19
  46.6 49.0 %collective-permute-start.3 = (bf16[128,1664]{1,0:T(8,128)(2,1)}, bf16[128,1664]{1,0:T(8,128)(2,1)S(1)}, u32[]{:S(2)}, u32[]{:S(2)}) collective-permute-start(bf16[128,1664]{1,0:T(8,128)(2,1)} %get-tuple-element.200), channel_id=1, source_target_pairs={{12,0},{16,4},{20,8},{24,12},{28,16},{32,20},{36,24},{40,28},{44,3... | collective-permute-start | bytes 1277960 | tf_op jit(solution)/shard_map/ppermute | solution.py:19
  103.1 31.5 %all-to-all-start.1 = ((bf16[2,2,1,128,1664]{4,3,1,2,0:T(8,128)(2,1)}), bf16[2,2,1,128,1664]{4,3,1,2,0:T(8,128)(2,1)}, u32[]{:S(2)}, u32[]{:S(2)}) async-start(bf16[2,2,1,128,1664]{4,3,1,2,0:T(8,128)(2,1)} %copy.59), calls=%async_computation.1 | async-start | bytes 3407872 | tf_op jit(solution)/shard_map/all_to_all | solution.py:37
  141.9 37.1 %collective-permute-start = (bf16[4,128,1664]{2,1,0:T(8,128)(2,1)}, bf16[4,128,1664]{2,1,0:T(8,128)(2,1)}, u32[]{:S(2)}, u32[]{:S(2)}) collective-permute-start(bf16[4,128,1664]{2,1,0:T(8,128)(2,1)} %get-tuple-element.268), channel_id=1, source_target_pairs={{16,0},{20,4},{24,8},{28,12},{32,16},{36,20},{40,24},{44,28},{48,3... | collective-permute-start | bytes 5111816 | tf_op jit(solution)/shard_map/while/body/eval_jaxpr/ppermute | solution.py:19
  189.1 32.6 %collective-permute-start = (bf16[4,128,1664]{2,1,0:T(8,128)(2,1)}, bf16[4,128,1664]{2,1,0:T(8,128)(2,1)}, u32[]{:S(2)}, u32[]{:S(2)}) collective-permute-start(bf16[4,128,1664]{2,1,0:T(8,128)(2,1)} %get-tuple-element.268), channel_id=1, source_target_pairs={{16,0},{20,4},{24,8},{28,12},{32,16},{36,20},{40,24},{44,28},{48,3... | collective-permute-start | bytes 5111816 | tf_op jit(solution)/shard_map/while/body/eval_jaxpr/ppermute | solution.py:19
  231.7 31.8 %collective-permute-start = (bf16[4,128,1664]{2,1,0:T(8,128)(2,1)}, bf16[4,128,1664]{2,1,0:T(8,128)(2,1)}, u32[]{:S(2)}, u32[]{:S(2)}) collective-permute-start(bf16[4,128,1664]{2,1,0:T(8,128)(2,1)} %get-tuple-element.268), channel_id=1, source_target_pairs={{16,0},{20,4},{24,8},{28,12},{32,16},{36,20},{40,24},{44,28},{48,3... | collective-permute-start | bytes 5111816 | tf_op jit(solution)/shard_map/while/body/eval_jaxpr/ppermute | solution.py:19
  273.5 60.3 %collective-permute-start = (bf16[4,128,1664]{2,1,0:T(8,128)(2,1)}, bf16[4,128,1664]{2,1,0:T(8,128)(2,1)}, u32[]{:S(2)}, u32[]{:S(2)}) collective-permute-start(bf16[4,128,1664]{2,1,0:T(8,128)(2,1)} %get-tuple-element.268), channel_id=1, source_target_pairs={{16,0},{20,4},{24,8},{28,12},{32,16},{36,20},{40,24},{44,28},{48,3... | collective-permute-start | bytes 5111816 | tf_op jit(solution)/shard_map/while/body/eval_jaxpr/ppermute | solution.py:19
  343.9 36.5 %collective-permute-start = (bf16[4,128,1664]{2,1,0:T(8,128)(2,1)}, bf16[4,128,1664]{2,1,0:T(8,128)(2,1)}, u32[]{:S(2)}, u32[]{:S(2)}) collective-permute-start(bf16[4,128,1664]{2,1,0:T(8,128)(2,1)} %get-tuple-element.268), channel_id=1, source_target_pairs={{16,0},{20,4},{24,8},{28,12},{32,16},{36,20},{40,24},{44,28},{48,3... | collective-permute-start | bytes 5111816 | tf_op jit(solution)/shard_map/while/body/eval_jaxpr/ppermute | solution.py:19
  390.3 35.7 %collective-permute-start = (bf16[4,128,1664]{2,1,0:T(8,128)(2,1)}, bf16[4,128,1664]{2,1,0:T(8,128)(2,1)}, u32[]{:S(2)}, u32[]{:S(2)}) collective-permute-start(bf16[4,128,1664]{2,1,0:T(8,128)(2,1)} %get-tuple-element.268), channel_id=1, source_target_pairs={{16,0},{20,4},{24,8},{28,12},{32,16},{36,20},{40,24},{44,28},{48,3... | collective-permute-start | bytes 5111816 | tf_op jit(solution)/shard_map/while/body/eval_jaxpr/ppermute | solution.py:19
  436.1 36.4 %collective-permute-start = (bf16[4,128,1664]{2,1,0:T(8,128)(2,1)}, bf16[4,128,1664]{2,1,0:T(8,128)(2,1)}, u32[]{:S(2)}, u32[]{:S(2)}) collective-permute-start(bf16[4,128,1664]{2,1,0:T(8,128)(2,1)} %get-tuple-element.268), channel_id=1, source_target_pairs={{16,0},{20,4},{24,8},{28,12},{32,16},{36,20},{40,24},{44,28},{48,3... | collective-permute-start | bytes 5111816 | tf_op jit(solution)/shard_map/while/body/eval_jaxpr/ppermute | solution.py:19
  482.5 35.5 %collective-permute-start = (bf16[4,128,1664]{2,1,0:T(8,128)(2,1)}, bf16[4,128,1664]{2,1,0:T(8,128)(2,1)}, u32[]{:S(2)}, u32[]{:S(2)}) collective-permute-start(bf16[4,128,1664]{2,1,0:T(8,128)(2,1)} %get-tuple-element.268), channel_id=1, source_target_pairs={{16,0},{20,4},{24,8},{28,12},{32,16},{36,20},{40,24},{44,28},{48,3... | collective-permute-start | bytes 5111816 | tf_op jit(solution)/shard_map/while/body/eval_jaxpr/ppermute | solution.py:19
  547.3 31.0 %all-to-all-start.3 = ((f32[64,1,1]{2,1,0:T(1,128)}), f32[64,1,1]{2,1,0:T(1,128)S(1)}, u32[]{:S(2)}, u32[]{:S(2)}) async-start(f32[64,1,1]{2,1,0:T(1,128)} %copy.61), calls=%async_computation.3 | async-start | bytes 65536 | tf_op jit(solution)/shard_map/all_to_all | solution.py:224
Sparse Core Ops, SparseCore 0:
  39.5 51.7 all-gather.2
where the time goes:
time: 604 us; the launch traced here: 602 us
  waiting for transfers between devices  331 us (55%)
  starting transfers between devices  93.8 us (16%)
  blocking collectives  62.9 us (10%)
  matrix products  61.7 us (10%)
  local copies, waits for them, and re-layouts  28.4 us (5%)
  between operations  14.3 us (2%)
    ppermute x11, waiting for transfers between devices, from_behind(): return lax.ppermute(block, axis, route)  298 us
    ppermute x11, starting transfers between devices, from_behind(): return lax.ppermute(block, axis, route)  64.6 us
    dot_general x36, matrix products, whole_tile(): lax.dot_general(left_whole[:, :, begin_col:end_col], right_whole[:, :, be...  57 us
    all_to_all x2, blocking collectives, copy_for_each(): lax.all_to_all(jnp.broadcast_to(value[None], (size, *value.shape)), axis,...  31.2 us
    all_to_all x1, waiting for transfers between devices, moved_by_axis(): lax.all_to_all(blocks, axes[k], split_axis=k, concat_axis=k, tiled=True)  24.3 us
    while x8, local copies, waits for them, and re-layouts  22.2 us
    all_to_all x1, starting transfers between devices, on_device(): lax.all_to_all(col_acc, 'seq', split_axis=0, concat_axis=1, tiled=True)  22 us
    all_gather x1, blocking collectives, attention_factors(): lax.all_gather(states, TP, axis=2, tiled=True)  14.6 us
  transfers between devices with their start and end apart: 14, of which 13 were waited for; matrix products, arithmetic and copies ran while one was open for 0% of the time, Pallas kernels for 0%

commit v1 on v0

v1 whole, which is shorter than its diff:
```python
import jax
import jax.numpy as jnp
from jax import lax
from jax.sharding import Mesh
from jax.sharding import PartitionSpec as P

HEADS = 32
KV_HEADS = 8
HEAD_DIM = 64
SEQ = ("zb", "za", "x", "y")
NEAR = ("za", "x", "y")
TP = ("h", "c")
EVERY = SEQ + TP
SWAP = ((0, 1), (1, 0))

theta_base = 500000.0


def swapped(value, axis):
    return lax.ppermute(value, axis, SWAP)


def in_order(own, other, axis, dim):
    first = lax.axis_index(axis) == 0
    return jnp.where(
        first,
        jnp.concatenate([own, other], axis=dim),
        jnp.concatenate([other, own], axis=dim),
    )


def all_features(part):
    far = swapped(part, "h")
    near = in_order(part, swapped(part, "c"), "c", 1)
    far = in_order(far, swapped(far, "c"), "c", 1)
    return in_order(near, far, "h", 1)


def rope_tables(length, head_dim):
    half_dim = head_dim // 2
    freqs_k = theta_base ** (-(jnp.arange(half_dim, dtype=jnp.float32) * 2.0 / head_dim))
    angles = jnp.arange(length, dtype=jnp.float32)[:, None] * freqs_k[None, :]
    angles = jnp.concatenate([angles, angles], axis=1)
    return (jnp.cos(angles)[:, None, :], jnp.sin(angles)[:, None, :])


def rotate(values_in, cos_table, sine_table):
    half_dim = values_in.shape[-1] // 2
    turned = jnp.concatenate([-values_in[..., half_dim:], values_in[..., :half_dim]], axis=-1)
    return values_in * cos_table + turned * sine_table


def attention_factors(full_states, full_cot, wq, wk, wv, wo):
    length = full_states.shape[0]
    kv_local = wk.shape[1] // HEAD_DIM
    group_size = HEADS // KV_HEADS
    cos_table, sine_table = rope_tables(length, HEAD_DIM)

    def project(w):
        return jnp.dot(full_states, w, preferred_element_type=jnp.float32)

    query_heads = project(wq).reshape(length, kv_local * group_size, HEAD_DIM)
    query_heads = (
        rotate(query_heads, cos_table, sine_table)
        .astype(jnp.bfloat16)
        .reshape(length, kv_local, group_size, HEAD_DIM)
    )
    key_heads = project(wk).reshape(length, kv_local, HEAD_DIM)
    key_heads = rotate(key_heads, cos_table, sine_table).astype(jnp.bfloat16)
    value_heads = project(wv).astype(jnp.bfloat16).reshape(length, kv_local, HEAD_DIM)
    scores = jnp.einsum(
        "qkgd,tkd->kgqt", query_heads, key_heads, preferred_element_type=jnp.float32
    ) * HEAD_DIM ** (-0.5)
    causal = jnp.arange(length)[:, None] >= jnp.arange(length)[None, :]
    scores = jnp.where(causal, scores, -jnp.inf)
    weights_bf = jax.nn.softmax(scores, axis=-1).astype(jnp.bfloat16)
    attended = (
        jnp.einsum("kgqt,tkd->qkgd", weights_bf, value_heads, preferred_element_type=jnp.float32)
        .astype(jnp.bfloat16)
        .reshape(length, -1)
    )
    grad_attended = (
        lax.dot_general(
            full_cot, wo, (((1,), (1,)), ((), ())), preferred_element_type=jnp.float32
        )
        .astype(jnp.bfloat16)
        .reshape(length, kv_local, group_size, HEAD_DIM)
    )
    value_gradient = (
        jnp.einsum("kgqt,qkgd->tkd", weights_bf, grad_attended, preferred_element_type=jnp.float32)
        .astype(jnp.bfloat16)
        .reshape(length, -1)
    )
    return jnp.concatenate([attended, value_gradient], axis=1)


def rows_by(left, right):
    return lax.dot_general(
        left, right, (((0,), (0,)), ((), ())), preferred_element_type=jnp.float32
    ).astype(jnp.bfloat16)


def gradient_blocks(factors, cot_half, states_half, blocks):
    part_width = HEADS * HEAD_DIM // 4
    both = jnp.concatenate(
        [
            rows_by(factors[:, :part_width], cot_half),
            rows_by(factors[:, part_width:], states_half),
        ],
        axis=0,
    )
    rows, cols = both.shape
    tall = blocks // (cols // 128)
    both = both.reshape(tall, rows // tall, cols // 128, 128)
    return jnp.transpose(both, (0, 2, 1, 3)).reshape(blocks, rows // tall, 128)


def on_device(states, cotangent, wq, wk, wv, wo):
    full_states = all_features(states[0])
    full_cot = all_features(cotangent[0])
    length, width = full_states.shape
    zb = lax.axis_index("zb")
    core = lax.axis_index("c")

    def sent_half(full):
        part = width // 4
        start = (1 - zb) * (2 * part) + core * part
        piece = lax.dynamic_slice_in_dim(full, start, part, 1)
        piece = swapped(piece, "zb")
        return in_order(piece, swapped(piece, "c"), "c", 1)

    def own_half(full):
        return jnp.where(zb == 0, full[:, : width // 2], full[:, width // 2 :])

    other_states, other_cot = sent_half(full_states), sent_half(full_cot)
    factors = attention_factors(full_states, full_cot, wq, wk, wv, wo)
    other_factors = swapped(factors, "zb")
    blocks = lax.axis_size(NEAR)
    own_blocks = gradient_blocks(factors, own_half(full_cot), own_half(full_states), blocks)
    other_blocks = gradient_blocks(other_factors, other_cot, other_states, blocks)
    sent = jnp.stack([own_blocks, other_blocks], axis=1)
    got = lax.all_to_all(sent, NEAR, 0, 0, tiled=True)
    seqs = 2 * blocks
    got = jnp.swapaxes(got, 0, 1).reshape(seqs, *got.shape[2:])
    share = jnp.einsum("irc,jrc->ij", got, got, preferred_element_type=jnp.float32)
    share = jnp.where(zb == 0, share, jnp.roll(share, (blocks, blocks), (0, 1)))
    rows = jnp.concatenate(
        [share, jnp.broadcast_to(jnp.diagonal(share)[None], share.shape)], axis=1
    )
    copies = lax.axis_size(TP)
    rows = jnp.broadcast_to(rows[:, None], (seqs, copies, 2 * seqs)).reshape(seqs * copies, 2 * seqs)
    total = jnp.sum(lax.all_to_all(rows, EVERY, 0, 0, tiled=True), axis=0, keepdims=True)
    row, diag = total[:, :seqs], total[:, seqs:]
    own_diag = lax.dynamic_slice_in_dim(diag, lax.axis_index(SEQ), 1, 1)
    return row / jnp.sqrt(own_diag * diag)


def solution(mesh):
    split = Mesh(
        mesh.devices.reshape(2, mesh.shape["seq"] // 32, 4, 4, 2, 2), EVERY
    )
    placed = (
        P(SEQ, None, TP),
        P(SEQ, None, TP),
        P(None, TP),
        P(None, TP),
        P(None, TP),
        P(TP, None),
    )
    return jax.shard_map(
        on_device, mesh=split, in_specs=placed, out_specs=P(SEQ, None), check_vma=False
    )
```

time: 604 us -> 133 us (0.22)
  waiting for transfers between devices: 331 us -> 63.3 us
  blocking collectives: 62.9 us -> 0 us
  starting transfers between devices: 93.8 us -> 40.1 us
  matrix products: 61.7 us -> 11.7 us
  local copies, waits for them, and re-layouts: 28.4 us -> 9.57 us
  between operations: 14.3 us -> 0.33 us
    ppermute x11, waiting for transfers between devices: 298 us -> 17.6 us  [swapped(): return lax.ppermute(value, axis, SWAP)]
    dot_general x43 -> x11, matrix products: 61.7 us -> 8.9 us  [the longest x3 3.81 us: project(): return jnp.dot(full_states, w, preferred_element_type=jnp.float32)]
    ppermute x11, starting transfers between devices: 64.6 us -> 19.4 us  [swapped(): return lax.ppermute(value, axis, SWAP)]
    all_to_all x3 -> x0, blocking collectives: 36.9 us -> none  [the longest x2 31.2 us: copy_for_each(): lax.all_to_all(jnp.broadcast_to(value[None], (size, *value.shape)), axis,...]
    all_gather x2 -> x0, blocking collectives: 25.9 us -> none  [the longest x1 14.6 us: attention_factors(): lax.all_gather(states, TP, axis=2, tiled=True)]
    while x8 -> x0, local copies, waits for them, and re-layouts: 22.2 us -> none
    all_to_all x2, waiting for transfers between devices: 33.3 us -> 45.7 us  [the longest x1 32.8 us: on_device(): got = lax.all_to_all(sent, NEAR, 0, 0, tiled=True)]
    all_to_all x2, starting transfers between devices: 29.2 us -> 20.7 us  [the longest x1 13.4 us: on_device(): lax.all_to_all(rows, EVERY, 0, 0, tiled=True)]
  transfers between devices with their start and end apart: 14 -> 13, of which waited for: 13 -> 5; matrix products, arithmetic and copies ran while one was open for 0% -> 13% of each run, Pallas kernels for 0% -> 0%
where the time goes in v1:
time: 133 us
  waiting for transfers between devices  63.3 us (48%)
  starting transfers between devices  40.1 us (30%)
  matrix products  11.7 us (9%)
  local copies, waits for them, and re-layouts  9.57 us (7%)
  other arithmetic  7.89 us (6%)
    all_to_all x1, waiting for transfers between devices, on_device(): got = lax.all_to_all(sent, NEAR, 0, 0, tiled=True)  32.8 us
    ppermute x11, starting transfers between devices, swapped(): return lax.ppermute(value, axis, SWAP)  19.4 us
    ppermute x11, waiting for transfers between devices, swapped(): return lax.ppermute(value, axis, SWAP)  17.6 us
    all_to_all x1, starting transfers between devices, on_device(): lax.all_to_all(rows, EVERY, 0, 0, tiled=True)  13.4 us
    all_to_all x1, waiting for transfers between devices, on_device(): lax.all_to_all(rows, EVERY, 0, 0, tiled=True)  12.9 us
    all_to_all x1, starting transfers between devices, on_device(): got = lax.all_to_all(sent, NEAR, 0, 0, tiled=True)  7.32 us
    dot_general x3, matrix products, project(): return jnp.dot(full_states, w, preferred_element_type=jnp.float32)  3.81 us
    transpose x1, local copies, waits for them, and re-layouts, on_device(): got = jnp.swapaxes(got, 0, 1).reshape(seqs, *got.shape[2:])  3.43 us
  transfers between devices with their start and end apart: 13, of which 5 were waited for; matrix products, arithmetic and copies ran while one was open for 13% of the time, Pallas kernels for 0%

profile of v1, /device:TPU:1, one launch (start us, length us, event | category | flops | bytes accessed | tf_op | source)
XLA Modules:
  0.0 132.9 jit_solution(13049272270850153254)
XLA Ops:
  0.0 7.7 %collective-permute-start.1 = (bf16[128,512]{1,0:T(8,128)(2,1)}, bf16[128,512]{1,0:T(8,128)(2,1)S(1)}, u32[]{:S(2)}, u32[]{:S(2)}) collective-permute-start(bf16[128,512]{1,0:T(8,128)(2,1)} %bitcast.96), channel_id=1, source_target_pairs={{0,2},{2,0},{1,3},{3,1},{4,6},{6,4},{5,7},{7,5},{8,10},{10,8},{9,1... | collective-permute-start | bytes 393224 | tf_op jit(solution)/shard_map/ppermute | solution.py:20
  7.7 1.0 collective-permute-start
  10.7 5.3 %collective-permute-start.2 = (bf16[128,512]{1,0:T(8,128)(2,1)S(1)}, bf16[128,512]{1,0:T(8,128)(2,1)S(1)}, u32[]{:S(2)}, u32[]{:S(2)}) collective-permute-start(bf16[128,512]{1,0:T(8,128)(2,1)S(1)} %collective-permute-done.1), channel_id=1, source_target_pairs={{0,1},{1,0},{2,3},{3,2},{4,5},{5,4},{6,7},{7,6},{8,9},{9,8},{10,11... | collective-permute-start | bytes 393224 | tf_op jit(solution)/shard_map/ppermute | solution.py:20
  16.0 4.9 %collective-permute-done.4 = bf16[128,512]{1,0:T(8,128)(2,1)S(1)} collective-permute-done((bf16[128,512]{1,0:T(8,128)(2,1)}, bf16[128,512]{1,0:T(8,128)(2,1)S(1)}, u32[]{:S(2)}, u32[]{:S(2)}) %collective-permute-start.4) | collective-permute-done | bytes 131104 | tf_op jit(solution)/shard_map/ppermute | solution.py:20
  20.9 0.9 collective-permute-start.5
  21.8 1.0 maximum_select_fusion.2
  22.8 1.0 maximum_select_fusion.4
  24.1 0.9 convolution_convert_fusion.6
  27.0 0.8 convolution_convert_fusion.4
  28.0 2.5 %fusion.61 = f32[128,512]{0,1:T(8,128)S(1)} fusion(bf16[128,2048]{1,0:T(8,128)(2,1)S(1)} %maximum_select_fusion, bf16[2048,512]{1,0:T(8,128)(2,1)} %param.8), kind=kOutput, calls=%fused_computation.88 | convolution fusion | flops 268435456 | bytes 2883584 | tf_op jit(solution)/shard_map/dot_general | solution.py:60
  31.2 2.8 %fusion.55 = (f32[2,4,128]{2,1,0:T(4,128)}, f32[2,4,128,128]{2,3,1,0:T(8,128)}) fusion(pred[128,128]{0,1:T(8,128)(4,1)S(1)} %iota_compare_fusion, f32[128,2,4,32]{0,3,2,1:T(8,128)} %bitcast.103, f32[128,2,4,32]{0,3,2,1:T(8,128)} %bitcast.102, f32[128,2,4,64]{0,3,2,1:T(8,128)S(1)} %bitcast.92, f32[128,64]{0,1:T(8,128)} %get-tuple-element.12, ...), kind=kOutput, calls=%fused_computation.86 | convolution fusion | flops 17711232 | bytes 1265664 | tf_op jit(solution)/shard_map/sub | solution.py:76
  34.0 1.1 divide_convert_fusion
  35.4 0.9 convolution_convert_fusion.5
  37.0 2.4 %collective-permute-start.6 = (bf16[128,640]{0,1:T(8,128)(2,1)S(1)}, bf16[128,640]{0,1:T(8,128)(2,1)S(1)}, u32[]{:S(2)}, u32[]{:S(2)}) collective-permute-start(bf16[128,640]{0,1:T(8,128)(2,1)S(1)} %pad_maximum_fusion.1), channel_id=1, source_target_pairs={{0,128},{128,0},{1,129},{129,1},{2,130},{130,2},{3,131},{131,3},{4... | collective-permute-start | bytes 491528 | tf_op jit(solution)/shard_map/ppermute | solution.py:20
  41.1 11.9 %collective-permute-done.7 = bf16[128,512]{1,0:T(8,128)(2,1)S(1)} collective-permute-done((bf16[128,512]{1,0:T(8,128)(2,1)S(1)}, bf16[128,512]{1,0:T(8,128)(2,1)S(1)}, u32[]{:S(2)}, u32[]{:S(2)}) %collective-permute-start.7) | collective-permute-done | bytes 131104 | tf_op jit(solution)/shard_map/ppermute | solution.py:20
  53.7 1.2 convolution_convert_fusion.2
  56.4 1.8 %copy.28 = bf16[32,2,160,128]{3,2,1,0:T(8,128)(2,1)} copy(bf16[32,2,160,128]{3,2,0,1:T(8,128)(2,1)S(1)} %pad_maximum_fusion) | data formatting | bytes 5242880 | tf_op jit(solution)/shard_map/stack | solution.py:141
  58.2 7.3 %all-to-all-start = ((bf16[32,2,160,128]{3,2,1,0:T(8,128)(2,1)}), bf16[32,2,160,128]{3,2,1,0:T(8,128)(2,1)}, u32[]{:S(2)}, u32[]{:S(2)}) async-start(bf16[32,2,160,128]{3,2,1,0:T(8,128)(2,1)} %copy.28), calls=%async_computation | async-start | bytes 5242880 | tf_op jit(solution)/shard_map/all_to_all | solution.py:142
  65.5 32.8 %all-to-all-done = bf16[32,2,160,128]{3,2,1,0:T(8,128)(2,1)} async-done(((bf16[32,2,160,128]{3,2,1,0:T(8,128)(2,1)}), bf16[32,2,160,128]{3,2,1,0:T(8,128)(2,1)}, u32[]{:S(2)}, u32[]{:S(2)}) %all-to-all-start) | async-done | bytes 2621472 | tf_op jit(solution)/shard_map/all_to_all | solution.py:142
  98.3 3.4 %copy.29 = bf16[2,32,160,128]{3,1,0,2:T(8,128)(2,1)S(1)} copy(bf16[2,32,160,128]{3,2,0,1:T(8,128)(2,1)} %bitcast.26) | data formatting | bytes 5242880 | tf_op jit(solution)/shard_map/transpose | solution.py:144
  101.7 0.8 convolution_bitcast_fusion.1
  104.3 13.4 %all-to-all-start.1 = ((f32[256,1,128]{2,1,0:T(1,128)}), f32[256,1,128]{2,1,0:T(1,128)S(1)}, u32[]{:S(2)}, u32[]{:S(2)}) async-start(f32[256,1,128]{2,1,0:T(1,128)} %bitcast.30), calls=%async_computation.1 | async-start | bytes 262144 | tf_op jit(solution)/shard_map/all_to_all | solution.py:152
  117.8 12.9 %all-to-all-done.1 = f32[256,1,128]{2,1,0:T(1,128)S(1)} async-done(((f32[256,1,128]{2,1,0:T(1,128)}), f32[256,1,128]{2,1,0:T(1,128)S(1)}, u32[]{:S(2)}, u32[]{:S(2)}) %all-to-all-start.1) | async-done | bytes 131104 | tf_op jit(solution)/shard_map/all_to_all | solution.py:152
  131.7 1.2 rsqrt_multiply_fusion
  (60 shorter events, 12.2 us)
Async XLA Ops:
  0.0 27.0 %copy-start = (bf16[512,2048]{1,0:T(8,128)(2,1)S(1)}, bf16[512,2048]{1,0:T(8,128)(2,1)}, u32[]{:S(2)}) copy-start(bf16[512,2048]{1,0:T(8,128)(2,1)} %param.11) | copy-start | bytes 6291460
  0.0 24.1 %copy-start.1 = (bf16[2048,128]{1,0:T(8,128)(2,1)S(1)}, bf16[2048,128]{1,0:T(8,128)(2,1)}, u32[]{:S(2)}) copy-start(bf16[2048,128]{1,0:T(8,128)(2,1)} %param.10) | copy-start | bytes 1572868
  0.0 10.7 %collective-permute-start.1 = (bf16[128,512]{1,0:T(8,128)(2,1)}, bf16[128,512]{1,0:T(8,128)(2,1)S(1)}, u32[]{:S(2)}, u32[]{:S(2)}) collective-permute-start(bf16[128,512]{1,0:T(8,128)(2,1)} %bitcast.96), channel_id=1, source_target_pairs={{0,2},{2,0},{1,3},{3,1},{4,6},{6,4},{5,7},{7,5},{8,10},{10,8},{9,1... | collective-permute-start | bytes 393224 | tf_op jit(solution)/shard_map/ppermute | solution.py:20
  7.7 14.0 %collective-permute-start = (bf16[128,512]{1,0:T(8,128)(2,1)}, bf16[128,512]{1,0:T(8,128)(2,1)S(1)}, u32[]{:S(2)}, u32[]{:S(2)}) collective-permute-start(bf16[128,512]{1,0:T(8,128)(2,1)} %bitcast.97), channel_id=1, source_target_pairs={{0,1},{1,0},{2,3},{3,2},{4,5},{5,4},{6,7},{7,6},{8,9},{9,8},{10,11... | collective-permute-start | bytes 393224 | tf_op jit(solution)/shard_map/ppermute | solution.py:20
  8.7 12.2 %collective-permute-start.4 = (bf16[128,512]{1,0:T(8,128)(2,1)}, bf16[128,512]{1,0:T(8,128)(2,1)S(1)}, u32[]{:S(2)}, u32[]{:S(2)}) collective-permute-start(bf16[128,512]{1,0:T(8,128)(2,1)} %bitcast.99), channel_id=1, source_target_pairs={{0,2},{2,0},{1,3},{3,1},{4,6},{6,4},{5,7},{7,5},{8,10},{10,8},{9,1... | collective-permute-start | bytes 393224 | tf_op jit(solution)/shard_map/ppermute | solution.py:20
  8.9 14.0 %collective-permute-start.3 = (bf16[128,512]{1,0:T(8,128)(2,1)}, bf16[128,512]{1,0:T(8,128)(2,1)S(1)}, u32[]{:S(2)}, u32[]{:S(2)}) collective-permute-start(bf16[128,512]{1,0:T(8,128)(2,1)} %bitcast.100), channel_id=1, source_target_pairs={{0,1},{1,0},{2,3},{3,2},{4,5},{5,4},{6,7},{7,6},{8,9},{9,8},{10,11... | collective-permute-start | bytes 393224 | tf_op jit(solution)/shard_map/ppermute | solution.py:20
  10.0 15.1 %copy-start.2 = (bf16[2048,128]{1,0:T(8,128)(2,1)S(1)}, bf16[2048,128]{1,0:T(8,128)(2,1)}, u32[]{:S(2)}) copy-start(bf16[2048,128]{1,0:T(8,128)(2,1)} %param.9) | copy-start | bytes 1572868
  10.7 13.2 %collective-permute-start.2 = (bf16[128,512]{1,0:T(8,128)(2,1)S(1)}, bf16[128,512]{1,0:T(8,128)(2,1)S(1)}, u32[]{:S(2)}, u32[]{:S(2)}) collective-permute-start(bf16[128,512]{1,0:T(8,128)(2,1)S(1)} %collective-permute-done.1), channel_id=1, source_target_pairs={{0,1},{1,0},{2,3},{3,2},{4,5},{5,4},{6,7},{7,6},{8,9},{9,8},{10,11... | collective-permute-start | bytes 393224 | tf_op jit(solution)/shard_map/ppermute | solution.py:20
  20.9 5.9 %collective-permute-start.5 = (bf16[128,512]{1,0:T(8,128)(2,1)S(1)}, bf16[128,512]{1,0:T(8,128)(2,1)S(1)}, u32[]{:S(2)}, u32[]{:S(2)}) collective-permute-start(bf16[128,512]{1,0:T(8,128)(2,1)S(1)} %collective-permute-done.4), channel_id=1, source_target_pairs={{0,1},{1,0},{2,3},{3,2},{4,5},{5,4},{6,7},{7,6},{8,9},{9,8},{10,11... | collective-permute-start | bytes 393224 | tf_op jit(solution)/shard_map/ppermute | solution.py:20
  25.4 1.3 copy-start.3
  26.1 13.4 %collective-permute-start.9 = (bf16[128,512]{1,0:T(8,128)(2,1)}, bf16[128,512]{1,0:T(8,128)(2,1)}, u32[]{:S(2)}, u32[]{:S(2)}) collective-permute-start(bf16[128,512]{1,0:T(8,128)(2,1)} %constant_dynamic-slice_fusion.1), channel_id=1, source_target_pairs={{0,128},{128,0},{1,129},{129,1},{2,130},{130,2},{3,131},{131,3},{4... | collective-permute-start | bytes 393224 | tf_op jit(solution)/shard_map/ppermute | solution.py:20
  37.0 16.7 %collective-permute-start.6 = (bf16[128,640]{0,1:T(8,128)(2,1)S(1)}, bf16[128,640]{0,1:T(8,128)(2,1)S(1)}, u32[]{:S(2)}, u32[]{:S(2)}) collective-permute-start(bf16[128,640]{0,1:T(8,128)(2,1)S(1)} %pad_maximum_fusion.1), channel_id=1, source_target_pairs={{0,128},{128,0},{1,129},{129,1},{2,130},{130,2},{3,131},{131,3},{4... | collective-permute-start | bytes 491528 | tf_op jit(solution)/shard_map/ppermute | solution.py:20
  39.4 13.6 %collective-permute-start.7 = (bf16[128,512]{1,0:T(8,128)(2,1)S(1)}, bf16[128,512]{1,0:T(8,128)(2,1)S(1)}, u32[]{:S(2)}, u32[]{:S(2)}) collective-permute-start(bf16[128,512]{1,0:T(8,128)(2,1)S(1)} %constant_dynamic-slice_fusion.2), channel_id=1, source_target_pairs={{0,128},{128,0},{1,129},{129,1},{2,130},{130,2},{3,131},{131,3},{4... | collective-permute-start | bytes 393224 | tf_op jit(solution)/shard_map/ppermute | solution.py:20
  39.5 14.2 %collective-permute-start.10 = (bf16[128,512]{1,0:T(8,128)(2,1)}, bf16[128,512]{1,0:T(8,128)(2,1)S(1)}, u32[]{:S(2)}, u32[]{:S(2)}) collective-permute-start(bf16[128,512]{1,0:T(8,128)(2,1)} %collective-permute-done.9), channel_id=1, source_target_pairs={{0,1},{1,0},{2,3},{3,2},{4,5},{5,4},{6,7},{7,6},{8,9},{9,8},{10,11... | collective-permute-start | bytes 393224 | tf_op jit(solution)/shard_map/ppermute | solution.py:20
  53.0 1.9 %collective-permute-start.8 = (bf16[128,512]{1,0:T(8,128)(2,1)S(1)}, bf16[128,512]{1,0:T(8,128)(2,1)S(1)}, u32[]{:S(2)}, u32[]{:S(2)}) collective-permute-start(bf16[128,512]{1,0:T(8,128)(2,1)S(1)} %collective-permute-done.7), channel_id=1, source_target_pairs={{0,1},{1,0},{2,3},{3,2},{4,5},{5,4},{6,7},{7,6},{8,9},{9,8},{10,11... | collective-permute-start | bytes 393224 | tf_op jit(solution)/shard_map/ppermute | solution.py:20
  58.2 40.1 %all-to-all-start = ((bf16[32,2,160,128]{3,2,1,0:T(8,128)(2,1)}), bf16[32,2,160,128]{3,2,1,0:T(8,128)(2,1)}, u32[]{:S(2)}, u32[]{:S(2)}) async-start(bf16[32,2,160,128]{3,2,1,0:T(8,128)(2,1)} %copy.28), calls=%async_computation | async-start | bytes 5242880 | tf_op jit(solution)/shard_map/all_to_all | solution.py:142
  104.3 26.3 %all-to-all-start.1 = ((f32[256,1,128]{2,1,0:T(1,128)}), f32[256,1,128]{2,1,0:T(1,128)S(1)}, u32[]{:S(2)}, u32[]{:S(2)}) async-start(f32[256,1,128]{2,1,0:T(1,128)} %bitcast.30), calls=%async_computation.1 | async-start | bytes 262144 | tf_op jit(solution)/shard_map/all_to_all | solution.py:152

commit v2 on v1

v2 whole, which is shorter than its diff:
```python
import functools

import jax
import jax.numpy as jnp
from jax import lax
from jax.experimental import pallas as pl
from jax.experimental.pallas import tpu as pltpu
from jax.sharding import Mesh
from jax.sharding import PartitionSpec as P

HEADS = 32
KV_HEADS = 8
HEAD_DIM = 64
LANES = 128
SEQ = ("zb", "za", "x", "y")
NEAR = ("za", "x", "y")
TP = ("h", "c")
EVERY = SEQ + TP
SWAP = ((0, 1), (1, 0))

theta_base = 500000.0


def swapped(value, axis):
    return lax.ppermute(value, axis, SWAP)


def rope_tables(length, head_dim):
    half_dim = head_dim // 2
    freqs_k = theta_base ** (-(jnp.arange(half_dim, dtype=jnp.float32) * 2.0 / head_dim))
    angles = jnp.arange(length, dtype=jnp.float32)[:, None] * freqs_k[None, :]
    sine = jnp.sin(angles)
    cos = jnp.tile(jnp.cos(angles), (1, LANES // half_dim))
    return cos, jnp.tile(jnp.concatenate([-sine, sine], axis=1), (1, LANES // head_dim))


def dot(left, right, dims=((1,), (0,))):
    return lax.dot_general(left, right, (dims, ((), ())), preferred_element_type=jnp.float32)


def kernel_call(body, outs, ins, scratch=(), vmem_mib=24):
    smem = pl.BlockSpec(memory_space=pltpu.SMEM)
    vmem = pl.BlockSpec(memory_space=pltpu.VMEM)
    return pl.pallas_call(
        body,
        out_shape=outs,
        in_specs=[smem if a.dtype == jnp.int32 else vmem for a in ins],
        out_specs=jax.tree.map(lambda _: vmem, outs),
        scratch_shapes=scratch,
        compiler_params=pltpu.CompilerParams(vmem_limit_bytes=vmem_mib * 2**20),
    )(*ins)


def lower_half(shape):
    return lax.broadcasted_iota(jnp.int32, shape, 1) % (2 * HEAD_DIM) < HEAD_DIM


def doubled(pair, low):
    turned = pltpu.roll(pair, HEAD_DIM, 1)
    return jnp.where(low, pair, turned), jnp.where(low, turned, pair)


def attention_body(at, s0, s1, s2, s3, wq, wk, wv, cos_ref, sine_ref, attended, probs):
    quarter = s0.shape[1]
    h, c = at[0], at[1]
    places = [2 * h + c, 2 * h + 1 - c, 2 * (1 - h) + c, 2 * (1 - h) + 1 - c]
    parts = [s0[...], s1[...], s2[...], s3[...]]

    def project(w):
        total = None
        for part, place in zip(parts, places):
            rows = pl.ds(pl.multiple_of(place * quarter, quarter), quarter)
            term = dot(part, w[rows, :])
            total = term if total is None else total + term
        return total

    cos, sine = cos_ref[...], sine_ref[...]
    length = cos.shape[0]
    lane = lax.broadcasted_iota(jnp.int32, cos.shape, 1)
    first = lane % HEAD_DIM < HEAD_DIM // 2
    low = lower_half(cos.shape)

    def rotate(tile):
        ahead = pltpu.roll(tile, LANES - HEAD_DIM // 2, 1)
        behind = pltpu.roll(tile, HEAD_DIM // 2, 1)
        return tile * cos + jnp.where(first, ahead, behind) * sine

    keys = doubled(rotate(project(wk)), low)
    keys = [k.astype(jnp.bfloat16) for k in keys]
    values = [v.astype(jnp.bfloat16) for v in doubled(project(wv), low)]
    queries = project(wq)
    causal = lax.broadcasted_iota(jnp.int32, (length, length), 0) >= lax.broadcasted_iota(
        jnp.int32, (length, length), 1
    )
    tiles = queries.shape[1] // LANES
    for t in range(tiles):
        group = 2 * t // (HEADS // KV_HEADS)
        query = rotate(queries[:, t * LANES : (t + 1) * LANES])
        found = []
        for s in range(2):
            mine = low if s == 0 else jnp.logical_not(low)
            q = jnp.where(mine, query, 0.0).astype(jnp.bfloat16)
            scores = dot(q, keys[group], ((1,), (1,))) * HEAD_DIM ** (-0.5)
            scores = jnp.where(causal, scores, -jnp.inf)
            e = jnp.exp(scores - jnp.max(scores, axis=1, keepdims=True))
            p = (e / jnp.sum(e, axis=1, keepdims=True)).astype(jnp.bfloat16)
            probs[(2 * t + s) * length : (2 * t + s + 1) * length, :] = p
            found.append(dot(p, values[group]))
        tile = jnp.where(low, found[0], found[1])
        attended[:, t * LANES : (t + 1) * LANES] = tile.astype(jnp.bfloat16)


def put_blocks(blocks, turned, kind_rows, cols, col_at):
    tall = blocks.shape[1]
    begin, end = kind_rows
    wide = cols.shape[1] // LANES
    across = 8
    product = dot(turned, cols).astype(jnp.bfloat16)
    row = begin
    while row < end:
        block_row = row // tall
        stop = min(end, (block_row + 1) * tall)
        for j in range(wide):
            blocks[block_row * across + col_at + j, row - block_row * tall : stop - block_row * tall, :] = product[
                row - begin : stop - begin, j * LANES : (j + 1) * LANES
            ]
        row = stop


def grads_body(
    at, c0, c1, c2, c3, s0, s1, s2, s3, wo, attended, probs, factors, blocks
):
    quarter = c0.shape[1]
    length = c0.shape[0]
    h, c, zb = at[0], at[1], at[2]
    places = [2 * h + c, 2 * h + 1 - c, 2 * (1 - h) + c, 2 * (1 - h) + 1 - c]
    grads = None
    for part, place in zip((c0, c1, c2, c3), places):
        cols = pl.ds(pl.multiple_of(place * quarter, quarter), quarter)
        term = dot(part[...], wo[:, cols], ((1,), (1,)))
        grads = term if grads is None else grads + term
    low = lower_half((length, LANES))
    group_size = HEADS // KV_HEADS
    tiles = grads.shape[1] // LANES
    sums = []
    for g in range(2):
        stacked = []
        for t in range(g * group_size // 2, (g + 1) * group_size // 2):
            tile = grads[:, t * LANES : (t + 1) * LANES]
            stacked.append(jnp.where(low, tile, 0.0).astype(jnp.bfloat16))
            stacked.append(jnp.where(low, 0.0, tile).astype(jnp.bfloat16))
        rows = group_size * length
        found = dot(probs[g * rows : (g + 1) * rows, :], jnp.concatenate(stacked, 0), ((0,), (0,)))
        sums.append(found + pltpu.roll(found, HEAD_DIM, 1))
    value_gradient = jnp.where(low, sums[0], sums[1]).astype(jnp.bfloat16)
    width = attended.shape[1]
    factors[:, :width] = attended[...]
    factors[:, width:] = value_gradient
    here = h == zb
    turned_a = attended[...].T
    turned_v = value_gradient.T
    swap = c == 1
    for k, ((cn, cf), (sn, sf)) in enumerate((((c0, c2), (s0, s2)), ((c1, c3), (s1, s3)))):
        cot = jnp.where(here, cn[...], cf[...])
        state = jnp.where(here, sn[...], sf[...])
        col_at = jnp.where(swap, 1 - k, k) * (quarter // LANES)
        put_blocks(blocks, turned_a, (0, width), cot, col_at)
        put_blocks(blocks, turned_v, (width, width + LANES), state, col_at)


def other_body(at, c0, c1, s0, s1, factors, blocks):
    quarter = c0.shape[1]
    width = factors.shape[1] - LANES
    swap = at[1] == 1
    turned_a = factors[:, :width].T
    turned_v = factors[:, width:].T
    for k, (cot, state) in enumerate(((c0, s0), (c1, s1))):
        col_at = jnp.where(swap, 1 - k, k) * (quarter // LANES)
        put_blocks(blocks, turned_a, (0, width), cot[...], col_at)
        put_blocks(blocks, turned_v, (width, width + LANES), state[...], col_at)


def share_body(at, own, other, rows_out, wide):
    zb = at[2]
    seqs, tall, _ = own.shape
    for k, ref in enumerate((own, other)):
        base = jnp.where(zb == k, 0, seqs)
        for s in range(seqs):
            start = pl.multiple_of((base + s) * tall, 8)
            wide[pl.ds(start, tall), :] = ref[s].astype(jnp.float32)
    total = jnp.zeros((2 * seqs, 2 * seqs), jnp.float32)
    for r in range(0, tall, 2):
        pair = [
            wide[pl.ds(r + k, 2 * seqs, stride=tall), :].astype(jnp.bfloat16) for k in range(2)
        ]
        x = jnp.concatenate(pair, axis=1)
        total = total + dot(x, x, ((1,), (1,)))
    eye = lax.broadcasted_iota(jnp.int32, total.shape, 0) == lax.broadcasted_iota(
        jnp.int32, total.shape, 1
    )
    diag = jnp.sum(jnp.where(eye, total, 0.0), axis=0, keepdims=True)
    rows = jnp.concatenate([total, jnp.broadcast_to(diag, total.shape)], axis=1)
    copies = rows_out.shape[0] // rows.shape[0]
    for k in range(copies):
        rows_out[pl.ds(k, rows.shape[0], stride=copies), :] = rows


def final_body(at, got, out):
    seqs = out.shape[1]
    total = jnp.sum(got[...], axis=0, keepdims=True)
    lane = lax.broadcasted_iota(jnp.int32, total.shape, 1)
    own_diag = jnp.sum(jnp.where(lane == at[3] + seqs, total, 0.0), axis=1, keepdims=True)
    diag = pltpu.roll(total, seqs, 1)
    out[...] = (total / jnp.sqrt(own_diag * diag))[:, :seqs]


def on_device(states, cotangent, wq, wk, wv, wo):
    bf16, f32 = jnp.bfloat16, jnp.float32
    length, part = states.shape[1:]
    at = jnp.stack([lax.axis_index("h"), lax.axis_index("c"), lax.axis_index("zb"), lax.axis_index(SEQ)])
    at = at.astype(jnp.int32)
    zb_is_0 = lax.axis_index("zb") == 0
    h_is_0 = lax.axis_index("h") == 0

    def gathered(own):
        far = swapped(own, "h")
        return own, swapped(own, "c"), far, swapped(far, "c")

    s = gathered(states[0])
    k = gathered(cotangent[0])
    cos, sine = rope_tables(length, HEAD_DIM)
    attended, probs = kernel_call(
        attention_body,
        (
            jax.ShapeDtypeStruct((length, part), bf16),
            jax.ShapeDtypeStruct((part // HEAD_DIM * length, length), bf16),
        ),
        (at, *s, wq, wk, wv, cos, sine),
    )
    blocks = lax.axis_size(NEAR)
    tall = (part + LANES) * (2 * part) // (LANES * blocks)
    block_shape = jax.ShapeDtypeStruct((blocks, tall, LANES), bf16)
    factors, own_blocks = kernel_call(
        grads_body,
        (jax.ShapeDtypeStruct((length, part + LANES), bf16), block_shape),
        (at, *k, *s, wo, attended, probs),
    )
    got_own = lax.all_to_all(own_blocks, NEAR, 0, 0, tiled=True)

    def partner(parts):
        own, _, far, _ = parts
        piece = swapped(jnp.where(h_is_0 == zb_is_0, far, own), "zb")
        return piece, swapped(piece, "c")

    other_factors = swapped(factors, "zb")
    other_blocks = kernel_call(
        other_body, block_shape, (at, *partner(k), *partner(s), other_factors)
    )
    got_other = lax.all_to_all(other_blocks, NEAR, 0, 0, tiled=True)
    seqs = 2 * blocks
    copies = lax.axis_size(TP)
    rows = kernel_call(
        share_body,
        jax.ShapeDtypeStruct((seqs * copies, 2 * seqs), f32),
        (at, got_own, got_other),
        (pltpu.VMEM((seqs * tall, LANES), f32),),
    )
    rows = rows.reshape(seqs * copies, 1, 2 * seqs)
    got = lax.all_to_all(rows, EVERY, 0, 0, tiled=True).reshape(seqs * copies, 2 * seqs)
    return kernel_call(final_body, jax.ShapeDtypeStruct((1, seqs), f32), (at, got))


def solution(mesh):
    split = Mesh(mesh.devices.reshape(2, mesh.shape["seq"] // 32, 4, 4, 2, 2), EVERY)
    placed = (
        P(SEQ, None, TP),
        P(SEQ, None, TP),
        P(None, TP),
        P(None, TP),
        P(None, TP),
        P(TP, None),
    )
    return jax.shard_map(
        on_device, mesh=split, in_specs=placed, out_specs=P(SEQ, None), check_vma=False
    )
```

time: 133 us -> 122 us (0.917)
  blocking collectives: 0 us -> 47.7 us
  waiting for transfers between devices: 63.3 us -> 27.1 us
  Pallas kernels: 0 us -> 13.9 us
  starting transfers between devices: 40.1 us -> 28 us
  matrix products: 11.7 us -> 0 us
  other arithmetic: 7.89 us -> 0.27 us
  local copies, waits for them, and re-layouts: 9.57 us -> 4.78 us
    all_to_all x0 -> x2, blocking collectives: none -> 47.7 us  [the longest x1 24.2 us: on_device(): lax.all_to_all(rows, EVERY, 0, 0, tiled=True)]
    all_to_all x2 -> x1, waiting for transfers between devices: 45.7 us -> 2.96 us  [on_device(): got_own = lax.all_to_all(own_blocks, NEAR, 0, 0, tiled=True)]
    pallas_call x0 -> x5, Pallas kernels: none -> 13.9 us  [kernel_call(): pl.pallas_call(body, out_shape=outs, in_specs=[smem if a.dtype == jnp.int...]
    all_to_all x2 -> x1, starting transfers between devices: 20.7 us -> 7.37 us  [on_device(): got_own = lax.all_to_all(own_blocks, NEAR, 0, 0, tiled=True)]
    dot_general x11 -> x0, matrix products: 8.9 us -> none  [the longest x3 3.81 us: project(): return jnp.dot(full_states, w, preferred_element_type=jnp.float32)]
    ppermute x11, waiting for transfers between devices: 17.6 us -> 24.1 us  [swapped(): return lax.ppermute(value, axis, SWAP)]
    unnamed x10 -> x14, local copies, waits for them, and re-layouts: 0.74 us -> 4.59 us
    transpose x1 -> x0, local copies, waits for them, and re-layouts: 3.43 us -> none  [on_device(): got = jnp.swapaxes(got, 0, 1).reshape(seqs, *got.shape[2:])]
  transfers between devices with their start and end apart: 13 -> 12, of which waited for: 5 -> 7; matrix products, arithmetic and copies ran while one was open for 13% -> 0% of each run, Pallas kernels for 0% -> 4%
where the time goes in v2:
time: 122 us
  blocking collectives  47.7 us (39%)
  starting transfers between devices  28 us (23%)
  waiting for transfers between devices  27.1 us (22%)
  Pallas kernels  13.9 us (11%)
  local copies, waits for them, and re-layouts  4.78 us (4%)
    all_to_all x1, blocking collectives, on_device(): lax.all_to_all(rows, EVERY, 0, 0, tiled=True)  24.2 us
    ppermute x11, waiting for transfers between devices, swapped(): return lax.ppermute(value, axis, SWAP)  24.1 us
    all_to_all x1, blocking collectives, on_device(): got_other = lax.all_to_all(other_blocks, NEAR, 0, 0, tiled=True)  23.5 us
    ppermute x11, starting transfers between devices, swapped(): return lax.ppermute(value, axis, SWAP)  20.6 us
    pallas_call x5, Pallas kernels, kernel_call(): pl.pallas_call(body, out_shape=outs, in_specs=[smem if a.dtype == jnp.int...  13.9 us
    all_to_all x1, starting transfers between devices, on_device(): got_own = lax.all_to_all(own_blocks, NEAR, 0, 0, tiled=True)  7.37 us
    unnamed x14, local copies, waits for them, and re-layouts  4.59 us
    all_to_all x1, waiting for transfers between devices, on_device(): got_own = lax.all_to_all(own_blocks, NEAR, 0, 0, tiled=True)  2.96 us
  transfers between devices with their start and end apart: 12, of which 7 were waited for; matrix products, arithmetic and copies ran while one was open for 0% of the time, Pallas kernels for 4%

profile of v2, /device:TPU:1, one launch (start us, length us, event | category | flops | bytes accessed | tf_op | source)
XLA Modules:
  0.0 121.9 jit_solution(18310637116641610804)
XLA Ops:
  0.0 7.7 %collective-permute-start.4 = (bf16[128,512]{1,0:T(8,128)(2,1)}, bf16[128,512]{1,0:T(8,128)(2,1)S(1)}, u32[]{:S(2)}, u32[]{:S(2)}) collective-permute-start(bf16[128,512]{1,0:T(8,128)(2,1)} %bitcast.14), channel_id=1, source_target_pairs={{0,2},{2,0},{1,3},{3,1},{4,6},{6,4},{5,7},{7,5},{8,10},{10,8},{9,1... | collective-permute-start | bytes 393224 | tf_op jit(solution)/shard_map/ppermute | solution.py:25
  7.7 1.0 collective-permute-start.3
  9.3 1.4 %collective-permute-done.4.s2 = bf16[128,512]{1,0:T(8,128)(2,1)S(1)} collective-permute-done((bf16[128,512]{1,0:T(8,128)(2,1)}, bf16[128,512]{1,0:T(8,128)(2,1)S(1)}, u32[]{:S(2)}, u32[]{:S(2)}) %collective-permute-start.4) | collective-permute-done | bytes 131104 | tf_op jit(solution)/shard_map/ppermute | solution.py:25
  10.7 5.3 %collective-permute-start.5 = (bf16[128,512]{1,0:T(8,128)(2,1)S(1)}, bf16[128,512]{1,0:T(8,128)(2,1)S(1)}, u32[]{:S(2)}, u32[]{:S(2)}) collective-permute-start(bf16[128,512]{1,0:T(8,128)(2,1)S(1)} %collective-permute-done.4.s2), channel_id=1, source_target_pairs={{0,1},{1,0},{2,3},{3,2},{4,5},{5,4},{6,7},{7,6},{8,9},{9,8},{10,11... | collective-permute-start | bytes 393224 | tf_op jit(solution)/shard_map/ppermute | solution.py:25
  16.0 4.9 %collective-permute-done.1.c2 = bf16[128,512]{1,0:T(8,128)(2,1)S(1)} collective-permute-done((bf16[128,512]{1,0:T(8,128)(2,1)}, bf16[128,512]{1,0:T(8,128)(2,1)S(1)}, u32[]{:S(2)}, u32[]{:S(2)}) %collective-permute-start.1) | collective-permute-done | bytes 131104 | tf_op jit(solution)/shard_map/ppermute | solution.py:25
  22.1 1.6 %copy-done = bf16[2048,512]{1,0:T(8,128)(2,1)S(1)} copy-done((bf16[2048,512]{1,0:T(8,128)(2,1)S(1)}, bf16[2048,512]{1,0:T(8,128)(2,1)}, u32[]{:S(2)}) %copy-start) | copy-done | bytes 2097176
  24.6 1.0 copy-done.4
  25.6 1.0 copy-done.5
  26.7 3.8 %shard_map.64 = (bf16[128,512]{1,0:T(8,128)(2,1)S(1)}, bf16[1024,128]{1,0:T(8,128)(2,1)S(1)}) custom-call(s32[4]{0:T(128)S(1)} %pad_add_fusion.at, bf16[128,512]{1,0:T(8,128)(2,1)S(1)} %bitcast.16, bf16[128,512]{1,0:T(8,128)(2,1)S(1)} %collective-permute-done.3.s1, bf16[128,512]{1,0:T(8,128)(2,1)S(1)} %collective-permute-done.4.s2, ...), custom_call_target="tpu_custom_call" | custom-call | tf_op jit(solution)/shard_map/pallas_call | solution.py:44
  30.5 3.1 %shard_map.65 = (bf16[128,640]{1,0:T(8,128)(2,1)S(1)}, bf16[32,160,128]{2,1,0:T(8,128)(2,1)}) custom-call(s32[4]{0:T(128)S(1)} %pad_add_fusion.at, bf16[128,512]{1,0:T(8,128)(2,1)S(1)} %bitcast.22, bf16[128,512]{1,0:T(8,128)(2,1)S(1)} %collective-permute-done.c1, bf16[128,512]{1,0:T(8,128)(2,1)S(1)} %collective-permute-done.1.c2, ...), custom_call_target="tpu_custom_call" | custom-call | tf_op jit(solution)/shard_map/pallas_call | solution.py:44
  33.6 7.4 %all-to-all-start = ((bf16[32,160,128]{2,1,0:T(8,128)(2,1)}), bf16[32,160,128]{2,1,0:T(8,128)(2,1)S(1)}, u32[]{:S(2)}, u32[]{:S(2)}) async-start(bf16[32,160,128]{2,1,0:T(8,128)(2,1)} %get-tuple-element.11), calls=%async_computation | async-start | bytes 2621440 | tf_op jit(solution)/shard_map/all_to_all | solution.py:248
  41.1 2.4 %collective-permute-start.6 = (bf16[128,512]{1,0:T(8,128)(2,1)S(1)}, bf16[128,512]{1,0:T(8,128)(2,1)S(1)}, u32[]{:S(2)}, u32[]{:S(2)}) collective-permute-start(bf16[128,512]{1,0:T(8,128)(2,1)S(1)} %broadcast_select_fusion.1), channel_id=1, source_target_pairs={{0,128},{128,0},{1,129},{129,1},{2,130},{130,2},{3,131},{131,3},{4... | collective-permute-start | bytes 393224 | tf_op jit(solution)/shard_map/ppermute | solution.py:25
  43.7 14.2 %collective-permute-done.8.s0 = bf16[128,512]{1,0:T(8,128)(2,1)S(1)} collective-permute-done((bf16[128,512]{1,0:T(8,128)(2,1)S(1)}, bf16[128,512]{1,0:T(8,128)(2,1)S(1)}, u32[]{:S(2)}, u32[]{:S(2)}) %collective-permute-start.8) | collective-permute-done | bytes 131104 | tf_op jit(solution)/shard_map/ppermute | solution.py:25
  57.8 1.3 %collective-permute-start.9 = (bf16[128,512]{1,0:T(8,128)(2,1)S(1)}, bf16[128,512]{1,0:T(8,128)(2,1)S(1)}, u32[]{:S(2)}, u32[]{:S(2)}) collective-permute-start(bf16[128,512]{1,0:T(8,128)(2,1)S(1)} %collective-permute-done.8.s0), channel_id=1, source_target_pairs={{0,1},{1,0},{2,3},{3,2},{4,5},{5,4},{6,7},{7,6},{8,9},{9,8},{10,11... | collective-permute-start | bytes 393224 | tf_op jit(solution)/shard_map/ppermute | solution.py:25
  59.2 1.5 %collective-permute-done.6.c0 = bf16[128,512]{1,0:T(8,128)(2,1)S(1)} collective-permute-done((bf16[128,512]{1,0:T(8,128)(2,1)S(1)}, bf16[128,512]{1,0:T(8,128)(2,1)S(1)}, u32[]{:S(2)}, u32[]{:S(2)}) %collective-permute-start.6) | collective-permute-done | bytes 131104 | tf_op jit(solution)/shard_map/ppermute | solution.py:25
  60.6 1.3 %collective-permute-start.7 = (bf16[128,512]{1,0:T(8,128)(2,1)S(1)}, bf16[128,512]{1,0:T(8,128)(2,1)S(1)}, u32[]{:S(2)}, u32[]{:S(2)}) collective-permute-start(bf16[128,512]{1,0:T(8,128)(2,1)S(1)} %collective-permute-done.6.c0), channel_id=1, source_target_pairs={{0,1},{1,0},{2,3},{3,2},{4,5},{5,4},{6,7},{7,6},{8,9},{9,8},{10,11... | collective-permute-start | bytes 393224 | tf_op jit(solution)/shard_map/ppermute | solution.py:25
  62.0 1.0 collective-permute-done.7.c1
  63.0 1.2 collective-permute-done.10.factors
  64.2 1.1 shard_map.66
  65.2 3.0 %all-to-all-done.own = bf16[32,160,128]{2,1,0:T(8,128)(2,1)S(1)} async-done(((bf16[32,160,128]{2,1,0:T(8,128)(2,1)}), bf16[32,160,128]{2,1,0:T(8,128)(2,1)S(1)}, u32[]{:S(2)}, u32[]{:S(2)}) %all-to-all-start) | async-done | bytes 1310752 | tf_op jit(solution)/shard_map/all_to_all | solution.py:248
  68.2 23.5 %all_to_all.15.other = bf16[32,160,128]{2,1,0:T(8,128)(2,1)S(1)} all-to-all(bf16[32,160,128]{2,1,0:T(8,128)(2,1)S(1)} %shard_map.66), channel_id=1, replica_groups=mesh['zb'=2,'za'=2,'x'=4,'y'=4,'h'=2,'c'=2] {'za','x','y'}, dimensions={0} | all-to-all | bytes 2621440 | tf_op jit(solution)/shard_map/all_to_all | solution.py:259
  91.7 4.8 %shard_map.67 = f32[256,128]{1,0:T(8,128)S(1)} custom-call(s32[4]{0:T(128)S(1)} %pad_add_fusion.at, bf16[32,160,128]{2,1,0:T(8,128)(2,1)S(1)} %all-to-all-done.own, bf16[32,160,128]{2,1,0:T(8,128)(2,1)S(1)} %all_to_all.15.other), custom_call_target="tpu_custom_call" | custom-call | tf_op jit(solution)/shard_map/pallas_call | solution.py:44
  96.5 24.2 %all_to_all.16 = f32[256,1,128]{2,1,0:T(1,128)S(1)} all-to-all(f32[256,1,128]{2,1,0:T(1,128)S(1)} %bitcast.18), channel_id=1, replica_groups=mesh['zb'=2,'za'=2,'x'=4,'y'=4,'h'=2,'c'=2] {'zb','za','x','y','h','c'}, dimensions={0} | all-to-all | bytes 262144 | tf_op jit(solution)/shard_map/all_to_all | solution.py:269
  120.7 1.2 shard_map.68
  (31 shorter events, 2.9 us)
Async XLA Ops:
  0.0 10.7 %collective-permute-start.4 = (bf16[128,512]{1,0:T(8,128)(2,1)}, bf16[128,512]{1,0:T(8,128)(2,1)S(1)}, u32[]{:S(2)}, u32[]{:S(2)}) collective-permute-start(bf16[128,512]{1,0:T(8,128)(2,1)} %bitcast.14), channel_id=1, source_target_pairs={{0,2},{2,0},{1,3},{3,1},{4,6},{6,4},{5,7},{7,5},{8,10},{10,8},{9,1... | collective-permute-start | bytes 393224 | tf_op jit(solution)/shard_map/ppermute | solution.py:25
  7.7 14.4 %collective-permute-start.3 = (bf16[128,512]{1,0:T(8,128)(2,1)}, bf16[128,512]{1,0:T(8,128)(2,1)S(1)}, u32[]{:S(2)}, u32[]{:S(2)}) collective-permute-start(bf16[128,512]{1,0:T(8,128)(2,1)} %bitcast.15), channel_id=1, source_target_pairs={{0,1},{1,0},{2,3},{3,2},{4,5},{5,4},{6,7},{7,6},{8,9},{9,8},{10,11... | collective-permute-start | bytes 393224 | tf_op jit(solution)/shard_map/ppermute | solution.py:25
  8.7 12.2 %collective-permute-start.1 = (bf16[128,512]{1,0:T(8,128)(2,1)}, bf16[128,512]{1,0:T(8,128)(2,1)S(1)}, u32[]{:S(2)}, u32[]{:S(2)}) collective-permute-start(bf16[128,512]{1,0:T(8,128)(2,1)} %bitcast.20), channel_id=1, source_target_pairs={{0,2},{2,0},{1,3},{3,1},{4,6},{6,4},{5,7},{7,5},{8,10},{10,8},{9,1... | collective-permute-start | bytes 393224 | tf_op jit(solution)/shard_map/ppermute | solution.py:25
  8.9 21.6 %collective-permute-start = (bf16[128,512]{1,0:T(8,128)(2,1)}, bf16[128,512]{1,0:T(8,128)(2,1)S(1)}, u32[]{:S(2)}, u32[]{:S(2)}) collective-permute-start(bf16[128,512]{1,0:T(8,128)(2,1)} %bitcast.21), channel_id=1, source_target_pairs={{0,1},{1,0},{2,3},{3,2},{4,5},{5,4},{6,7},{7,6},{8,9},{9,8},{10,11... | collective-permute-start | bytes 393224 | tf_op jit(solution)/shard_map/ppermute | solution.py:25
  10.7 11.4 %collective-permute-start.5 = (bf16[128,512]{1,0:T(8,128)(2,1)S(1)}, bf16[128,512]{1,0:T(8,128)(2,1)S(1)}, u32[]{:S(2)}, u32[]{:S(2)}) collective-permute-start(bf16[128,512]{1,0:T(8,128)(2,1)S(1)} %collective-permute-done.4.s2), channel_id=1, source_target_pairs={{0,1},{1,0},{2,3},{3,2},{4,5},{5,4},{6,7},{7,6},{8,9},{9,8},{10,11... | collective-permute-start | bytes 393224 | tf_op jit(solution)/shard_map/ppermute | solution.py:25
  20.9 9.6 %collective-permute-start.2 = (bf16[128,512]{1,0:T(8,128)(2,1)S(1)}, bf16[128,512]{1,0:T(8,128)(2,1)S(1)}, u32[]{:S(2)}, u32[]{:S(2)}) collective-permute-start(bf16[128,512]{1,0:T(8,128)(2,1)S(1)} %collective-permute-done.1.c2), channel_id=1, source_target_pairs={{0,1},{1,0},{2,3},{3,2},{4,5},{5,4},{6,7},{7,6},{8,9},{9,8},{10,11... | collective-permute-start | bytes 393224 | tf_op jit(solution)/shard_map/ppermute | solution.py:25
  22.1 1.6 %copy-start = (bf16[2048,512]{1,0:T(8,128)(2,1)S(1)}, bf16[2048,512]{1,0:T(8,128)(2,1)}, u32[]{:S(2)}) copy-start(bf16[2048,512]{1,0:T(8,128)(2,1)} %wq.1) | copy-start | bytes 6291460
  23.7 0.9 copy-start.2
  24.6 1.0 copy-start.4
  25.6 1.0 copy-start.5
  26.7 3.8 %copy-start.1 = (bf16[512,2048]{1,0:T(8,128)(2,1)S(1)}, bf16[512,2048]{1,0:T(8,128)(2,1)}, u32[]{:S(2)}) copy-start(bf16[512,2048]{1,0:T(8,128)(2,1)} %wo.1) | copy-start | bytes 6291460
  26.7 3.8 %copy-start.6 = (bf16[1,128,512]{2,1,0:T(8,128)(2,1)S(1)}, bf16[1,128,512]{2,1,0:T(8,128)(2,1)}, u32[]{:S(2)}) copy-start(bf16[1,128,512]{2,1,0:T(8,128)(2,1)} %param.7) | copy-start | bytes 393220
  33.6 7.4 %copy-start.3 = (bf16[1,128,512]{2,1,0:T(8,128)(2,1)S(1)}, bf16[1,128,512]{2,1,0:T(8,128)(2,1)}, u32[]{:S(2)}) copy-start(bf16[1,128,512]{2,1,0:T(8,128)(2,1)} %param.6) | copy-start | bytes 393220
  33.6 34.6 %all-to-all-start = ((bf16[32,160,128]{2,1,0:T(8,128)(2,1)}), bf16[32,160,128]{2,1,0:T(8,128)(2,1)S(1)}, u32[]{:S(2)}, u32[]{:S(2)}) async-start(bf16[32,160,128]{2,1,0:T(8,128)(2,1)} %get-tuple-element.11), calls=%async_computation | async-start | bytes 2621440 | tf_op jit(solution)/shard_map/all_to_all | solution.py:248
  41.0 16.8 %collective-permute-start.8 = (bf16[128,512]{1,0:T(8,128)(2,1)S(1)}, bf16[128,512]{1,0:T(8,128)(2,1)S(1)}, u32[]{:S(2)}, u32[]{:S(2)}) collective-permute-start(bf16[128,512]{1,0:T(8,128)(2,1)S(1)} %broadcast_select_fusion), channel_id=1, source_target_pairs={{0,128},{128,0},{1,129},{129,1},{2,130},{130,2},{3,131},{131,3},{4... | collective-permute-start | bytes 393224 | tf_op jit(solution)/shard_map/ppermute | solution.py:25
  41.1 19.5 %collective-permute-start.6 = (bf16[128,512]{1,0:T(8,128)(2,1)S(1)}, bf16[128,512]{1,0:T(8,128)(2,1)S(1)}, u32[]{:S(2)}, u32[]{:S(2)}) collective-permute-start(bf16[128,512]{1,0:T(8,128)(2,1)S(1)} %broadcast_select_fusion.1), channel_id=1, source_target_pairs={{0,128},{128,0},{1,129},{129,1},{2,130},{130,2},{3,131},{131,3},{4... | collective-permute-start | bytes 393224 | tf_op jit(solution)/shard_map/ppermute | solution.py:25
  43.6 20.6 %collective-permute-start.10 = (bf16[128,640]{1,0:T(8,128)(2,1)S(1)}, bf16[128,640]{1,0:T(8,128)(2,1)S(1)}, u32[]{:S(2)}, u32[]{:S(2)}) collective-permute-start(bf16[128,640]{1,0:T(8,128)(2,1)S(1)} %get-tuple-element.12), channel_id=1, source_target_pairs={{0,128},{128,0},{1,129},{129,1},{2,130},{130,2},{3,131},{131,3},{4... | collective-permute-start | bytes 491528 | tf_op jit(solution)/shard_map/ppermute | solution.py:25
  57.8 4.1 %collective-permute-start.9 = (bf16[128,512]{1,0:T(8,128)(2,1)S(1)}, bf16[128,512]{1,0:T(8,128)(2,1)S(1)}, u32[]{:S(2)}, u32[]{:S(2)}) collective-permute-start(bf16[128,512]{1,0:T(8,128)(2,1)S(1)} %collective-permute-done.8.s0), channel_id=1, source_target_pairs={{0,1},{1,0},{2,3},{3,2},{4,5},{5,4},{6,7},{7,6},{8,9},{9,8},{10,11... | collective-permute-start | bytes 393224 | tf_op jit(solution)/shard_map/ppermute | solution.py:25
  60.6 2.3 %collective-permute-start.7 = (bf16[128,512]{1,0:T(8,128)(2,1)S(1)}, bf16[128,512]{1,0:T(8,128)(2,1)S(1)}, u32[]{:S(2)}, u32[]{:S(2)}) collective-permute-start(bf16[128,512]{1,0:T(8,128)(2,1)S(1)} %collective-permute-done.6.c0), channel_id=1, source_target_pairs={{0,1},{1,0},{2,3},{3,2},{4,5},{5,4},{6,7},{7,6},{8,9},{9,8},{10,11... | collective-permute-start | bytes 393224 | tf_op jit(solution)/shard_map/ppermute | solution.py:25

commit v3 on v2

v3 whole, which is shorter than its diff:
```python
import jax
import jax.numpy as jnp
from jax import lax
from jax.experimental import pallas as pl
from jax.experimental.pallas import tpu as pltpu
from jax.sharding import Mesh
from jax.sharding import PartitionSpec as P


HEADS = 32
KV_HEADS = 8
HEAD_DIM = 64
LANES = 128
SEQ = ("zb", "za", "x", "y")
NEAR = ("za", "x", "y")
TP = ("h", "c")
EVERY = SEQ + TP
SWAP = ((0, 1), (1, 0))

theta_base = 500000.0


def swapped(value, axis):
    return lax.ppermute(value, axis, SWAP)


def rope_tables(length, head_dim):
    half_dim = head_dim // 2
    freqs_k = theta_base ** (-(jnp.arange(half_dim, dtype=jnp.float32) * 2.0 / head_dim))
    angles = jnp.arange(length, dtype=jnp.float32)[:, None] * freqs_k[None, :]
    sine = jnp.sin(angles)
    cos = jnp.tile(jnp.cos(angles), (1, LANES // half_dim))
    return cos, jnp.tile(jnp.concatenate([-sine, sine], axis=1), (1, LANES // head_dim))


def dot(left, right, dims=((1,), (0,))):
    return lax.dot_general(left, right, (dims, ((), ())), preferred_element_type=jnp.float32)


def kernel_call(body, outs, ins, scratch=(), vmem_mib=16, far=()):
    hbm = pl.BlockSpec(memory_space=pl.ANY)
    smem = pl.BlockSpec(memory_space=pltpu.SMEM)
    vmem = pl.BlockSpec(memory_space=pltpu.VMEM)
    return pl.pallas_call(
        body,
        out_shape=outs,
        in_specs=[
            hbm if i in far else smem if a.dtype == jnp.int32 else vmem for i, a in enumerate(ins)
        ],
        out_specs=jax.tree.map(lambda _: vmem, outs),
        scratch_shapes=scratch,
        compiler_params=pltpu.CompilerParams(vmem_limit_bytes=vmem_mib * 2**20),
    )(*ins)


def lower_half(shape):
    return lax.broadcasted_iota(jnp.int32, shape, 1) % (2 * HEAD_DIM) < HEAD_DIM


def doubled(pair, low):
    turned = pltpu.roll(pair, HEAD_DIM, 1)
    return jnp.where(low, pair, turned), jnp.where(low, turned, pair)


def places_of(at):
    h, c = at[0], at[1]
    return [2 * h + c, 2 * h + 1 - c, 2 * (1 - h) + c, 2 * (1 - h) + 1 - c]


def rows_at(place, size):
    return pl.ds(pl.multiple_of(place * size, size), size)


def start_body(
    at, s0, s1, c0, c1, wq, wk, wv, wo, s_out, c_out, wq_out, wk_out, wv_out, wo_out, sums, grads, sems
):
    moves = [
        pltpu.make_async_copy(src, dst, sems.at[i])
        for i, (src, dst) in enumerate(
            ((wq, wq_out), (wk, wk_out), (wv, wv_out), (wo, wo_out), (s0, s_out), (c0, c_out))
        )
    ]
    for move in moves:
        move.start()
    for move in moves:
        move.wait()
    quarter = s_out.shape[1]
    near = places_of(at)[:2]
    begin = 0
    for w in (wq_out, wk_out, wv_out):
        end = begin + w.shape[1]
        sums[:, begin:end] = dot(s_out[...], w[rows_at(near[0], quarter), :]) + dot(
            s1[...], w[rows_at(near[1], quarter), :]
        )
        begin = end
    nt = ((1,), (1,))
    grads[...] = dot(c_out[...], wo_out[:, rows_at(near[0], quarter)], nt) + dot(
        c1[...], wo_out[:, rows_at(near[1], quarter)], nt
    )


def attention_body(at, s2, s3, wq, wk, wv, sums, cos_ref, sine_ref, attended, probs):
    quarter = s2.shape[1]
    far = places_of(at)[2:]

    def project(w, begin):
        total = sums[:, begin : begin + w.shape[1]]
        for part, place in zip((s2, s3), far):
            total = total + dot(part[...], w[rows_at(place, quarter), :])
        return total

    cos, sine = cos_ref[...], sine_ref[...]
    length = cos.shape[0]
    lane = lax.broadcasted_iota(jnp.int32, cos.shape, 1)
    first = lane % HEAD_DIM < HEAD_DIM // 2
    low = lower_half(cos.shape)

    def rotate(tile):
        ahead = pltpu.roll(tile, LANES - HEAD_DIM // 2, 1)
        behind = pltpu.roll(tile, HEAD_DIM // 2, 1)
        return tile * cos + jnp.where(first, ahead, behind) * sine

    width = wq.shape[1]
    keys = [k.astype(jnp.bfloat16) for k in doubled(rotate(project(wk, width)), low)]
    values = [v.astype(jnp.bfloat16) for v in doubled(project(wv, width + LANES), low)]
    queries = project(wq, 0)
    causal = lax.broadcasted_iota(jnp.int32, (length, length), 0) >= lax.broadcasted_iota(
        jnp.int32, (length, length), 1
    )
    for t in range(width // LANES):
        group = 2 * t // (HEADS // KV_HEADS)
        query = rotate(queries[:, t * LANES : (t + 1) * LANES])
        found = []
        for s in range(2):
            mine = low if s == 0 else jnp.logical_not(low)
            q = jnp.where(mine, query, 0.0).astype(jnp.bfloat16)
            scores = dot(q, keys[group], ((1,), (1,))) * HEAD_DIM ** (-0.5)
            scores = jnp.where(causal, scores, -jnp.inf)
            e = jnp.exp(scores - jnp.max(scores, axis=1, keepdims=True))
            p = (e / jnp.sum(e, axis=1, keepdims=True)).astype(jnp.bfloat16)
            probs[(2 * t + s) * length : (2 * t + s + 1) * length, :] = p
            found.append(dot(p, values[group]))
        tile = jnp.where(low, found[0], found[1])
        attended[:, t * LANES : (t + 1) * LANES] = tile.astype(jnp.bfloat16)


def put_blocks(blocks, turned, kind_rows, cols, col_at):
    tall = blocks.shape[1]
    begin, end = kind_rows
    wide = cols.shape[1] // LANES
    across = 8
    product = dot(turned, cols).astype(jnp.bfloat16)
    row = begin
    while row < end:
        block_row = row // tall
        stop = min(end, (block_row + 1) * tall)
        for j in range(wide):
            blocks[block_row * across + col_at + j, row - block_row * tall : stop - block_row * tall, :] = product[
                row - begin : stop - begin, j * LANES : (j + 1) * LANES
            ]
        row = stop


def grads_body(at, c2, c3, wo, partial, attended, probs, factors):
    length, quarter = c2.shape
    grads = partial[...]
    for part, place in zip((c2, c3), places_of(at)[2:]):
        grads = grads + dot(part[...], wo[:, rows_at(place, quarter)], ((1,), (1,)))
    low = lower_half((length, LANES))
    group_size = HEADS // KV_HEADS
    sums = []
    for g in range(2):
        stacked = []
        for t in range(g * group_size // 2, (g + 1) * group_size // 2):
            tile = grads[:, t * LANES : (t + 1) * LANES]
            stacked.append(jnp.where(low, tile, 0.0).astype(jnp.bfloat16))
            stacked.append(jnp.where(low, 0.0, tile).astype(jnp.bfloat16))
        rows = group_size * length
        found = dot(probs[g * rows : (g + 1) * rows, :], jnp.concatenate(stacked, 0), ((0,), (0,)))
        sums.append(found + pltpu.roll(found, HEAD_DIM, 1))
    width = attended.shape[1]
    factors[:, :width] = attended[...]
    factors[:, width:] = jnp.where(low, sums[0], sums[1]).astype(jnp.bfloat16)


def put_all(at, factors, cots, states, blocks):
    width = factors.shape[1] - LANES
    turned_a = factors[:, :width].T
    turned_v = factors[:, width:].T
    for k, (cot, state) in enumerate(zip(cots, states)):
        col_at = jnp.where(at[1] == 1, 1 - k, k) * (cot.shape[1] // LANES)
        put_blocks(blocks, turned_a, (0, width), cot, col_at)
        put_blocks(blocks, turned_v, (width, width + LANES), state, col_at)


def own_body(at, c0, c1, c2, c3, s0, s1, s2, s3, factors, blocks):
    here = at[0] == at[2]

    def half(parts):
        return [jnp.where(here, parts[k][...], parts[k + 2][...]) for k in range(2)]

    put_all(at, factors, half((c0, c1, c2, c3)), half((s0, s1, s2, s3)), blocks)


def other_body(at, c0, c1, s0, s1, factors, blocks):
    put_all(at, factors, (c0[...], c1[...]), (s0[...], s1[...]), blocks)


def turn_blocks(got, wide, keep):
    seqs, tall, _ = got.shape
    for s in range(seqs):
        wide[pl.ds(s * tall, tall), :] = got[s].astype(jnp.float32)
    for r in range(tall):
        keep(r, wide[pl.ds(r, seqs, stride=tall), :].astype(jnp.bfloat16))


def turn_body(got, turned, wide):
    def keep(r, rows):
        turned[r] = rows

    turn_blocks(got, wide, keep)


def share_body(at, own, other, rows_out, wide):
    _, seqs, _ = own.shape
    straight = at[2] == 0
    total = jnp.zeros((2 * seqs, 2 * seqs), jnp.float32)
    waiting = []

    def keep(r, rows):
        nonlocal total
        mine = own[r]
        waiting.append(
            jnp.concatenate([jnp.where(straight, mine, rows), jnp.where(straight, rows, mine)], axis=0)
        )
        if len(waiting) == 2:
            x = jnp.concatenate(waiting, axis=1)
            total = total + dot(x, x, ((1,), (1,)))
            waiting.clear()

    turn_blocks(other, wide, keep)
    eye = lax.broadcasted_iota(jnp.int32, total.shape, 0) == lax.broadcasted_iota(
        jnp.int32, total.shape, 1
    )
    diag = jnp.sum(jnp.where(eye, total, 0.0), axis=0, keepdims=True)
    rows = jnp.concatenate([total, jnp.broadcast_to(diag, total.shape)], axis=1)
    copies = rows_out.shape[0] // rows.shape[0]
    for k in range(copies):
        rows_out[pl.ds(k, rows.shape[0], stride=copies), :] = rows


def final_body(at, got, out):
    seqs = out.shape[1]
    total = jnp.sum(got[...], axis=0, keepdims=True)
    lane = lax.broadcasted_iota(jnp.int32, total.shape, 1)
    own_diag = jnp.sum(jnp.where(lane == at[3] + seqs, total, 0.0), axis=1, keepdims=True)
    diag = pltpu.roll(total, seqs, 1)
    out[...] = (total / jnp.sqrt(own_diag * diag))[:, :seqs]


def on_device(states, cotangent, wq, wk, wv, wo):
    bf16, f32 = jnp.bfloat16, jnp.float32
    shape = jax.ShapeDtypeStruct
    length, part = states.shape[1:]
    states, cotangent = states[0], cotangent[0]
    axes = (lax.axis_index("h"), lax.axis_index("c"), lax.axis_index("zb"), lax.axis_index(SEQ))
    at = jnp.stack(axes).astype(jnp.int32)
    far_half = axes[0] == axes[2]
    blocks = lax.axis_size(NEAR)
    seqs = 2 * blocks
    tall = (part + LANES) * (2 * part) // (LANES * blocks)
    block_shape = shape((blocks, tall, LANES), bf16)
    wide = pltpu.VMEM((blocks * tall, LANES), f32)

    def gathered(own):
        far = swapped(own, "h")
        near = swapped(own, "c")
        return near, far, swapped(far, "c")

    def partner(own, far):
        piece = swapped(jnp.where(far_half, far, own), "zb")
        return piece, swapped(piece, "c")

    s1, s2, s3 = gathered(states)
    c1, c2, c3 = gathered(cotangent)
    cos, sine = rope_tables(length, HEAD_DIM)
    kv = wk.shape[1]
    s0, c0, wq, wk, wv, wo, sums, grads = kernel_call(
        start_body,
        (
            *(shape(a.shape, bf16) for a in (states, cotangent, wq, wk, wv, wo)),
            shape((length, part + 2 * kv), f32),
            shape((length, part), f32),
        ),
        (at, states, s1, cotangent, c1, wq, wk, wv, wo),
        (pltpu.SemaphoreType.DMA((6,)),),
        far=(1, 3, 5, 6, 7, 8),
    )
    attended, probs = kernel_call(
        attention_body,
        (shape((length, part), bf16), shape((part // HEAD_DIM * length, length), bf16)),
        (at, s2, s3, wq, wk, wv, sums, cos, sine),
    )
    factors = kernel_call(
        grads_body, shape((length, part + LANES), bf16), (at, c2, c3, wo, grads, attended, probs)
    )
    other_factors = swapped(factors, "zb")
    own_blocks = kernel_call(own_body, block_shape, (at, c0, c1, c2, c3, s0, s1, s2, s3, factors))
    got_own = lax.all_to_all(own_blocks, NEAR, 0, 0, tiled=True)
    other_blocks = kernel_call(
        other_body,
        block_shape,
        (at, *partner(c0, c2), *partner(s0, s2), other_factors),
    )
    got_other = lax.all_to_all(other_blocks, NEAR, 0, 0, tiled=True)
    own_turned = kernel_call(turn_body, shape((tall, blocks, LANES), bf16), (got_own,), (wide,))
    copies = lax.axis_size(TP)
    rows = kernel_call(
        share_body,
        shape((seqs * copies, 2 * seqs), f32),
        (at, own_turned, got_other),
        (wide,),
    )
    rows = rows.reshape(seqs * copies, 1, 2 * seqs)
    got = lax.all_to_all(rows, EVERY, 0, 0, tiled=True).reshape(seqs * copies, 2 * seqs)
    return kernel_call(final_body, shape((1, seqs), f32), (at, got))


def solution(mesh):
    split = Mesh(mesh.devices.reshape(2, mesh.shape["seq"] // 32, 4, 4, 2, 2), EVERY)
    placed = (
        P(SEQ, None, TP),
        P(SEQ, None, TP),
        P(None, TP),
        P(None, TP),
        P(None, TP),
        P(TP, None),
    )

    return jax.shard_map(
        on_device, mesh=split, in_specs=placed, out_specs=P(SEQ, None), check_vma=False
    )
```

time: 122 us -> 128 us (1.049)
  blocking collectives: 47.7 us -> 25 us
  waiting for transfers between devices: 27.1 us -> 38.8 us
  starting transfers between devices: 28 us -> 36.6 us
  local copies, waits for them, and re-layouts: 4.78 us -> 9.64 us
  Pallas kernels: 13.9 us -> 16.8 us
    all_to_all x1 -> x0, blocking collectives: 23.5 us -> none  [on_device(): got_other = lax.all_to_all(other_blocks, NEAR, 0, 0, tiled=True)]
    all_to_all x0 -> x1, waiting for transfers between devices: none -> 14.1 us  [on_device(): got_other = lax.all_to_all(other_blocks, NEAR, 0, 0, tiled=True)]
    all_to_all x0 -> x1, starting transfers between devices: none -> 7.36 us  [on_device(): got_other = lax.all_to_all(other_blocks, NEAR, 0, 0, tiled=True)]
    unnamed x14 -> x16, local copies, waits for them, and re-layouts: 4.59 us -> 9.45 us
    pallas_call x5 -> x8, Pallas kernels: 13.9 us -> 16.8 us  [kernel_call(): pl.pallas_call(body, out_shape=outs, in_specs=[hbm if i in far else smem...]
    ppermute x11, waiting for transfers between devices: 24.1 us -> 22.7 us  [swapped(): return lax.ppermute(value, axis, SWAP)]
  transfers between devices with their start and end apart: 12 -> 13, of which waited for: 7 -> 8; matrix products, arithmetic and copies ran while one was open for 0% -> 0% of each run, Pallas kernels for 4% -> 7%
where the time goes in v3:
time: 128 us; the launch traced here: 127 us
  waiting for transfers between devices  38.8 us (30%)
  starting transfers between devices  36.6 us (29%)
  blocking collectives  25 us (20%)
  Pallas kernels  16.8 us (13%)
  local copies, waits for them, and re-layouts  9.64 us (8%)
    all_to_all x1, blocking collectives, on_device(): lax.all_to_all(rows, EVERY, 0, 0, tiled=True)  25 us
    ppermute x11, waiting for transfers between devices, swapped(): return lax.ppermute(value, axis, SWAP)  22.7 us
    ppermute x11, starting transfers between devices, swapped(): return lax.ppermute(value, axis, SWAP)  21.7 us
    pallas_call x8, Pallas kernels, kernel_call(): pl.pallas_call(body, out_shape=outs, in_specs=[hbm if i in far else smem...  16.8 us
    all_to_all x1, waiting for transfers between devices, on_device(): got_other = lax.all_to_all(other_blocks, NEAR, 0, 0, tiled=True)  14.1 us
    unnamed x16, local copies, waits for them, and re-layouts  9.45 us
    all_to_all x1, starting transfers between devices, on_device(): got_own = lax.all_to_all(own_blocks, NEAR, 0, 0, tiled=True)  7.53 us
    all_to_all x1, starting transfers between devices, on_device(): got_other = lax.all_to_all(other_blocks, NEAR, 0, 0, tiled=True)  7.36 us
  transfers between devices with their start and end apart: 13, of which 8 were waited for; matrix products, arithmetic and copies ran while one was open for 0% of the time, Pallas kernels for 7%

profile of v3, /device:TPU:1, one launch (start us, length us, event | category | flops | bytes accessed | tf_op | source)
XLA Modules:
  0.0 127.3 jit_solution(16173157344381035622)
XLA Ops:
  0.0 3.2 %collective-permute-start = (bf16[128,512]{1,0:T(8,128)(2,1)}, bf16[128,512]{1,0:T(8,128)(2,1)S(1)}, u32[]{:S(2)}, u32[]{:S(2)}) collective-permute-start(bf16[128,512]{1,0:T(8,128)(2,1)} %bitcast.14), channel_id=1, source_target_pairs={{0,1},{1,0},{2,3},{3,2},{4,5},{5,4},{6,7},{7,6},{8,9},{9,8},{10,11... | collective-permute-start | bytes 393224 | tf_op jit(solution)/shard_map/ppermute | solution.py:24
  3.2 5.2 %collective-permute-start.4 = (bf16[128,512]{1,0:T(8,128)(2,1)}, bf16[128,512]{1,0:T(8,128)(2,1)S(1)}, u32[]{:S(2)}, u32[]{:S(2)}) collective-permute-start(bf16[128,512]{1,0:T(8,128)(2,1)} %bitcast.15), channel_id=1, source_target_pairs={{0,2},{2,0},{1,3},{3,1},{4,6},{6,4},{5,7},{7,5},{8,10},{10,8},{9,1... | collective-permute-start | bytes 393224 | tf_op jit(solution)/shard_map/ppermute | solution.py:24
  9.0 3.3 %collective-permute-done.4.s2 = bf16[128,512]{1,0:T(8,128)(2,1)S(1)} collective-permute-done((bf16[128,512]{1,0:T(8,128)(2,1)}, bf16[128,512]{1,0:T(8,128)(2,1)S(1)}, u32[]{:S(2)}, u32[]{:S(2)}) %collective-permute-start.4) | collective-permute-done | bytes 131104 | tf_op jit(solution)/shard_map/ppermute | solution.py:24
  12.4 3.1 %collective-permute-start.5 = (bf16[128,512]{1,0:T(8,128)(2,1)S(1)}, bf16[128,512]{1,0:T(8,128)(2,1)S(1)}, u32[]{:S(2)}, u32[]{:S(2)}) collective-permute-start(bf16[128,512]{1,0:T(8,128)(2,1)S(1)} %collective-permute-done.4.s2), channel_id=1, source_target_pairs={{0,1},{1,0},{2,3},{3,2},{4,5},{5,4},{6,7},{7,6},{8,9},{9,8},{10,11... | collective-permute-start | bytes 393224 | tf_op jit(solution)/shard_map/ppermute | solution.py:24
  15.4 2.2 %collective-permute-done.2.c2 = bf16[128,512]{1,0:T(8,128)(2,1)S(1)} collective-permute-done((bf16[128,512]{1,0:T(8,128)(2,1)}, bf16[128,512]{1,0:T(8,128)(2,1)S(1)}, u32[]{:S(2)}, u32[]{:S(2)}) %collective-permute-start.2) | collective-permute-done | bytes 131104 | tf_op jit(solution)/shard_map/ppermute | solution.py:24
  17.6 3.9 %collective-permute-start.3 = (bf16[128,512]{1,0:T(8,128)(2,1)S(1)}, bf16[128,512]{1,0:T(8,128)(2,1)S(1)}, u32[]{:S(2)}, u32[]{:S(2)}) collective-permute-start(bf16[128,512]{1,0:T(8,128)(2,1)S(1)} %collective-permute-done.2.c2), channel_id=1, source_target_pairs={{0,1},{1,0},{2,3},{3,2},{4,5},{5,4},{6,7},{7,6},{8,9},{9,8},{10,11... | collective-permute-start | bytes 393224 | tf_op jit(solution)/shard_map/ppermute | solution.py:24
  21.8 1.6 %copy-done.2 = bf16[2048,512]{1,0:T(8,128)(2,1)S(1)} copy-done((bf16[2048,512]{1,0:T(8,128)(2,1)S(1)}, bf16[2048,512]{1,0:T(8,128)(2,1)}, u32[]{:S(2)}) %copy-start.2) | copy-done | bytes 2097176
  23.4 1.6 %copy-done.3 = bf16[512,2048]{1,0:T(8,128)(2,1)S(1)} copy-done((bf16[512,2048]{1,0:T(8,128)(2,1)S(1)}, bf16[512,2048]{1,0:T(8,128)(2,1)}, u32[]{:S(2)}) %copy-start.3) | copy-done | bytes 2097176
  28.9 2.1 %shard_map.64 = (bf16[128,512]{1,0:T(8,128)(2,1)S(1)}, bf16[128,512]{1,0:T(8,128)(2,1)S(1)}, bf16[2048,512]{1,0:T(8,128)(2,1)S(1)}, bf16[2048,128]{1,0:T(8,128)(...) custom-call(s32[4]{0:T(128)S(1)} %pad_add_fusion.at, ...), custom_call_target="tpu_custom_call" | custom-call | tf_op jit(solution)/shard_map/pallas_call | solution.py:44
  31.0 3.5 %shard_map.65 = (bf16[128,512]{1,0:T(8,128)(2,1)S(1)}, bf16[1024,128]{1,0:T(8,128)(2,1)S(1)}) custom-call(s32[4]{0:T(128)S(1)} %pad_add_fusion.at, bf16[128,512]{1,0:T(8,128)(2,1)S(1)} %collective-permute-done.4.s2, bf16[128,512]{1,0:T(8,128)(2,1)S(1)} %collective-permute-done.5.s3, bf16[2048,512]{1,0:T(8,128)(2,1)S(1)} %get-tuple-element.19.wq, ...), custom_call_target="tpu_custom_call" | custom-call | tf_op jit(solution)/shard_map/pallas_call | solution.py:44
  35.8 2.1 %shard_map.67 = bf16[32,160,128]{2,1,0:T(8,128)(2,1)} custom-call(s32[4]{0:T(128)S(1)} %pad_add_fusion.at, bf16[128,512]{1,0:T(8,128)(2,1)S(1)} %get-tuple-element.15.c0, bf16[128,512]{1,0:T(8,128)(2,1)S(1)} %collective-permute-done.1.c1, bf16[128,512]{1,0:T(8,128)(2,1)S(1)} %collective-permute-done.2.c2, bf16[128,512]{1,0:T(8,128)(2,1)S(1)} %collective-permute-done.3.c3, ...), custom_call_target="tpu_custom_call" | custom-call | tf_op jit(solution)/shard_map/pallas_call | solution.py:44
  37.9 7.5 %all-to-all-start = ((bf16[32,160,128]{2,1,0:T(8,128)(2,1)}), bf16[32,160,128]{2,1,0:T(8,128)(2,1)S(1)}, u32[]{:S(2)}, u32[]{:S(2)}) async-start(bf16[32,160,128]{2,1,0:T(8,128)(2,1)} %shard_map.67), calls=%async_computation | async-start | bytes 2621440 | tf_op jit(solution)/shard_map/all_to_all | solution.py:309
  46.3 1.7 %collective-permute-start.8 = (bf16[128,512]{1,0:T(8,128)(2,1)S(1)}, bf16[128,512]{1,0:T(8,128)(2,1)S(1)}, u32[]{:S(2)}, u32[]{:S(2)}) collective-permute-start(bf16[128,512]{1,0:T(8,128)(2,1)S(1)} %broadcast_select_fusion), channel_id=1, source_target_pairs={{0,128},{128,0},{1,129},{129,1},{2,130},{130,2},{3,131},{131,3},{4... | collective-permute-start | bytes 393224 | tf_op jit(solution)/shard_map/ppermute | solution.py:24
  48.8 13.5 %collective-permute-done.6.c0 = bf16[128,512]{1,0:T(8,128)(2,1)S(1)} collective-permute-done((bf16[128,512]{1,0:T(8,128)(2,1)S(1)}, bf16[128,512]{1,0:T(8,128)(2,1)S(1)}, u32[]{:S(2)}, u32[]{:S(2)}) %collective-permute-start.6) | collective-permute-done | bytes 131104 | tf_op jit(solution)/shard_map/ppermute | solution.py:24
  62.3 1.3 %collective-permute-start.7 = (bf16[128,512]{1,0:T(8,128)(2,1)S(1)}, bf16[128,512]{1,0:T(8,128)(2,1)S(1)}, u32[]{:S(2)}, u32[]{:S(2)}) collective-permute-start(bf16[128,512]{1,0:T(8,128)(2,1)S(1)} %collective-permute-done.6.c0), channel_id=1, source_target_pairs={{0,1},{1,0},{2,3},{3,2},{4,5},{5,4},{6,7},{7,6},{8,9},{9,8},{10,11... | collective-permute-start | bytes 393224 | tf_op jit(solution)/shard_map/ppermute | solution.py:24
  63.7 1.5 %collective-permute-done.8.s0 = bf16[128,512]{1,0:T(8,128)(2,1)S(1)} collective-permute-done((bf16[128,512]{1,0:T(8,128)(2,1)S(1)}, bf16[128,512]{1,0:T(8,128)(2,1)S(1)}, u32[]{:S(2)}, u32[]{:S(2)}) %collective-permute-start.8) | collective-permute-done | bytes 131104 | tf_op jit(solution)/shard_map/ppermute | solution.py:24
  65.1 1.3 %collective-permute-start.9 = (bf16[128,512]{1,0:T(8,128)(2,1)S(1)}, bf16[128,512]{1,0:T(8,128)(2,1)S(1)}, u32[]{:S(2)}, u32[]{:S(2)}) collective-permute-start(bf16[128,512]{1,0:T(8,128)(2,1)S(1)} %collective-permute-done.8.s0), channel_id=1, source_target_pairs={{0,1},{1,0},{2,3},{3,2},{4,5},{5,4},{6,7},{7,6},{8,9},{9,8},{10,11... | collective-permute-start | bytes 393224 | tf_op jit(solution)/shard_map/ppermute | solution.py:24
  68.7 2.1 %shard_map.69 = bf16[32,160,128]{2,1,0:T(8,128)(2,1)} custom-call(s32[4]{0:T(128)S(1)} %pad_add_fusion.at, bf16[128,512]{1,0:T(8,128)(2,1)S(1)} %collective-permute-done.6.c0, bf16[128,512]{1,0:T(8,128)(2,1)S(1)} %collective-permute-done.7.c1, bf16[128,512]{1,0:T(8,128)(2,1)S(1)} %collective-permute-done.8.s0, ...), custom_call_target="tpu_custom_call" | custom-call | tf_op jit(solution)/shard_map/pallas_call | solution.py:44
  70.8 1.9 %all-to-all-done.got = bf16[32,160,128]{2,1,0:T(8,128)(2,1)S(1)} async-done(((bf16[32,160,128]{2,1,0:T(8,128)(2,1)}), bf16[32,160,128]{2,1,0:T(8,128)(2,1)S(1)}, u32[]{:S(2)}, u32[]{:S(2)}) %all-to-all-start) | async-done | bytes 1310752 | tf_op jit(solution)/shard_map/all_to_all | solution.py:309
  72.7 7.4 %all-to-all-start.1 = ((bf16[32,160,128]{2,1,0:T(8,128)(2,1)}), bf16[32,160,128]{2,1,0:T(8,128)(2,1)S(1)}, u32[]{:S(2)}, u32[]{:S(2)}) async-start(bf16[32,160,128]{2,1,0:T(8,128)(2,1)} %shard_map.69), calls=%async_computation.1 | async-start | bytes 2621440 | tf_op jit(solution)/shard_map/all_to_all | solution.py:315
  80.0 1.6 %shard_map.68.own = bf16[160,32,128]{2,1,0:T(8,128)(2,1)S(1)} custom-call(bf16[32,160,128]{2,1,0:T(8,128)(2,1)S(1)} %all-to-all-done.got), custom_call_target="tpu_custom_call" | custom-call | tf_op jit(solution)/shard_map/pallas_call | solution.py:44
  82.7 14.1 %all-to-all-done.1.other = bf16[32,160,128]{2,1,0:T(8,128)(2,1)S(1)} async-done(((bf16[32,160,128]{2,1,0:T(8,128)(2,1)}), bf16[32,160,128]{2,1,0:T(8,128)(2,1)S(1)}, u32[]{:S(2)}, u32[]{:S(2)}) %all-to-all-start.1) | async-done | bytes 1310752 | tf_op jit(solution)/shard_map/all_to_all | solution.py:315
  98.2 2.9 %shard_map.70 = f32[256,128]{1,0:T(8,128)S(1)} custom-call(s32[4]{0:T(128)S(1)} %pad_add_fusion.at, bf16[160,32,128]{2,1,0:T(8,128)(2,1)S(1)} %copy-done.1, bf16[32,160,128]{2,1,0:T(8,128)(2,1)S(1)} %all-to-all-done.1.other), custom_call_target="tpu_custom_call" | custom-call | tf_op jit(solution)/shard_map/pallas_call | solution.py:44
  101.1 25.0 %all_to_all.15 = f32[256,1,128]{2,1,0:T(1,128)S(1)} all-to-all(f32[256,1,128]{2,1,0:T(1,128)S(1)} %bitcast.12), channel_id=1, replica_groups=mesh['zb'=2,'za'=2,'x'=4,'y'=4,'h'=2,'c'=2] {'zb','za','x','y','h','c'}, dimensions={0} | all-to-all | bytes 262144 | tf_op jit(solution)/shard_map/all_to_all | solution.py:325
  (37 shorter events, 13.4 us)
Async XLA Ops:
  0.0 21.8 %collective-permute-start = (bf16[128,512]{1,0:T(8,128)(2,1)}, bf16[128,512]{1,0:T(8,128)(2,1)S(1)}, u32[]{:S(2)}, u32[]{:S(2)}) collective-permute-start(bf16[128,512]{1,0:T(8,128)(2,1)} %bitcast.14), channel_id=1, source_target_pairs={{0,1},{1,0},{2,3},{3,2},{4,5},{5,4},{6,7},{7,6},{8,9},{9,8},{10,11... | collective-permute-start | bytes 393224 | tf_op jit(solution)/shard_map/ppermute | solution.py:24
  3.2 9.2 %collective-permute-start.4 = (bf16[128,512]{1,0:T(8,128)(2,1)}, bf16[128,512]{1,0:T(8,128)(2,1)S(1)}, u32[]{:S(2)}, u32[]{:S(2)}) collective-permute-start(bf16[128,512]{1,0:T(8,128)(2,1)} %bitcast.15), channel_id=1, source_target_pairs={{0,2},{2,0},{1,3},{3,1},{4,6},{6,4},{5,7},{7,5},{8,10},{10,8},{9,1... | collective-permute-start | bytes 393224 | tf_op jit(solution)/shard_map/ppermute | solution.py:24
  8.4 13.4 %collective-permute-start.1 = (bf16[128,512]{1,0:T(8,128)(2,1)}, bf16[128,512]{1,0:T(8,128)(2,1)S(1)}, u32[]{:S(2)}, u32[]{:S(2)}) collective-permute-start(bf16[128,512]{1,0:T(8,128)(2,1)} %bitcast.17), channel_id=1, source_target_pairs={{0,1},{1,0},{2,3},{3,2},{4,5},{5,4},{6,7},{7,6},{8,9},{9,8},{10,11... | collective-permute-start | bytes 393224 | tf_op jit(solution)/shard_map/ppermute | solution.py:24
  8.7 8.9 %collective-permute-start.2 = (bf16[128,512]{1,0:T(8,128)(2,1)}, bf16[128,512]{1,0:T(8,128)(2,1)S(1)}, u32[]{:S(2)}, u32[]{:S(2)}) collective-permute-start(bf16[128,512]{1,0:T(8,128)(2,1)} %bitcast.18), channel_id=1, source_target_pairs={{0,2},{2,0},{1,3},{3,1},{4,6},{6,4},{5,7},{7,5},{8,10},{10,8},{9,1... | collective-permute-start | bytes 393224 | tf_op jit(solution)/shard_map/ppermute | solution.py:24
  12.4 18.6 %collective-permute-start.5 = (bf16[128,512]{1,0:T(8,128)(2,1)S(1)}, bf16[128,512]{1,0:T(8,128)(2,1)S(1)}, u32[]{:S(2)}, u32[]{:S(2)}) collective-permute-start(bf16[128,512]{1,0:T(8,128)(2,1)S(1)} %collective-permute-done.4.s2), channel_id=1, source_target_pairs={{0,1},{1,0},{2,3},{3,2},{4,5},{5,4},{6,7},{7,6},{8,9},{9,8},{10,11... | collective-permute-start | bytes 393224 | tf_op jit(solution)/shard_map/ppermute | solution.py:24
  17.6 16.8 %collective-permute-start.3 = (bf16[128,512]{1,0:T(8,128)(2,1)S(1)}, bf16[128,512]{1,0:T(8,128)(2,1)S(1)}, u32[]{:S(2)}, u32[]{:S(2)}) collective-permute-start(bf16[128,512]{1,0:T(8,128)(2,1)S(1)} %collective-permute-done.2.c2), channel_id=1, source_target_pairs={{0,1},{1,0},{2,3},{3,2},{4,5},{5,4},{6,7},{7,6},{8,9},{9,8},{10,11... | collective-permute-start | bytes 393224 | tf_op jit(solution)/shard_map/ppermute | solution.py:24
  21.8 1.6 %copy-start.2 = (bf16[2048,512]{1,0:T(8,128)(2,1)S(1)}, bf16[2048,512]{1,0:T(8,128)(2,1)}, u32[]{:S(2)}) copy-start(bf16[2048,512]{1,0:T(8,128)(2,1)} %wq.1) | copy-start | bytes 6291460
  23.4 1.6 %copy-start.3 = (bf16[512,2048]{1,0:T(8,128)(2,1)S(1)}, bf16[512,2048]{1,0:T(8,128)(2,1)}, u32[]{:S(2)}) copy-start(bf16[512,2048]{1,0:T(8,128)(2,1)} %wo.1) | copy-start | bytes 6291460
  25.0 1.0 copy-start.4
  26.0 1.0 copy-start.5
  27.1 0.9 copy-start.6
  28.0 0.9 copy-start.7
  37.9 34.7 %all-to-all-start = ((bf16[32,160,128]{2,1,0:T(8,128)(2,1)}), bf16[32,160,128]{2,1,0:T(8,128)(2,1)S(1)}, u32[]{:S(2)}, u32[]{:S(2)}) async-start(bf16[32,160,128]{2,1,0:T(8,128)(2,1)} %shard_map.67), calls=%async_computation | async-start | bytes 2621440 | tf_op jit(solution)/shard_map/all_to_all | solution.py:309
  45.5 16.8 %collective-permute-start.6 = (bf16[128,512]{1,0:T(8,128)(2,1)S(1)}, bf16[128,512]{1,0:T(8,128)(2,1)S(1)}, u32[]{:S(2)}, u32[]{:S(2)}) collective-permute-start(bf16[128,512]{1,0:T(8,128)(2,1)S(1)} %broadcast_select_fusion.1), channel_id=1, source_target_pairs={{0,128},{128,0},{1,129},{129,1},{2,130},{130,2},{3,131},{131,3},{4... | collective-permute-start | bytes 393224 | tf_op jit(solution)/shard_map/ppermute | solution.py:24
  46.3 18.8 %collective-permute-start.8 = (bf16[128,512]{1,0:T(8,128)(2,1)S(1)}, bf16[128,512]{1,0:T(8,128)(2,1)S(1)}, u32[]{:S(2)}, u32[]{:S(2)}) collective-permute-start(bf16[128,512]{1,0:T(8,128)(2,1)S(1)} %broadcast_select_fusion), channel_id=1, source_target_pairs={{0,128},{128,0},{1,129},{129,1},{2,130},{130,2},{3,131},{131,3},{4... | collective-permute-start | bytes 393224 | tf_op jit(solution)/shard_map/ppermute | solution.py:24
  48.1 20.6 %collective-permute-start.10 = (bf16[128,640]{1,0:T(8,128)(2,1)S(1)}, bf16[128,640]{1,0:T(8,128)(2,1)S(1)}, u32[]{:S(2)}, u32[]{:S(2)}) collective-permute-start(bf16[128,640]{1,0:T(8,128)(2,1)S(1)} %shard_map.66.factors), channel_id=1, source_target_pairs={{0,128},{128,0},{1,129},{129,1},{2,130},{130,2},{3,131},{131,3},{4... | collective-permute-start | bytes 491528 | tf_op jit(solution)/shard_map/ppermute | solution.py:24
  62.3 4.2 %collective-permute-start.7 = (bf16[128,512]{1,0:T(8,128)(2,1)S(1)}, bf16[128,512]{1,0:T(8,128)(2,1)S(1)}, u32[]{:S(2)}, u32[]{:S(2)}) collective-permute-start(bf16[128,512]{1,0:T(8,128)(2,1)S(1)} %collective-permute-done.6.c0), channel_id=1, source_target_pairs={{0,1},{1,0},{2,3},{3,2},{4,5},{5,4},{6,7},{7,6},{8,9},{9,8},{10,11... | collective-permute-start | bytes 393224 | tf_op jit(solution)/shard_map/ppermute | solution.py:24
  65.1 2.3 %collective-permute-start.9 = (bf16[128,512]{1,0:T(8,128)(2,1)S(1)}, bf16[128,512]{1,0:T(8,128)(2,1)S(1)}, u32[]{:S(2)}, u32[]{:S(2)}) collective-permute-start(bf16[128,512]{1,0:T(8,128)(2,1)S(1)} %collective-permute-done.8.s0), channel_id=1, source_target_pairs={{0,1},{1,0},{2,3},{3,2},{4,5},{5,4},{6,7},{7,6},{8,9},{9,8},{10,11... | collective-permute-start | bytes 393224 | tf_op jit(solution)/shard_map/ppermute | solution.py:24
  72.7 24.2 %all-to-all-start.1 = ((bf16[32,160,128]{2,1,0:T(8,128)(2,1)}), bf16[32,160,128]{2,1,0:T(8,128)(2,1)S(1)}, u32[]{:S(2)}, u32[]{:S(2)}) async-start(bf16[32,160,128]{2,1,0:T(8,128)(2,1)} %shard_map.69), calls=%async_computation.1 | async-start | bytes 2621440 | tf_op jit(solution)/shard_map/all_to_all | solution.py:315
  81.6 1.1 copy-start
  96.8 1.3 %copy-start.1 = (bf16[160,32,128]{2,1,0:T(8,128)(2,1)S(1)}, bf16[160,32,128]{2,1,0:T(8,128)(2,1)}, u32[]{:S(2)}) copy-start(bf16[160,32,128]{2,1,0:T(8,128)(2,1)} %copy-done) | copy-start | bytes 3932164

commit v4 on v3

--- a/solution.py
+++ b/solution.py
@@ -1,5 +1,6 @@
 import jax
 import jax.numpy as jnp
+import numpy as np
 from jax import lax
 from jax.experimental import pallas as pl
 from jax.experimental.pallas import tpu as pltpu
@@ -26,11 +27,12 @@
 
 def rope_tables(length, head_dim):
     half_dim = head_dim // 2
-    freqs_k = theta_base ** (-(jnp.arange(half_dim, dtype=jnp.float32) * 2.0 / head_dim))
-    angles = jnp.arange(length, dtype=jnp.float32)[:, None] * freqs_k[None, :]
-    sine = jnp.sin(angles)
-    cos = jnp.tile(jnp.cos(angles), (1, LANES // half_dim))
-    return cos, jnp.tile(jnp.concatenate([-sine, sine], axis=1), (1, LANES // head_dim))
+    steps = np.arange(half_dim, dtype=np.float32) * np.float32(2.0) / np.float32(head_dim)
+    freqs_k = np.power(np.float32(theta_base), -steps)
+    angles = np.arange(length, dtype=np.float32)[:, None] * freqs_k[None, :]
+    sine = np.sin(angles)
+    cos = np.tile(np.cos(angles), (1, LANES // half_dim))
+    return cos, np.tile(np.concatenate([-sine, sine], axis=1), (1, LANES // head_dim))
 
 
 def dot(left, right, dims=((1,), (0,))):
@@ -38,7 +40,8 @@
 
 
 def kernel_call(body, outs, ins, scratch=(), vmem_mib=16, far=()):
-    hbm = pl.BlockSpec(memory_space=pl.ANY)
+    ins = [pltpu.with_memory_space_constraint(a, pltpu.HBM) if i in far else a for i, a in enumerate(ins)]
+    hbm = pl.BlockSpec(memory_space=pltpu.HBM)
     smem = pl.BlockSpec(memory_space=pltpu.SMEM)
     vmem = pl.BlockSpec(memory_space=pltpu.VMEM)
     return pl.pallas_call(
@@ -72,8 +75,10 @@
 
 
 def start_body(
-    at, s0, s1, c0, c1, wq, wk, wv, wo, s_out, c_out, wq_out, wk_out, wv_out, wo_out, sums, grads, sems
+    at, s0, s1, c0, c1, wq, wk, wv, wo, own, wq_out, wk_out, wv_out, wo_out, sums, grads, sems
 ):
+    length = s0.shape[0]
+    s_out, c_out = own.at[:length, :], own.at[length:, :]
     moves = [
         pltpu.make_async_copy(src, dst, sems.at[i])
         for i, (src, dst) in enumerate(
@@ -193,23 +198,34 @@
         put_blocks(blocks, turned_v, (width, width + LANES), state, col_at)
 
 
-def own_body(at, c0, c1, c2, c3, s0, s1, s2, s3, factors, blocks):
+def own_body(at, own, s1, s2, s3, c1, c2, c3, factors, blocks):
     here = at[0] == at[2]
-
-    def half(parts):
-        return [jnp.where(here, parts[k][...], parts[k + 2][...]) for k in range(2)]
-
-    put_all(at, factors, half((c0, c1, c2, c3)), half((s0, s1, s2, s3)), blocks)
-
-
-def other_body(at, c0, c1, s0, s1, factors, blocks):
-    put_all(at, factors, (c0[...], c1[...]), (s0[...], s1[...]), blocks)
-
-
-def turn_blocks(got, wide, keep):
+    length = s1.shape[0]
+
+    def half(p0, p1, p2, p3):
+        return [jnp.where(here, p0, p2[...]), jnp.where(here, p1[...], p3[...])]
+
+    states = half(own[:length, :], s1, s2, s3)
+    cots = half(own[length:, :], c1, c2, c3)
+    put_all(at, factors, cots, states, blocks)
+
+
+def pick_body(at, same, cross, piece):
+    piece[...] = jnp.where(at[0] == at[2], same[...], cross[...])
+
+
+def other_body(at, piece, near, factors, blocks):
+    length = factors.shape[0]
+    states = [p[:length, :] for p in (piece, near)]
+    cots = [p[length:, :] for p in (piece, near)]
+    put_all(at, factors, cots, states, blocks)
+
+
+def turn_blocks(got, wide, keep, ready=lambda: None):
     seqs, tall, _ = got.shape
     for s in range(seqs):
         wide[pl.ds(s * tall, tall), :] = got[s].astype(jnp.float32)
+    ready()
     for r in range(tall):
         keep(r, wide[pl.ds(r, seqs, stride=tall), :].astype(jnp.bfloat16))
 
@@ -221,8 +237,10 @@
     turn_blocks(got, wide, keep)
 
 
-def share_body(at, own, other, rows_out, wide):
+def share_body(at, own_far, other, rows_out, wide, own, sem):
     _, seqs, _ = own.shape
+    fetch = pltpu.make_async_copy(own_far, own, sem)
+    fetch.start()
     straight = at[2] == 0
     total = jnp.zeros((2 * seqs, 2 * seqs), jnp.float32)
     waiting = []
@@ -238,7 +256,7 @@
             total = total + dot(x, x, ((1,), (1,)))
             waiting.clear()
 
-    turn_blocks(other, wide, keep)
+    turn_blocks(other, wide, keep, fetch.wait)
     eye = lax.broadcasted_iota(jnp.int32, total.shape, 0) == lax.broadcasted_iota(
         jnp.int32, total.shape, 1
     )
@@ -247,6 +265,11 @@
     copies = rows_out.shape[0] // rows.shape[0]
     for k in range(copies):
         rows_out[pl.ds(k, rows.shape[0], stride=copies), :] = rows
+
+
+def between_body(at, out):
+    for k in range(at.shape[0]):
+        out[k] = at[k]
 
 
 def final_body(at, got, out):
@@ -265,7 +288,6 @@
     states, cotangent = states[0], cotangent[0]
     axes = (lax.axis_index("h"), lax.axis_index("c"), lax.axis_index("zb"), lax.axis_index(SEQ))
     at = jnp.stack(axes).astype(jnp.int32)
-    far_half = axes[0] == axes[2]
     blocks = lax.axis_size(NEAR)
     seqs = 2 * blocks
     tall = (part + LANES) * (2 * part) // (LANES * blocks)
@@ -277,18 +299,15 @@
         near = swapped(own, "c")
         return near, far, swapped(far, "c")
 
-    def partner(own, far):
-        piece = swapped(jnp.where(far_half, far, own), "zb")
-        return piece, swapped(piece, "c")
-
     s1, s2, s3 = gathered(states)
     c1, c2, c3 = gathered(cotangent)
     cos, sine = rope_tables(length, HEAD_DIM)
     kv = wk.shape[1]
-    s0, c0, wq, wk, wv, wo, sums, grads = kernel_call(
+    own, wq, wk, wv, wo, sums, grads = kernel_call(
         start_body,
         (
-            *(shape(a.shape, bf16) for a in (states, cotangent, wq, wk, wv, wo)),
+            shape((2 * length, part), bf16),
+            *(shape(a.shape, bf16) for a in (wq, wk, wv, wo)),
             shape((length, part + 2 * kv), f32),
             shape((length, part), f32),
         ),
@@ -296,22 +315,30 @@
         (pltpu.SemaphoreType.DMA((6,)),),
         far=(1, 3, 5, 6, 7, 8),
     )
+    same = lax.ppermute(own, ("zb", "h"), ((2, 0), (1, 3)))
+    cross = lax.ppermute(own, ("zb", "h"), ((2, 1), (1, 2)))
+    smem = pl.BlockSpec(memory_space=pltpu.SMEM)
+    at_later = pl.pallas_call(
+        between_body,
+        out_shape=shape(at.shape, at.dtype),
+        in_specs=[smem],
+        out_specs=smem,
+        compiler_params=pltpu.CompilerParams(vmem_limit_bytes=2**20),
+    )(at)
     attended, probs = kernel_call(
         attention_body,
         (shape((length, part), bf16), shape((part // HEAD_DIM * length, length), bf16)),
-        (at, s2, s3, wq, wk, wv, sums, cos, sine),
+        (at_later, s2, s3, wq, wk, wv, sums, cos, sine),
     )
     factors = kernel_call(
         grads_body, shape((length, part + LANES), bf16), (at, c2, c3, wo, grads, attended, probs)
     )
     other_factors = swapped(factors, "zb")
-    own_blocks = kernel_call(own_body, block_shape, (at, c0, c1, c2, c3, s0, s1, s2, s3, factors))
+    own_blocks = kernel_call(own_body, block_shape, (at, own, s1, s2, s3, c1, c2, c3, factors))
     got_own = lax.all_to_all(own_blocks, NEAR, 0, 0, tiled=True)
-    other_blocks = kernel_call(
-        other_body,
-        block_shape,
-        (at, *partner(c0, c2), *partner(s0, s2), other_factors),
-    )
+    piece = kernel_call(pick_body, shape(own.shape, bf16), (at, same, cross))
+    near = swapped(piece, "c")
+    other_blocks = kernel_call(other_body, block_shape, (at, piece, near, other_factors))
     got_other = lax.all_to_all(other_blocks, NEAR, 0, 0, tiled=True)
     own_turned = kernel_call(turn_body, shape((tall, blocks, LANES), bf16), (got_own,), (wide,))
     copies = lax.axis_size(TP)
@@ -319,7 +346,8 @@
         share_body,
         shape((seqs * copies, 2 * seqs), f32),
         (at, own_turned, got_other),
-        (wide,),
+        (wide, pltpu.VMEM(own_turned.shape, bf16), pltpu.SemaphoreType.DMA),
+        far=(1,),
     )
     rows = rows.reshape(seqs * copies, 1, 2 * seqs)
     got = lax.all_to_all(rows, EVERY, 0, 0, tiled=True).reshape(seqs * copies, 2 * seqs)

time: 128 us -> 132 us (1.031)
  starting transfers between devices: 36.6 us -> 51.1 us
  local copies, waits for them, and re-layouts: 9.64 us -> 1.08 us
  Pallas kernels: 16.8 us -> 21.5 us
  waiting for transfers between devices: 38.8 us -> 34.5 us
  blocking collectives: 25 us -> 23.3 us
    ppermute x11 -> x8, waiting for transfers between devices: 22.7 us -> 11.5 us  [swapped(): return lax.ppermute(value, axis, SWAP)]
    ppermute x0 -> x2, waiting for transfers between devices: none -> 8.45 us  [the longest x1 8.45 us: on_device(): same = lax.ppermute(own, ('zb', 'h'), ((2, 0), (1, 3)))]
    unnamed x16 -> x6, local copies, waits for them, and re-layouts: 9.45 us -> 1.08 us
    ppermute x11 -> x8, starting transfers between devices: 21.7 us -> 29.7 us  [swapped(): return lax.ppermute(value, axis, SWAP)]
    all_to_all x1, starting transfers between devices: 7.36 us -> 11.5 us  [on_device(): got_other = lax.all_to_all(other_blocks, NEAR, 0, 0, tiled=True)]
    pallas_call x8 -> x9, Pallas kernels: 16.8 us -> 20.4 us  [kernel_call(): pl.pallas_call(body, out_shape=outs, in_specs=[hbm if i in far else smem...]
    ppermute x0 -> x2, starting transfers between devices: none -> 1.97 us  [the longest x1 1.29 us: on_device(): same = lax.ppermute(own, ('zb', 'h'), ((2, 0), (1, 3)))]
    all_to_all x1, waiting for transfers between devices: 1.9 us -> 0.01 us  [on_device(): got_own = lax.all_to_all(own_blocks, NEAR, 0, 0, tiled=True)]
  transfers between devices with their start and end apart: 13 -> 12, of which waited for: 8 -> 5; matrix products, arithmetic and copies ran while one was open for 0% -> 0% of each run, Pallas kernels for 7% -> 10%
where the time goes in v4:
time: 132 us
  starting transfers between devices  51.1 us (39%)
  waiting for transfers between devices  34.5 us (26%)
  blocking collectives  23.3 us (18%)
  Pallas kernels  21.5 us (16%)
    ppermute x8, starting transfers between devices, swapped(): return lax.ppermute(value, axis, SWAP)  29.7 us
    all_to_all x1, blocking collectives, on_device(): lax.all_to_all(rows, EVERY, 0, 0, tiled=True)  23.3 us
    pallas_call x9, Pallas kernels, kernel_call(): pl.pallas_call(body, out_shape=outs, in_specs=[hbm if i in far else smem...  20.4 us
    all_to_all x1, waiting for transfers between devices, on_device(): got_other = lax.all_to_all(other_blocks, NEAR, 0, 0, tiled=True)  14.6 us
    ppermute x8, waiting for transfers between devices, swapped(): return lax.ppermute(value, axis, SWAP)  11.5 us
    all_to_all x1, starting transfers between devices, on_device(): got_other = lax.all_to_all(other_blocks, NEAR, 0, 0, tiled=True)  11.5 us
    ppermute x1, waiting for transfers between devices, on_device(): same = lax.ppermute(own, ('zb', 'h'), ((2, 0), (1, 3)))  8.45 us
    all_to_all x1, starting transfers between devices, on_device(): got_own = lax.all_to_all(own_blocks, NEAR, 0, 0, tiled=True)  7.95 us
  transfers between devices with their start and end apart: 12, of which 5 were waited for; matrix products, arithmetic and copies ran while one was open for 0% of the time, Pallas kernels for 10%

profile of v4, /device:TPU:1, one launch (start us, length us, event | category | flops | bytes accessed | tf_op | source)
XLA Modules:
  0.0 131.8 jit_solution(7356530405514953374)
XLA Ops:
  0.0 7.7 %collective-permute-start.2 = (bf16[128,512]{1,0:T(8,128)(2,1)}, bf16[128,512]{1,0:T(8,128)(2,1)S(1)}, u32[]{:S(2)}, u32[]{:S(2)}) collective-permute-start(bf16[128,512]{1,0:T(8,128)(2,1)} %bitcast.12), channel_id=1, source_target_pairs={{0,2},{2,0},{1,3},{3,1},{4,6},{6,4},{5,7},{7,5},{8,10},{10,8},{9,1... | collective-permute-start | bytes 393224 | tf_op jit(solution)/shard_map/ppermute | solution.py:25
  7.7 1.4 %collective-permute-start = (bf16[128,512]{1,0:T(8,128)(2,1)}, bf16[128,512]{1,0:T(8,128)(2,1)S(1)}, u32[]{:S(2)}, u32[]{:S(2)}) collective-permute-start(bf16[128,512]{1,0:T(8,128)(2,1)} %bitcast.13), channel_id=1, source_target_pairs={{0,1},{1,0},{2,3},{3,2},{4,5},{5,4},{6,7},{7,6},{8,9},{9,8},{10,11... | collective-permute-start | bytes 393224 | tf_op jit(solution)/shard_map/ppermute | solution.py:25
  9.1 1.5 %collective-permute-done.2.s2 = bf16[128,512]{1,0:T(8,128)(2,1)S(1)} collective-permute-done((bf16[128,512]{1,0:T(8,128)(2,1)}, bf16[128,512]{1,0:T(8,128)(2,1)S(1)}, u32[]{:S(2)}, u32[]{:S(2)}) %collective-permute-start.2) | collective-permute-done | bytes 131104 | tf_op jit(solution)/shard_map/ppermute | solution.py:25
  10.7 4.8 %collective-permute-start.3 = (bf16[128,512]{1,0:T(8,128)(2,1)S(1)}, bf16[128,512]{1,0:T(8,128)(2,1)S(1)}, u32[]{:S(2)}, u32[]{:S(2)}) collective-permute-start(bf16[128,512]{1,0:T(8,128)(2,1)S(1)} %collective-permute-done.2.s2), channel_id=1, source_target_pairs={{0,1},{1,0},{2,3},{3,2},{4,5},{5,4},{6,7},{7,6},{8,9},{9,8},{10,11... | collective-permute-start | bytes 393224 | tf_op jit(solution)/shard_map/ppermute | solution.py:25
  15.8 4.6 %collective-permute-start.5 = (bf16[128,512]{1,0:T(8,128)(2,1)S(1)}, bf16[128,512]{1,0:T(8,128)(2,1)S(1)}, u32[]{:S(2)}, u32[]{:S(2)}) collective-permute-start(bf16[128,512]{1,0:T(8,128)(2,1)S(1)} %collective-permute-done.4.c2), channel_id=1, source_target_pairs={{0,1},{1,0},{2,3},{3,2},{4,5},{5,4},{6,7},{7,6},{8,9},{9,8},{10,11... | collective-permute-start | bytes 393224 | tf_op jit(solution)/shard_map/ppermute | solution.py:25
  20.5 1.1 shard_map.83.at
  21.7 3.9 %shard_map.82 = (bf16[256,512]{1,0:T(8,128)(2,1)S(1)}, bf16[2048,512]{1,0:T(8,128)(2,1)S(1)}, bf16[2048,128]{1,0:T(8,128)(2,1)S(1)}, bf16[2048,128]{1,0:T(8,128)...) custom-call(s32[4]{0:T(128)S(1)} %pad_add_fusion.at, ...), custom_call_target="tpu_custom_call" | custom-call | tf_op jit(solution)/shard_map/pallas_call | solution.py:47
  25.6 3.5 %shard_map.84 = (bf16[128,512]{1,0:T(8,128)(2,1)S(1)}, bf16[1024,128]{1,0:T(8,128)(2,1)S(1)}) custom-call(s32[4]{0:T(128)S(1)} %shard_map.83.at, bf16[128,512]{1,0:T(8,128)(2,1)S(1)} %collective-permute-done.2.s2, bf16[128,512]{1,0:T(8,128)(2,1)S(1)} %collective-permute-done.3.s3, bf16[2048,512]{1,0:T(8,128)(2,1)S(1)} %get-tuple-element.17.wq, ...), custom_call_target="tpu_custom_call" | custom-call | tf_op jit(solution)/shard_map/pallas_call | solution.py:47
  29.1 1.3 shard_map.85.factors
  30.5 2.1 %shard_map.86 = bf16[32,160,128]{2,1,0:T(8,128)(2,1)} custom-call(s32[4]{0:T(128)S(1)} %pad_add_fusion.at, bf16[256,512]{1,0:T(8,128)(2,1)S(1)} %get-tuple-element.14.own, bf16[128,512]{1,0:T(8,128)(2,1)S(1)} %collective-permute-done.s1, bf16[128,512]{1,0:T(8,128)(2,1)S(1)} %collective-permute-done.2.s2, bf16[128,512]{1,0:T(8,128)(2,1)S(1)} %collective-permute-done.3.s3, ...), custom_call_target="tpu_custom_call" | custom-call | tf_op jit(solution)/shard_map/pallas_call | solution.py:47
  32.6 8.0 %all-to-all-start = ((bf16[32,160,128]{2,1,0:T(8,128)(2,1)}), bf16[32,160,128]{2,1,0:T(8,128)(2,1)S(1)}, u32[]{:S(2)}, u32[]{:S(2)}) async-start(bf16[32,160,128]{2,1,0:T(8,128)(2,1)} %shard_map.86), calls=%async_computation | async-start | bytes 2621440 | tf_op jit(solution)/shard_map/all_to_all | solution.py:338
  40.6 1.3 collective-permute-start.6
  42.5 8.4 %collective-permute-done.6.same = bf16[256,512]{1,0:T(8,128)(2,1)S(1)} collective-permute-done((bf16[256,512]{1,0:T(8,128)(2,1)S(1)}, bf16[256,512]{1,0:T(8,128)(2,1)S(1)}, u32[]{:S(2)}, u32[]{:S(2)}) %collective-permute-start.6) | collective-permute-done | bytes 262176 | tf_op jit(solution)/shard_map/ppermute | solution.py:318
  51.6 1.3 collective-permute-start.8
  52.8 9.9 %collective-permute-start.9 = (bf16[128,640]{1,0:T(8,128)(2,1)S(1)}, bf16[128,640]{1,0:T(8,128)(2,1)S(1)}, u32[]{:S(2)}, u32[]{:S(2)}) collective-permute-start(bf16[128,640]{1,0:T(8,128)(2,1)S(1)} %shard_map.85.factors), channel_id=1, source_target_pairs={{0,128},{128,0},{1,129},{129,1},{2,130},{130,2},{3,131},{131,3},{4... | collective-permute-start | bytes 491528 | tf_op jit(solution)/shard_map/ppermute | solution.py:25
  62.8 9.6 %collective-permute-done.9.factors = bf16[128,640]{1,0:T(8,128)(2,1)S(1)} collective-permute-done((bf16[128,640]{1,0:T(8,128)(2,1)S(1)}, bf16[128,640]{1,0:T(8,128)(2,1)S(1)}, u32[]{:S(2)}, u32[]{:S(2)}) %collective-permute-start.9) | collective-permute-done | bytes 163872 | tf_op jit(solution)/shard_map/ppermute | solution.py:25
  72.3 2.2 %shard_map.89 = bf16[32,160,128]{2,1,0:T(8,128)(2,1)} custom-call(s32[4]{0:T(128)S(1)} %pad_add_fusion.at, bf16[256,512]{1,0:T(8,128)(2,1)S(1)} %shard_map.88.piece, bf16[256,512]{1,0:T(8,128)(2,1)S(1)} %collective-permute-done.8.near, bf16[128,640]{1,0:T(8,128)(2,1)S(1)} %collective-permute-done.9.factors), custom_call_target="tpu_custom_call" | custom-call | tf_op jit(solution)/shard_map/pallas_call | solution.py:47
  74.5 11.5 %all-to-all-start.1 = ((bf16[32,160,128]{2,1,0:T(8,128)(2,1)}), bf16[32,160,128]{2,1,0:T(8,128)(2,1)S(1)}, u32[]{:S(2)}, u32[]{:S(2)}) async-start(bf16[32,160,128]{2,1,0:T(8,128)(2,1)} %shard_map.89), calls=%async_computation.1 | async-start | bytes 2621440 | tf_op jit(solution)/shard_map/all_to_all | solution.py:342
  86.0 1.6 %shard_map.87.own_far = bf16[160,32,128]{2,1,0:T(8,128)(2,1)S(1)} custom-call(bf16[32,160,128]{2,1,0:T(8,128)(2,1)S(1)} %all-to-all-done.got), custom_call_target="tpu_custom_call" | custom-call | tf_op jit(solution)/shard_map/pallas_call | solution.py:47
  87.6 1.1 copy-done
  88.7 14.6 %all-to-all-done.1.other = bf16[32,160,128]{2,1,0:T(8,128)(2,1)S(1)} async-done(((bf16[32,160,128]{2,1,0:T(8,128)(2,1)}), bf16[32,160,128]{2,1,0:T(8,128)(2,1)S(1)}, u32[]{:S(2)}, u32[]{:S(2)}) %all-to-all-start.1) | async-done | bytes 1310752 | tf_op jit(solution)/shard_map/all_to_all | solution.py:342
  103.2 4.1 %shard_map.90 = f32[256,128]{1,0:T(8,128)S(1)} custom-call(s32[4]{0:T(128)S(1)} %pad_add_fusion.at, bf16[160,32,128]{2,1,0:T(8,128)(2,1)} %copy-done, bf16[32,160,128]{2,1,0:T(8,128)(2,1)S(1)} %all-to-all-done.1.other), custom_call_target="tpu_custom_call" | custom-call | tf_op jit(solution)/shard_map/pallas_call | solution.py:47
  107.3 23.3 %all_to_all.15 = f32[256,1,128]{2,1,0:T(1,128)S(1)} all-to-all(f32[256,1,128]{2,1,0:T(1,128)S(1)} %bitcast.10), channel_id=1, replica_groups=mesh['zb'=2,'za'=2,'x'=4,'y'=4,'h'=2,'c'=2] {'zb','za','x','y','h','c'}, dimensions={0} | all-to-all | bytes 262144 | tf_op jit(solution)/shard_map/all_to_all | solution.py:353
  130.6 1.2 shard_map.91
  (18 shorter events, 1.7 us)
Async XLA Ops:
  0.0 10.7 %collective-permute-start.2 = (bf16[128,512]{1,0:T(8,128)(2,1)}, bf16[128,512]{1,0:T(8,128)(2,1)S(1)}, u32[]{:S(2)}, u32[]{:S(2)}) collective-permute-start(bf16[128,512]{1,0:T(8,128)(2,1)} %bitcast.12), channel_id=1, source_target_pairs={{0,2},{2,0},{1,3},{3,1},{4,6},{6,4},{5,7},{7,5},{8,10},{10,8},{9,1... | collective-permute-start | bytes 393224 | tf_op jit(solution)/shard_map/ppermute | solution.py:25
  7.7 8.1 %collective-permute-start.4 = (bf16[128,512]{1,0:T(8,128)(2,1)}, bf16[128,512]{1,0:T(8,128)(2,1)S(1)}, u32[]{:S(2)}, u32[]{:S(2)}) collective-permute-start(bf16[128,512]{1,0:T(8,128)(2,1)} %bitcast.15), channel_id=1, source_target_pairs={{0,2},{2,0},{1,3},{3,1},{4,6},{6,4},{5,7},{7,5},{8,10},{10,8},{9,1... | collective-permute-start | bytes 393224 | tf_op jit(solution)/shard_map/ppermute | solution.py:25
  7.7 13.9 %collective-permute-start = (bf16[128,512]{1,0:T(8,128)(2,1)}, bf16[128,512]{1,0:T(8,128)(2,1)S(1)}, u32[]{:S(2)}, u32[]{:S(2)}) collective-permute-start(bf16[128,512]{1,0:T(8,128)(2,1)} %bitcast.13), channel_id=1, source_target_pairs={{0,1},{1,0},{2,3},{3,2},{4,5},{5,4},{6,7},{7,6},{8,9},{9,8},{10,11... | collective-permute-start | bytes 393224 | tf_op jit(solution)/shard_map/ppermute | solution.py:25
  9.1 12.5 %collective-permute-start.1 = (bf16[128,512]{1,0:T(8,128)(2,1)}, bf16[128,512]{1,0:T(8,128)(2,1)S(1)}, u32[]{:S(2)}, u32[]{:S(2)}) collective-permute-start(bf16[128,512]{1,0:T(8,128)(2,1)} %bitcast.16), channel_id=1, source_target_pairs={{0,1},{1,0},{2,3},{3,2},{4,5},{5,4},{6,7},{7,6},{8,9},{9,8},{10,11... | collective-permute-start | bytes 393224 | tf_op jit(solution)/shard_map/ppermute | solution.py:25
  10.7 14.9 %collective-permute-start.3 = (bf16[128,512]{1,0:T(8,128)(2,1)S(1)}, bf16[128,512]{1,0:T(8,128)(2,1)S(1)}, u32[]{:S(2)}, u32[]{:S(2)}) collective-permute-start(bf16[128,512]{1,0:T(8,128)(2,1)S(1)} %collective-permute-done.2.s2), channel_id=1, source_target_pairs={{0,1},{1,0},{2,3},{3,2},{4,5},{5,4},{6,7},{7,6},{8,9},{9,8},{10,11... | collective-permute-start | bytes 393224 | tf_op jit(solution)/shard_map/ppermute | solution.py:25
  15.8 13.3 %collective-permute-start.5 = (bf16[128,512]{1,0:T(8,128)(2,1)S(1)}, bf16[128,512]{1,0:T(8,128)(2,1)S(1)}, u32[]{:S(2)}, u32[]{:S(2)}) collective-permute-start(bf16[128,512]{1,0:T(8,128)(2,1)S(1)} %collective-permute-done.4.c2), channel_id=1, source_target_pairs={{0,1},{1,0},{2,3},{3,2},{4,5},{5,4},{6,7},{7,6},{8,9},{9,8},{10,11... | collective-permute-start | bytes 393224 | tf_op jit(solution)/shard_map/ppermute | solution.py:25
  21.6 4.0 %copy-start.1 = (f32[128,128]{1,0:T(8,128)S(1)}, f32[128,128]{1,0:T(8,128)}, u32[]{:S(2)}) copy-start(f32[128,128]{1,0:T(8,128)} %constant.33.clone.cos_ref) | copy-start | bytes 196612
  21.6 4.0 %copy-start.2 = (f32[128,128]{1,0:T(8,128)S(1)}, f32[128,128]{1,0:T(8,128)}, u32[]{:S(2)}) copy-start(f32[128,128]{1,0:T(8,128)} %constant.34.clone.sine_ref) | copy-start | bytes 196612
  32.6 41.9 %all-to-all-start = ((bf16[32,160,128]{2,1,0:T(8,128)(2,1)}), bf16[32,160,128]{2,1,0:T(8,128)(2,1)S(1)}, u32[]{:S(2)}, u32[]{:S(2)}) async-start(bf16[32,160,128]{2,1,0:T(8,128)(2,1)} %shard_map.86), calls=%async_computation | async-start | bytes 2621440 | tf_op jit(solution)/shard_map/all_to_all | solution.py:338
  40.6 10.4 %collective-permute-start.6 = (bf16[256,512]{1,0:T(8,128)(2,1)S(1)}, bf16[256,512]{1,0:T(8,128)(2,1)S(1)}, u32[]{:S(2)}, u32[]{:S(2)}) collective-permute-start(bf16[256,512]{1,0:T(8,128)(2,1)S(1)} %get-tuple-element.14.own), channel_id=1, source_target_pairs={{128,0},{2,130},{129,1},{3,131},{132,4},{6,134},{133,5},{7,135},{1... | collective-permute-start | bytes 786440 | tf_op jit(solution)/shard_map/ppermute | solution.py:318
  41.9 9.1 %collective-permute-start.7 = (bf16[256,512]{1,0:T(8,128)(2,1)S(1)}, bf16[256,512]{1,0:T(8,128)(2,1)S(1)}, u32[]{:S(2)}, u32[]{:S(2)}) collective-permute-start(bf16[256,512]{1,0:T(8,128)(2,1)S(1)} %get-tuple-element.14.own), channel_id=1, source_target_pairs={{128,2},{2,128},{129,3},{3,129},{132,6},{6,132},{133,7},{7,133},{1... | collective-permute-start | bytes 786440 | tf_op jit(solution)/shard_map/ppermute | solution.py:319
  51.6 20.8 %collective-permute-start.8 = (bf16[256,512]{1,0:T(8,128)(2,1)S(1)}, bf16[256,512]{1,0:T(8,128)(2,1)S(1)}, u32[]{:S(2)}, u32[]{:S(2)}) collective-permute-start(bf16[256,512]{1,0:T(8,128)(2,1)S(1)} %shard_map.88.piece), channel_id=1, source_target_pairs={{0,1},{1,0},{2,3},{3,2},{4,5},{5,4},{6,7},{7,6},{8,9},{9,8},{10,11... | collective-permute-start | bytes 786440 | tf_op jit(solution)/shard_map/ppermute | solution.py:25
  52.8 19.5 %collective-permute-start.9 = (bf16[128,640]{1,0:T(8,128)(2,1)S(1)}, bf16[128,640]{1,0:T(8,128)(2,1)S(1)}, u32[]{:S(2)}, u32[]{:S(2)}) collective-permute-start(bf16[128,640]{1,0:T(8,128)(2,1)S(1)} %shard_map.85.factors), channel_id=1, source_target_pairs={{0,128},{128,0},{1,129},{129,1},{2,130},{130,2},{3,131},{131,3},{4... | collective-permute-start | bytes 491528 | tf_op jit(solution)/shard_map/ppermute | solution.py:25
  74.5 28.7 %all-to-all-start.1 = ((bf16[32,160,128]{2,1,0:T(8,128)(2,1)}), bf16[32,160,128]{2,1,0:T(8,128)(2,1)S(1)}, u32[]{:S(2)}, u32[]{:S(2)}) async-start(bf16[32,160,128]{2,1,0:T(8,128)(2,1)} %shard_map.89), calls=%async_computation.1 | async-start | bytes 2621440 | tf_op jit(solution)/shard_map/all_to_all | solution.py:342
  87.6 1.1 copy-start

commit v5 on v3

--- a/solution.py
+++ b/solution.py
@@ -1,5 +1,6 @@
 import jax
 import jax.numpy as jnp
+import numpy as np
 from jax import lax
 from jax.experimental import pallas as pl
 from jax.experimental.pallas import tpu as pltpu
@@ -26,19 +27,21 @@
 
 def rope_tables(length, head_dim):
     half_dim = head_dim // 2
-    freqs_k = theta_base ** (-(jnp.arange(half_dim, dtype=jnp.float32) * 2.0 / head_dim))
-    angles = jnp.arange(length, dtype=jnp.float32)[:, None] * freqs_k[None, :]
-    sine = jnp.sin(angles)
-    cos = jnp.tile(jnp.cos(angles), (1, LANES // half_dim))
-    return cos, jnp.tile(jnp.concatenate([-sine, sine], axis=1), (1, LANES // head_dim))
+    steps = np.arange(half_dim, dtype=np.float32) * np.float32(2.0) / np.float32(head_dim)
+    freqs_k = np.power(np.float32(theta_base), -steps)
+    angles = np.arange(length, dtype=np.float32)[:, None] * freqs_k[None, :]
+    sine = np.sin(angles)
+    cos = np.tile(np.cos(angles), (1, LANES // half_dim))
+    return cos, np.tile(np.concatenate([-sine, sine], axis=1), (1, LANES // head_dim))
 
 
 def dot(left, right, dims=((1,), (0,))):
     return lax.dot_general(left, right, (dims, ((), ())), preferred_element_type=jnp.float32)
 
 
-def kernel_call(body, outs, ins, scratch=(), vmem_mib=16, far=()):
-    hbm = pl.BlockSpec(memory_space=pl.ANY)
+def kernel_call(body, outs, ins, scratch=(), vmem_mib=20, far=()):
+    ins = [pltpu.with_memory_space_constraint(a, pltpu.HBM) if i in far else a for i, a in enumerate(ins)]
+    hbm = pl.BlockSpec(memory_space=pltpu.HBM)
     smem = pl.BlockSpec(memory_space=pltpu.SMEM)
     vmem = pl.BlockSpec(memory_space=pltpu.VMEM)
     return pl.pallas_call(
@@ -193,52 +196,44 @@
         put_blocks(blocks, turned_v, (width, width + LANES), state, col_at)
 
 
-def own_body(at, c0, c1, c2, c3, s0, s1, s2, s3, factors, blocks):
+def own_body(at, s0, s1, s2, s3, c0, c1, c2, c3, factors, blocks):
     here = at[0] == at[2]
 
-    def half(parts):
+    def half(*parts):
         return [jnp.where(here, parts[k][...], parts[k + 2][...]) for k in range(2)]
 
-    put_all(at, factors, half((c0, c1, c2, c3)), half((s0, s1, s2, s3)), blocks)
-
-
-def other_body(at, c0, c1, s0, s1, factors, blocks):
-    put_all(at, factors, (c0[...], c1[...]), (s0[...], s1[...]), blocks)
-
-
-def turn_blocks(got, wide, keep):
-    seqs, tall, _ = got.shape
+    put_all(at, factors, half(c0, c1, c2, c3), half(s0, s1, s2, s3), blocks)
+
+
+def pick_body(at, own, far, piece):
+    piece[...] = jnp.where(at[0] == at[2], far[...], own[...])
+
+
+def other_body(at, s0, s1, c0, c1, factors, own_blocks, blocks):
+    tall = own_blocks.shape[1]
+    blocks[:, :tall, :] = own_blocks[...]
+    put_all(at, factors, (c0[...], c1[...]), (s0[...], s1[...]), blocks.at[:, tall:, :])
+
+
+def share_body(at, got, rows_out, wide):
+    seqs, both, _ = got.shape
+    tall = both // 2
+    straight = at[2] == 0
     for s in range(seqs):
-        wide[pl.ds(s * tall, tall), :] = got[s].astype(jnp.float32)
-    for r in range(tall):
-        keep(r, wide[pl.ds(r, seqs, stride=tall), :].astype(jnp.bfloat16))
-
-
-def turn_body(got, turned, wide):
-    def keep(r, rows):
-        turned[r] = rows
-
-    turn_blocks(got, wide, keep)
-
-
-def share_body(at, own, other, rows_out, wide):
-    _, seqs, _ = own.shape
-    straight = at[2] == 0
+        wide[pl.ds(s * both, both), :] = got[s].astype(jnp.float32)
+
+    def rows_of(r):
+        found = [
+            wide[pl.ds(r + k * tall, seqs, stride=both), :].astype(jnp.bfloat16) for k in range(2)
+        ]
+        return jnp.concatenate(
+            [jnp.where(straight, found[0], found[1]), jnp.where(straight, found[1], found[0])], axis=0
+        )
+
     total = jnp.zeros((2 * seqs, 2 * seqs), jnp.float32)
-    waiting = []
-
-    def keep(r, rows):
-        nonlocal total
-        mine = own[r]
-        waiting.append(
-            jnp.concatenate([jnp.where(straight, mine, rows), jnp.where(straight, rows, mine)], axis=0)
-        )
-        if len(waiting) == 2:
-            x = jnp.concatenate(waiting, axis=1)
-            total = total + dot(x, x, ((1,), (1,)))
-            waiting.clear()
-
-    turn_blocks(other, wide, keep)
+    for r in range(0, tall, 2):
+        x = jnp.concatenate([rows_of(r), rows_of(r + 1)], axis=1)
+        total = total + dot(x, x, ((1,), (1,)))
     eye = lax.broadcasted_iota(jnp.int32, total.shape, 0) == lax.broadcasted_iota(
         jnp.int32, total.shape, 1
     )
@@ -265,21 +260,15 @@
     states, cotangent = states[0], cotangent[0]
     axes = (lax.axis_index("h"), lax.axis_index("c"), lax.axis_index("zb"), lax.axis_index(SEQ))
     at = jnp.stack(axes).astype(jnp.int32)
-    far_half = axes[0] == axes[2]
     blocks = lax.axis_size(NEAR)
     seqs = 2 * blocks
     tall = (part + LANES) * (2 * part) // (LANES * blocks)
     block_shape = shape((blocks, tall, LANES), bf16)
-    wide = pltpu.VMEM((blocks * tall, LANES), f32)
 
     def gathered(own):
         far = swapped(own, "h")
         near = swapped(own, "c")
         return near, far, swapped(far, "c")
-
-    def partner(own, far):
-        piece = swapped(jnp.where(far_half, far, own), "zb")
-        return piece, swapped(piece, "c")
 
     s1, s2, s3 = gathered(states)
     c1, c2, c3 = gathered(cotangent)
@@ -296,6 +285,14 @@
         (pltpu.SemaphoreType.DMA((6,)),),
         far=(1, 3, 5, 6, 7, 8),
     )
+
+    def partner(own, far):
+        piece = kernel_call(pick_body, shape(far.shape, bf16), (at, own, far))
+        piece = swapped(piece, "zb")
+        return piece, swapped(piece, "c")
+
+    s_pieces = partner(s0, s2)
+    c_pieces = partner(c0, c2)
     attended, probs = kernel_call(
         attention_body,
         (shape((length, part), bf16), shape((part // HEAD_DIM * length, length), bf16)),
@@ -305,21 +302,19 @@
         grads_body, shape((length, part + LANES), bf16), (at, c2, c3, wo, grads, attended, probs)
     )
     other_factors = swapped(factors, "zb")
-    own_blocks = kernel_call(own_body, block_shape, (at, c0, c1, c2, c3, s0, s1, s2, s3, factors))
-    got_own = lax.all_to_all(own_blocks, NEAR, 0, 0, tiled=True)
-    other_blocks = kernel_call(
+    own_blocks = kernel_call(own_body, block_shape, (at, s0, s1, s2, s3, c0, c1, c2, c3, factors))
+    sent = kernel_call(
         other_body,
-        block_shape,
-        (at, *partner(c0, c2), *partner(s0, s2), other_factors),
-    )
-    got_other = lax.all_to_all(other_blocks, NEAR, 0, 0, tiled=True)
-    own_turned = kernel_call(turn_body, shape((tall, blocks, LANES), bf16), (got_own,), (wide,))
+        shape((blocks, 2 * tall, LANES), bf16),
+        (at, *s_pieces, *c_pieces, other_factors, own_blocks),
+    )
+    got = lax.all_to_all(sent, NEAR, 0, 0, tiled=True)
     copies = lax.axis_size(TP)
     rows = kernel_call(
         share_body,
         shape((seqs * copies, 2 * seqs), f32),
-        (at, own_turned, got_other),
-        (wide,),
+        (at, got),
+        (pltpu.VMEM((seqs * tall, LANES), f32),),
     )
     rows = rows.reshape(seqs * copies, 1, 2 * seqs)
     got = lax.all_to_all(rows, EVERY, 0, 0, tiled=True).reshape(seqs * copies, 2 * seqs)

time: 128 us -> 117 us (0.914)
  blocking collectives: 25 us -> 63.6 us
  waiting for transfers between devices: 38.8 us -> 9.79 us
  starting transfers between devices: 36.6 us -> 25.6 us
  local copies, waits for them, and re-layouts: 9.64 us -> 0.01 us
    all_to_all x0 -> x1, blocking collectives: none -> 39.1 us  [on_device(): got = lax.all_to_all(sent, NEAR, 0, 0, tiled=True)]
    all_to_all x2 -> x0, waiting for transfers between devices: 16 us -> none  [the longest x1 14.1 us: on_device(): got_other = lax.all_to_all(other_blocks, NEAR, 0, 0, tiled=True)]
    all_to_all x2 -> x0, starting transfers between devices: 14.9 us -> none  [the longest x1 7.53 us: on_device(): got_own = lax.all_to_all(own_blocks, NEAR, 0, 0, tiled=True)]
    ppermute x11, waiting for transfers between devices: 22.7 us -> 9.79 us  [swapped(): return lax.ppermute(value, axis, SWAP)]
    unnamed x16 -> x4, local copies, waits for them, and re-layouts: 9.45 us -> 0.01 us
    ppermute x11, starting transfers between devices: 21.7 us -> 25.6 us  [swapped(): return lax.ppermute(value, axis, SWAP)]
    pallas_call x8 -> x9, Pallas kernels: 16.8 us -> 17.7 us  [kernel_call(): pl.pallas_call(body, out_shape=outs, in_specs=[hbm if i in far else smem...]
  transfers between devices with their start and end apart: 13 -> 11, of which waited for: 8 -> 5; matrix products, arithmetic and copies ran while one was open for 0% -> 0% of each run, Pallas kernels for 7% -> 9%
where the time goes in v5:
time: 117 us
  blocking collectives  63.6 us (54%)
  starting transfers between devices  25.6 us (22%)
  Pallas kernels  17.7 us (15%)
  waiting for transfers between devices  9.79 us (8%)
    all_to_all x1, blocking collectives, on_device(): got = lax.all_to_all(sent, NEAR, 0, 0, tiled=True)  39.1 us
    ppermute x11, starting transfers between devices, swapped(): return lax.ppermute(value, axis, SWAP)  25.6 us
    all_to_all x1, blocking collectives, on_device(): lax.all_to_all(rows, EVERY, 0, 0, tiled=True)  24.6 us
    pallas_call x9, Pallas kernels, kernel_call(): pl.pallas_call(body, out_shape=outs, in_specs=[hbm if i in far else smem...  17.7 us
    ppermute x11, waiting for transfers between devices, swapped(): return lax.ppermute(value, axis, SWAP)  9.79 us
  transfers between devices with their start and end apart: 11, of which 5 were waited for; matrix products, arithmetic and copies ran while one was open for 0% of the time, Pallas kernels for 9%

profile of v5, /device:TPU:1, one launch (start us, length us, event | category | flops | bytes accessed | tf_op | source)
XLA Modules:
  0.0 116.9 jit_solution(8268029622370710163)
XLA Ops:
  0.0 7.7 %collective-permute-start.2 = (bf16[128,512]{1,0:T(8,128)(2,1)}, bf16[128,512]{1,0:T(8,128)(2,1)S(1)}, u32[]{:S(2)}, u32[]{:S(2)}) collective-permute-start(bf16[128,512]{1,0:T(8,128)(2,1)} %bitcast.12), channel_id=1, source_target_pairs={{0,2},{2,0},{1,3},{3,1},{4,6},{6,4},{5,7},{7,5},{8,10},{10,8},{9,1... | collective-permute-start | bytes 393224 | tf_op jit(solution)/shard_map/ppermute | solution.py:25
  7.7 1.4 %collective-permute-start = (bf16[128,512]{1,0:T(8,128)(2,1)}, bf16[128,512]{1,0:T(8,128)(2,1)S(1)}, u32[]{:S(2)}, u32[]{:S(2)}) collective-permute-start(bf16[128,512]{1,0:T(8,128)(2,1)} %bitcast.13), channel_id=1, source_target_pairs={{0,1},{1,0},{2,3},{3,2},{4,5},{5,4},{6,7},{7,6},{8,9},{9,8},{10,11... | collective-permute-start | bytes 393224 | tf_op jit(solution)/shard_map/ppermute | solution.py:25
  9.1 1.5 %collective-permute-done.2.far.s2 = bf16[128,512]{1,0:T(8,128)(2,1)S(1)} collective-permute-done((bf16[128,512]{1,0:T(8,128)(2,1)}, bf16[128,512]{1,0:T(8,128)(2,1)S(1)}, u32[]{:S(2)}, u32[]{:S(2)}) %collective-permute-start.2) | collective-permute-done | bytes 131104 | tf_op jit(solution)/shard_map/ppermute | solution.py:25
  10.7 4.8 %collective-permute-start.9 = (bf16[128,512]{1,0:T(8,128)(2,1)S(1)}, bf16[128,512]{1,0:T(8,128)(2,1)S(1)}, u32[]{:S(2)}, u32[]{:S(2)}) collective-permute-start(bf16[128,512]{1,0:T(8,128)(2,1)S(1)} %collective-permute-done.2.far.s2), channel_id=1, source_target_pairs={{0,1},{1,0},{2,3},{3,2},{4,5},{5,4},{6,7},{7,6},{8,9},{9,8},{10,11... | collective-permute-start | bytes 393224 | tf_op jit(solution)/shard_map/ppermute | solution.py:25
  15.8 4.6 %collective-permute-start.8 = (bf16[128,512]{1,0:T(8,128)(2,1)S(1)}, bf16[128,512]{1,0:T(8,128)(2,1)S(1)}, u32[]{:S(2)}, u32[]{:S(2)}) collective-permute-start(bf16[128,512]{1,0:T(8,128)(2,1)S(1)} %collective-permute-done.5.far.c2), channel_id=1, source_target_pairs={{0,1},{1,0},{2,3},{3,2},{4,5},{5,4},{6,7},{7,6},{8,9},{9,8},{10,11... | collective-permute-start | bytes 393224 | tf_op jit(solution)/shard_map/ppermute | solution.py:25
  20.5 4.0 %shard_map.82 = (bf16[128,512]{1,0:T(8,128)(2,1)S(1)}, bf16[128,512]{1,0:T(8,128)(2,1)S(1)}, bf16[2048,512]{1,0:T(8,128)(2,1)S(1)}, bf16[2048,128]{1,0:T(8,128)(...) custom-call(s32[4]{0:T(128)S(1)} %pad_add_fusion.at, ...), custom_call_target="tpu_custom_call" | custom-call | tf_op jit(solution)/shard_map/pallas_call | solution.py:47
  24.5 0.6 shard_map.84
  25.0 2.0 %collective-permute-start.6 = (bf16[128,512]{1,0:T(8,128)(2,1)S(1)}, bf16[128,512]{1,0:T(8,128)(2,1)S(1)}, u32[]{:S(2)}, u32[]{:S(2)}) collective-permute-start(bf16[128,512]{1,0:T(8,128)(2,1)S(1)} %shard_map.84), channel_id=1, source_target_pairs={{0,128},{128,0},{1,129},{129,1},{2,130},{130,2},{3,131},{131,3},{4... | collective-permute-start | bytes 393224 | tf_op jit(solution)/shard_map/ppermute | solution.py:25
  27.0 0.6 shard_map.83
  27.6 0.6 collective-permute-start.3
  28.2 3.5 %shard_map.85 = (bf16[128,512]{1,0:T(8,128)(2,1)S(1)}, bf16[1024,128]{1,0:T(8,128)(2,1)S(1)}) custom-call(s32[4]{0:T(128)S(1)} %pad_add_fusion.at, bf16[128,512]{1,0:T(8,128)(2,1)S(1)} %collective-permute-done.2.far.s2, bf16[128,512]{1,0:T(8,128)(2,1)S(1)} %collective-permute-done.9.s3, bf16[2048,512]{1,0:T(8,128)(2,1)S(1)} %get-tuple-element.19.wq, ...), custom_call_target="tpu_custom_call" | custom-call | tf_op jit(solution)/shard_map/pallas_call | solution.py:47
  31.7 1.3 %shard_map.86.factors = bf16[128,640]{1,0:T(8,128)(2,1)S(1)} custom-call(s32[4]{0:T(128)S(1)} %pad_add_fusion.at, bf16[128,512]{1,0:T(8,128)(2,1)S(1)} %collective-permute-done.5.far.c2, bf16[128,512]{1,0:T(8,128)(2,1)S(1)} %collective-permute-done.8.c3, bf16[512,2048]{1,0:T(8,128)(2,1)S(1)} %get-tuple-element.17.wo, ...), custom_call_target="tpu_custom_call" | custom-call | tf_op jit(solution)/shard_map/pallas_call | solution.py:47
  33.0 2.0 %collective-permute-start.10 = (bf16[128,640]{1,0:T(8,128)(2,1)S(1)}, bf16[128,640]{1,0:T(8,128)(2,1)S(1)}, u32[]{:S(2)}, u32[]{:S(2)}) collective-permute-start(bf16[128,640]{1,0:T(8,128)(2,1)S(1)} %shard_map.86.factors), channel_id=1, source_target_pairs={{0,128},{128,0},{1,129},{129,1},{2,130},{130,2},{3,131},{131,3},{4... | collective-permute-start | bytes 491528 | tf_op jit(solution)/shard_map/ppermute | solution.py:25
  34.9 1.8 %collective-permute-done.6.c0 = bf16[128,512]{1,0:T(8,128)(2,1)S(1)} collective-permute-done((bf16[128,512]{1,0:T(8,128)(2,1)S(1)}, bf16[128,512]{1,0:T(8,128)(2,1)S(1)}, u32[]{:S(2)}, u32[]{:S(2)}) %collective-permute-start.6) | collective-permute-done | bytes 131104 | tf_op jit(solution)/shard_map/ppermute | solution.py:25
  36.7 1.3 %collective-permute-start.7 = (bf16[128,512]{1,0:T(8,128)(2,1)S(1)}, bf16[128,512]{1,0:T(8,128)(2,1)S(1)}, u32[]{:S(2)}, u32[]{:S(2)}) collective-permute-start(bf16[128,512]{1,0:T(8,128)(2,1)S(1)} %collective-permute-done.6.c0), channel_id=1, source_target_pairs={{0,1},{1,0},{2,3},{3,2},{4,5},{5,4},{6,7},{7,6},{8,9},{9,8},{10,11... | collective-permute-start | bytes 393224 | tf_op jit(solution)/shard_map/ppermute | solution.py:25
  38.0 5.0 %collective-permute-done.3.s0 = bf16[128,512]{1,0:T(8,128)(2,1)S(1)} collective-permute-done((bf16[128,512]{1,0:T(8,128)(2,1)S(1)}, bf16[128,512]{1,0:T(8,128)(2,1)S(1)}, u32[]{:S(2)}, u32[]{:S(2)}) %collective-permute-start.3) | collective-permute-done | bytes 131104 | tf_op jit(solution)/shard_map/ppermute | solution.py:25
  43.0 1.3 %collective-permute-start.4 = (bf16[128,512]{1,0:T(8,128)(2,1)S(1)}, bf16[128,512]{1,0:T(8,128)(2,1)S(1)}, u32[]{:S(2)}, u32[]{:S(2)}) collective-permute-start(bf16[128,512]{1,0:T(8,128)(2,1)S(1)} %collective-permute-done.3.s0), channel_id=1, source_target_pairs={{0,1},{1,0},{2,3},{3,2},{4,5},{5,4},{6,7},{7,6},{8,9},{9,8},{10,11... | collective-permute-start | bytes 393224 | tf_op jit(solution)/shard_map/ppermute | solution.py:25
  44.3 1.1 shard_map.87.own_blocks
  45.4 1.1 collective-permute-done.10.factors
  46.5 1.1 shard_map.88
  47.7 39.1 %all_to_all.10.got = bf16[32,320,128]{2,1,0:T(8,128)(2,1)S(1)} all-to-all(bf16[32,320,128]{2,1,0:T(8,128)(2,1)S(1)} %shard_map.88), channel_id=1, replica_groups=mesh['zb'=2,'za'=2,'x'=4,'y'=4,'h'=2,'c'=2] {'za','x','y'}, dimensions={0} | all-to-all | bytes 5242880 | tf_op jit(solution)/shard_map/all_to_all | solution.py:311
  86.7 4.5 %shard_map.89 = f32[256,128]{1,0:T(8,128)S(1)} custom-call(s32[4]{0:T(128)S(1)} %pad_add_fusion.at, bf16[32,320,128]{2,1,0:T(8,128)(2,1)S(1)} %all_to_all.10.got), custom_call_target="tpu_custom_call" | custom-call | tf_op jit(solution)/shard_map/pallas_call | solution.py:47
  91.2 24.6 %all_to_all.11 = f32[256,1,128]{2,1,0:T(1,128)S(1)} all-to-all(f32[256,1,128]{2,1,0:T(1,128)S(1)} %bitcast.10), channel_id=1, replica_groups=mesh['zb'=2,'za'=2,'x'=4,'y'=4,'h'=2,'c'=2] {'zb','za','x','y','h','c'}, dimensions={0} | all-to-all | bytes 262144 | tf_op jit(solution)/shard_map/all_to_all | solution.py:320
  115.8 1.2 %shard_map.90 = f32[1,64]{1,0:T(1,128)} custom-call(s32[4]{0:T(128)S(1)} %pad_add_fusion.at, f32[256,128]{1,0:T(8,128)S(1)} %bitcast.11), custom_call_target="tpu_custom_call" | custom-call | tf_op jit(solution)/shard_map/pallas_call | solution.py:47
  (14 shorter events, 0.5 us)
Async XLA Ops:
  0.0 10.7 %collective-permute-start.2 = (bf16[128,512]{1,0:T(8,128)(2,1)}, bf16[128,512]{1,0:T(8,128)(2,1)S(1)}, u32[]{:S(2)}, u32[]{:S(2)}) collective-permute-start(bf16[128,512]{1,0:T(8,128)(2,1)} %bitcast.12), channel_id=1, source_target_pairs={{0,2},{2,0},{1,3},{3,1},{4,6},{6,4},{5,7},{7,5},{8,10},{10,8},{9,1... | collective-permute-start | bytes 393224 | tf_op jit(solution)/shard_map/ppermute | solution.py:25
  7.7 8.1 %collective-permute-start.5 = (bf16[128,512]{1,0:T(8,128)(2,1)}, bf16[128,512]{1,0:T(8,128)(2,1)S(1)}, u32[]{:S(2)}, u32[]{:S(2)}) collective-permute-start(bf16[128,512]{1,0:T(8,128)(2,1)} %bitcast.15), channel_id=1, source_target_pairs={{0,2},{2,0},{1,3},{3,1},{4,6},{6,4},{5,7},{7,5},{8,10},{10,8},{9,1... | collective-permute-start | bytes 393224 | tf_op jit(solution)/shard_map/ppermute | solution.py:25
  7.7 12.7 %collective-permute-start = (bf16[128,512]{1,0:T(8,128)(2,1)}, bf16[128,512]{1,0:T(8,128)(2,1)S(1)}, u32[]{:S(2)}, u32[]{:S(2)}) collective-permute-start(bf16[128,512]{1,0:T(8,128)(2,1)} %bitcast.13), channel_id=1, source_target_pairs={{0,1},{1,0},{2,3},{3,2},{4,5},{5,4},{6,7},{7,6},{8,9},{9,8},{10,11... | collective-permute-start | bytes 393224 | tf_op jit(solution)/shard_map/ppermute | solution.py:25
  9.1 11.4 %collective-permute-start.1 = (bf16[128,512]{1,0:T(8,128)(2,1)}, bf16[128,512]{1,0:T(8,128)(2,1)S(1)}, u32[]{:S(2)}, u32[]{:S(2)}) collective-permute-start(bf16[128,512]{1,0:T(8,128)(2,1)} %bitcast.16), channel_id=1, source_target_pairs={{0,1},{1,0},{2,3},{3,2},{4,5},{5,4},{6,7},{7,6},{8,9},{9,8},{10,11... | collective-permute-start | bytes 393224 | tf_op jit(solution)/shard_map/ppermute | solution.py:25
  10.7 17.5 %collective-permute-start.9 = (bf16[128,512]{1,0:T(8,128)(2,1)S(1)}, bf16[128,512]{1,0:T(8,128)(2,1)S(1)}, u32[]{:S(2)}, u32[]{:S(2)}) collective-permute-start(bf16[128,512]{1,0:T(8,128)(2,1)S(1)} %collective-permute-done.2.far.s2), channel_id=1, source_target_pairs={{0,1},{1,0},{2,3},{3,2},{4,5},{5,4},{6,7},{7,6},{8,9},{9,8},{10,11... | collective-permute-start | bytes 393224 | tf_op jit(solution)/shard_map/ppermute | solution.py:25
  15.8 15.8 %collective-permute-start.8 = (bf16[128,512]{1,0:T(8,128)(2,1)S(1)}, bf16[128,512]{1,0:T(8,128)(2,1)S(1)}, u32[]{:S(2)}, u32[]{:S(2)}) collective-permute-start(bf16[128,512]{1,0:T(8,128)(2,1)S(1)} %collective-permute-done.5.far.c2), channel_id=1, source_target_pairs={{0,1},{1,0},{2,3},{3,2},{4,5},{5,4},{6,7},{7,6},{8,9},{9,8},{10,11... | collective-permute-start | bytes 393224 | tf_op jit(solution)/shard_map/ppermute | solution.py:25
  20.5 7.7 %copy-start = (f32[128,128]{1,0:T(8,128)S(1)}, f32[128,128]{1,0:T(8,128)}, u32[]{:S(2)}) copy-start(f32[128,128]{1,0:T(8,128)} %constant.33.clone.cos_ref) | copy-start | bytes 196612
  20.5 7.7 %copy-start.1 = (f32[128,128]{1,0:T(8,128)S(1)}, f32[128,128]{1,0:T(8,128)}, u32[]{:S(2)}) copy-start(f32[128,128]{1,0:T(8,128)} %constant.34.clone.sine_ref) | copy-start | bytes 196612
  25.0 11.7 %collective-permute-start.6 = (bf16[128,512]{1,0:T(8,128)(2,1)S(1)}, bf16[128,512]{1,0:T(8,128)(2,1)S(1)}, u32[]{:S(2)}, u32[]{:S(2)}) collective-permute-start(bf16[128,512]{1,0:T(8,128)(2,1)S(1)} %shard_map.84), channel_id=1, source_target_pairs={{0,128},{128,0},{1,129},{129,1},{2,130},{130,2},{3,131},{131,3},{4... | collective-permute-start | bytes 393224 | tf_op jit(solution)/shard_map/ppermute | solution.py:25
  27.6 15.4 %collective-permute-start.3 = (bf16[128,512]{1,0:T(8,128)(2,1)S(1)}, bf16[128,512]{1,0:T(8,128)(2,1)S(1)}, u32[]{:S(2)}, u32[]{:S(2)}) collective-permute-start(bf16[128,512]{1,0:T(8,128)(2,1)S(1)} %shard_map.83), channel_id=1, source_target_pairs={{0,128},{128,0},{1,129},{129,1},{2,130},{130,2},{3,131},{131,3},{4... | collective-permute-start | bytes 393224 | tf_op jit(solution)/shard_map/ppermute | solution.py:25
  33.0 13.6 %collective-permute-start.10 = (bf16[128,640]{1,0:T(8,128)(2,1)S(1)}, bf16[128,640]{1,0:T(8,128)(2,1)S(1)}, u32[]{:S(2)}, u32[]{:S(2)}) collective-permute-start(bf16[128,640]{1,0:T(8,128)(2,1)S(1)} %shard_map.86.factors), channel_id=1, source_target_pairs={{0,128},{128,0},{1,129},{129,1},{2,130},{130,2},{3,131},{131,3},{4... | collective-permute-start | bytes 491528 | tf_op jit(solution)/shard_map/ppermute | solution.py:25
  36.7 8.7 %collective-permute-start.7 = (bf16[128,512]{1,0:T(8,128)(2,1)S(1)}, bf16[128,512]{1,0:T(8,128)(2,1)S(1)}, u32[]{:S(2)}, u32[]{:S(2)}) collective-permute-start(bf16[128,512]{1,0:T(8,128)(2,1)S(1)} %collective-permute-done.6.c0), channel_id=1, source_target_pairs={{0,1},{1,0},{2,3},{3,2},{4,5},{5,4},{6,7},{7,6},{8,9},{9,8},{10,11... | collective-permute-start | bytes 393224 | tf_op jit(solution)/shard_map/ppermute | solution.py:25
  43.0 2.4 %collective-permute-start.4 = (bf16[128,512]{1,0:T(8,128)(2,1)S(1)}, bf16[128,512]{1,0:T(8,128)(2,1)S(1)}, u32[]{:S(2)}, u32[]{:S(2)}) collective-permute-start(bf16[128,512]{1,0:T(8,128)(2,1)S(1)} %collective-permute-done.3.s0), channel_id=1, source_target_pairs={{0,1},{1,0},{2,3},{3,2},{4,5},{5,4},{6,7},{7,6},{8,9},{9,8},{10,11... | collective-permute-start | bytes 393224 | tf_op jit(solution)/shard_map/ppermute | solution.py:25

commit v6 on v3

--- a/solution.py
+++ b/solution.py
@@ -1,5 +1,6 @@
 import jax
 import jax.numpy as jnp
+import numpy as np
 from jax import lax
 from jax.experimental import pallas as pl
 from jax.experimental.pallas import tpu as pltpu
@@ -26,11 +27,12 @@
 
 def rope_tables(length, head_dim):
     half_dim = head_dim // 2
-    freqs_k = theta_base ** (-(jnp.arange(half_dim, dtype=jnp.float32) * 2.0 / head_dim))
-    angles = jnp.arange(length, dtype=jnp.float32)[:, None] * freqs_k[None, :]
-    sine = jnp.sin(angles)
-    cos = jnp.tile(jnp.cos(angles), (1, LANES // half_dim))
-    return cos, jnp.tile(jnp.concatenate([-sine, sine], axis=1), (1, LANES // head_dim))
+    steps = np.arange(half_dim, dtype=np.float32) * np.float32(2.0) / np.float32(head_dim)
+    freqs_k = np.power(np.float32(theta_base), -steps)
+    angles = np.arange(length, dtype=np.float32)[:, None] * freqs_k[None, :]
+    sine = np.sin(angles)
+    cos = np.tile(np.cos(angles), (1, LANES // half_dim))
+    return cos, np.tile(np.concatenate([-sine, sine], axis=1), (1, LANES // head_dim))
 
 
 def dot(left, right, dims=((1,), (0,))):
@@ -38,7 +40,8 @@
 
 
 def kernel_call(body, outs, ins, scratch=(), vmem_mib=16, far=()):
-    hbm = pl.BlockSpec(memory_space=pl.ANY)
+    ins = [pltpu.with_memory_space_constraint(a, pltpu.HBM) if i in far else a for i, a in enumerate(ins)]
+    hbm = pl.BlockSpec(memory_space=pltpu.HBM)
     smem = pl.BlockSpec(memory_space=pltpu.SMEM)
     vmem = pl.BlockSpec(memory_space=pltpu.VMEM)
     return pl.pallas_call(
@@ -99,7 +102,10 @@
     )
 
 
-def attention_body(at, s2, s3, wq, wk, wv, sums, cos_ref, sine_ref, attended, probs):
+def attention_body(
+    at, s0, s2, s3, wq, wk, wv, sums, cos_ref, sine_ref, attended, probs, piece
+):
+    piece[...] = jnp.where(at[0] == at[2], s2[...], s0[...])
     quarter = s2.shape[1]
     far = places_of(at)[2:]
 
@@ -161,7 +167,7 @@
         row = stop
 
 
-def grads_body(at, c2, c3, wo, partial, attended, probs, factors):
+def grads_body(at, c0, c2, c3, wo, partial, attended, probs, packed):
     length, quarter = c2.shape
     grads = partial[...]
     for part, place in zip((c2, c3), places_of(at)[2:]):
@@ -179,37 +185,41 @@
         found = dot(probs[g * rows : (g + 1) * rows, :], jnp.concatenate(stacked, 0), ((0,), (0,)))
         sums.append(found + pltpu.roll(found, HEAD_DIM, 1))
     width = attended.shape[1]
-    factors[:, :width] = attended[...]
-    factors[:, width:] = jnp.where(low, sums[0], sums[1]).astype(jnp.bfloat16)
-
-
-def put_all(at, factors, cots, states, blocks):
-    width = factors.shape[1] - LANES
-    turned_a = factors[:, :width].T
-    turned_v = factors[:, width:].T
+    packed[:, :width] = attended[...]
+    packed[:, width : width + LANES] = jnp.where(low, sums[0], sums[1]).astype(jnp.bfloat16)
+    packed[:, width + LANES :] = jnp.where(at[0] == at[2], c2[...], c0[...])
+
+
+def put_all(at, packed, cots, states, blocks):
+    width = states[0].shape[1]
+    turned_a = packed[:, :width].T
+    turned_v = packed[:, width : width + LANES].T
     for k, (cot, state) in enumerate(zip(cots, states)):
-        col_at = jnp.where(at[1] == 1, 1 - k, k) * (cot.shape[1] // LANES)
+        col_at = jnp.where(at[1] == 1, 1 - k, k) * (width // LANES)
         put_blocks(blocks, turned_a, (0, width), cot, col_at)
         put_blocks(blocks, turned_v, (width, width + LANES), state, col_at)
 
 
-def own_body(at, c0, c1, c2, c3, s0, s1, s2, s3, factors, blocks):
+def own_body(at, s0, s1, s2, s3, c0, c1, c2, c3, packed, blocks):
     here = at[0] == at[2]
 
-    def half(parts):
+    def half(*parts):
         return [jnp.where(here, parts[k][...], parts[k + 2][...]) for k in range(2)]
 
-    put_all(at, factors, half((c0, c1, c2, c3)), half((s0, s1, s2, s3)), blocks)
-
-
-def other_body(at, c0, c1, s0, s1, factors, blocks):
-    put_all(at, factors, (c0[...], c1[...]), (s0[...], s1[...]), blocks)
-
-
-def turn_blocks(got, wide, keep):
+    put_all(at, packed, half(c0, c1, c2, c3), half(s0, s1, s2, s3), blocks)
+
+
+def other_body(at, s0, s1, packed, packed_near, blocks):
+    begin = s0.shape[1] + LANES
+    cots = (packed[:, begin:], packed_near[:, begin:])
+    put_all(at, packed, cots, (s0[...], s1[...]), blocks)
+
+
+def turn_blocks(got, wide, keep, ready=lambda: None):
     seqs, tall, _ = got.shape
     for s in range(seqs):
         wide[pl.ds(s * tall, tall), :] = got[s].astype(jnp.float32)
+    ready()
     for r in range(tall):
         keep(r, wide[pl.ds(r, seqs, stride=tall), :].astype(jnp.bfloat16))
 
@@ -221,8 +231,10 @@
     turn_blocks(got, wide, keep)
 
 
-def share_body(at, own, other, rows_out, wide):
+def share_body(at, own_far, other, rows_out, wide, own, sem):
     _, seqs, _ = own.shape
+    fetch = pltpu.make_async_copy(own_far, own, sem)
+    fetch.start()
     straight = at[2] == 0
     total = jnp.zeros((2 * seqs, 2 * seqs), jnp.float32)
     waiting = []
@@ -238,7 +250,7 @@
             total = total + dot(x, x, ((1,), (1,)))
             waiting.clear()
 
-    turn_blocks(other, wide, keep)
+    turn_blocks(other, wide, keep, fetch.wait)
     eye = lax.broadcasted_iota(jnp.int32, total.shape, 0) == lax.broadcasted_iota(
         jnp.int32, total.shape, 1
     )
@@ -265,7 +277,6 @@
     states, cotangent = states[0], cotangent[0]
     axes = (lax.axis_index("h"), lax.axis_index("c"), lax.axis_index("zb"), lax.axis_index(SEQ))
     at = jnp.stack(axes).astype(jnp.int32)
-    far_half = axes[0] == axes[2]
     blocks = lax.axis_size(NEAR)
     seqs = 2 * blocks
     tall = (part + LANES) * (2 * part) // (LANES * blocks)
@@ -276,10 +287,6 @@
         far = swapped(own, "h")
         near = swapped(own, "c")
         return near, far, swapped(far, "c")
-
-    def partner(own, far):
-        piece = swapped(jnp.where(far_half, far, own), "zb")
-        return piece, swapped(piece, "c")
 
     s1, s2, s3 = gathered(states)
     c1, c2, c3 = gathered(cotangent)
@@ -296,21 +303,28 @@
         (pltpu.SemaphoreType.DMA((6,)),),
         far=(1, 3, 5, 6, 7, 8),
     )
-    attended, probs = kernel_call(
+    attended, probs, s_piece = kernel_call(
         attention_body,
-        (shape((length, part), bf16), shape((part // HEAD_DIM * length, length), bf16)),
-        (at, s2, s3, wq, wk, wv, sums, cos, sine),
-    )
-    factors = kernel_call(
-        grads_body, shape((length, part + LANES), bf16), (at, c2, c3, wo, grads, attended, probs)
-    )
-    other_factors = swapped(factors, "zb")
-    own_blocks = kernel_call(own_body, block_shape, (at, c0, c1, c2, c3, s0, s1, s2, s3, factors))
+        (
+            shape((length, part), bf16),
+            shape((part // HEAD_DIM * length, length), bf16),
+            shape((length, part), bf16),
+        ),
+        (at, s0, s2, s3, wq, wk, wv, sums, cos, sine),
+    )
+    s_piece = swapped(s_piece, "zb")
+    packed = kernel_call(
+        grads_body,
+        shape((length, 2 * part + LANES), bf16),
+        (at, c0, c2, c3, wo, grads, attended, probs),
+    )
+    other_packed = swapped(packed, "zb")
+    own_blocks = kernel_call(own_body, block_shape, (at, s0, s1, s2, s3, c0, c1, c2, c3, packed))
     got_own = lax.all_to_all(own_blocks, NEAR, 0, 0, tiled=True)
+    s_near = swapped(s_piece, "c")
+    packed_near = swapped(other_packed, "c")
     other_blocks = kernel_call(
-        other_body,
-        block_shape,
-        (at, *partner(c0, c2), *partner(s0, s2), other_factors),
+        other_body, block_shape, (at, s_piece, s_near, other_packed, packed_near)
     )
     got_other = lax.all_to_all(other_blocks, NEAR, 0, 0, tiled=True)
     own_turned = kernel_call(turn_body, shape((tall, blocks, LANES), bf16), (got_own,), (wide,))
@@ -319,7 +333,8 @@
         share_body,
         shape((seqs * copies, 2 * seqs), f32),
         (at, own_turned, got_other),
-        (wide,),
+        (wide, pltpu.VMEM(own_turned.shape, bf16), pltpu.SemaphoreType.DMA),
+        far=(1,),
     )
     rows = rows.reshape(seqs * copies, 1, 2 * seqs)
     got = lax.all_to_all(rows, EVERY, 0, 0, tiled=True).reshape(seqs * copies, 2 * seqs)

time: 128 us -> 129 us (level)
  local copies, waits for them, and re-layouts: 9.64 us -> 1.07 us
  waiting for transfers between devices: 38.8 us -> 43.8 us
  Pallas kernels: 16.8 us -> 19.9 us
  starting transfers between devices: 36.6 us -> 39.2 us
    unnamed x16 -> x6, local copies, waits for them, and re-layouts: 9.45 us -> 1.07 us
    ppermute x11 -> x10, waiting for transfers between devices: 22.7 us -> 28.9 us  [swapped(): return lax.ppermute(value, axis, SWAP)]
    pallas_call x8, Pallas kernels: 16.8 us -> 19.9 us  [kernel_call(): pl.pallas_call(body, out_shape=outs, in_specs=[hbm if i in far else smem...]
    ppermute x11 -> x10, starting transfers between devices: 21.7 us -> 24.1 us  [swapped(): return lax.ppermute(value, axis, SWAP)]
    all_to_all x1, waiting for transfers between devices: 1.9 us -> 0.01 us  [on_device(): got_own = lax.all_to_all(own_blocks, NEAR, 0, 0, tiled=True)]
  transfers between devices with their start and end apart: 13 -> 12, of which waited for: 8 -> 6; matrix products, arithmetic and copies ran while one was open for 0% -> 0% of each run, Pallas kernels for 7% -> 9%
where the time goes in v6:
time: 129 us
  waiting for transfers between devices  43.8 us (34%)
  starting transfers between devices  39.2 us (30%)
  blocking collectives  24.7 us (19%)
  Pallas kernels  19.9 us (15%)
    ppermute x10, waiting for transfers between devices, swapped(): return lax.ppermute(value, axis, SWAP)  28.9 us
    all_to_all x1, blocking collectives, on_device(): lax.all_to_all(rows, EVERY, 0, 0, tiled=True)  24.7 us
    ppermute x10, starting transfers between devices, swapped(): return lax.ppermute(value, axis, SWAP)  24.1 us
    pallas_call x8, Pallas kernels, kernel_call(): pl.pallas_call(body, out_shape=outs, in_specs=[hbm if i in far else smem...  19.9 us
    all_to_all x1, waiting for transfers between devices, on_device(): got_other = lax.all_to_all(other_blocks, NEAR, 0, 0, tiled=True)  14.9 us
    all_to_all x1, starting transfers between devices, on_device(): got_own = lax.all_to_all(own_blocks, NEAR, 0, 0, tiled=True)  7.94 us
    all_to_all x1, starting transfers between devices, on_device(): got_other = lax.all_to_all(other_blocks, NEAR, 0, 0, tiled=True)  7.12 us
  transfers between devices with their start and end apart: 12, of which 6 were waited for; matrix products, arithmetic and copies ran while one was open for 0% of the time, Pallas kernels for 9%

profile of v6, /device:TPU:1, one launch (start us, length us, event | category | flops | bytes accessed | tf_op | source)
XLA Modules:
  0.0 128.7 jit_solution(14465206769520666226)
XLA Ops:
  0.0 7.7 %collective-permute-start.2 = (bf16[128,512]{1,0:T(8,128)(2,1)}, bf16[128,512]{1,0:T(8,128)(2,1)S(1)}, u32[]{:S(2)}, u32[]{:S(2)}) collective-permute-start(bf16[128,512]{1,0:T(8,128)(2,1)} %bitcast.12), channel_id=1, source_target_pairs={{0,2},{2,0},{1,3},{3,1},{4,6},{6,4},{5,7},{7,5},{8,10},{10,8},{9,1... | collective-permute-start | bytes 393224 | tf_op jit(solution)/shard_map/ppermute | solution.py:25
  7.7 1.4 %collective-permute-start = (bf16[128,512]{1,0:T(8,128)(2,1)}, bf16[128,512]{1,0:T(8,128)(2,1)S(1)}, u32[]{:S(2)}, u32[]{:S(2)}) collective-permute-start(bf16[128,512]{1,0:T(8,128)(2,1)} %bitcast.13), channel_id=1, source_target_pairs={{0,1},{1,0},{2,3},{3,2},{4,5},{5,4},{6,7},{7,6},{8,9},{9,8},{10,11... | collective-permute-start | bytes 393224 | tf_op jit(solution)/shard_map/ppermute | solution.py:25
  9.1 1.5 %collective-permute-done.2.s2 = bf16[128,512]{1,0:T(8,128)(2,1)S(1)} collective-permute-done((bf16[128,512]{1,0:T(8,128)(2,1)}, bf16[128,512]{1,0:T(8,128)(2,1)S(1)}, u32[]{:S(2)}, u32[]{:S(2)}) %collective-permute-start.2) | collective-permute-done | bytes 131104 | tf_op jit(solution)/shard_map/ppermute | solution.py:25
  10.7 4.8 %collective-permute-start.3 = (bf16[128,512]{1,0:T(8,128)(2,1)S(1)}, bf16[128,512]{1,0:T(8,128)(2,1)S(1)}, u32[]{:S(2)}, u32[]{:S(2)}) collective-permute-start(bf16[128,512]{1,0:T(8,128)(2,1)S(1)} %collective-permute-done.2.s2), channel_id=1, source_target_pairs={{0,1},{1,0},{2,3},{3,2},{4,5},{5,4},{6,7},{7,6},{8,9},{9,8},{10,11... | collective-permute-start | bytes 393224 | tf_op jit(solution)/shard_map/ppermute | solution.py:25
  15.8 4.6 %collective-permute-start.5 = (bf16[128,512]{1,0:T(8,128)(2,1)S(1)}, bf16[128,512]{1,0:T(8,128)(2,1)S(1)}, u32[]{:S(2)}, u32[]{:S(2)}) collective-permute-start(bf16[128,512]{1,0:T(8,128)(2,1)S(1)} %collective-permute-done.4.c2), channel_id=1, source_target_pairs={{0,1},{1,0},{2,3},{3,2},{4,5},{5,4},{6,7},{7,6},{8,9},{9,8},{10,11... | collective-permute-start | bytes 393224 | tf_op jit(solution)/shard_map/ppermute | solution.py:25
  20.5 3.9 %shard_map.82 = (bf16[128,512]{1,0:T(8,128)(2,1)S(1)}, bf16[128,512]{1,0:T(8,128)(2,1)S(1)}, bf16[2048,512]{1,0:T(8,128)(2,1)S(1)}, bf16[2048,128]{1,0:T(8,128)(...) custom-call(s32[4]{0:T(128)S(1)} %pad_add_fusion.at, ...), custom_call_target="tpu_custom_call" | custom-call | tf_op jit(solution)/shard_map/pallas_call | solution.py:47
  24.5 3.5 %shard_map.83 = (bf16[128,512]{1,0:T(8,128)(2,1)S(1)}, bf16[1024,128]{1,0:T(8,128)(2,1)S(1)}, bf16[128,512]{1,0:T(8,128)(2,1)S(1)}) custom-call(s32[4]{0:T(128)S(1)} %pad_add_fusion.at, bf16[128,512]{1,0:T(8,128)(2,1)S(1)} %get-tuple-element.16.s0, bf16[128,512]{1,0:T(8,128)(2,1)S(1)} %collective-permute-done.2.s2, ...), custom_call_target="tpu_custom_call" | custom-call | tf_op jit(solution)/shard_map/pallas_call | solution.py:47
  28.0 1.3 %shard_map.84.packed = bf16[128,1152]{1,0:T(8,128)(2,1)S(1)} custom-call(s32[4]{0:T(128)S(1)} %pad_add_fusion.at, bf16[128,512]{1,0:T(8,128)(2,1)S(1)} %get-tuple-element.17.c0, bf16[128,512]{1,0:T(8,128)(2,1)S(1)} %collective-permute-done.4.c2, bf16[128,512]{1,0:T(8,128)(2,1)S(1)} %collective-permute-done.5.c3, bf16[512,2048]{1,0:T(8,128)(2,1)S(1)} %get-tuple-element.18.wo, ...), custom_call_target="tpu_custom_call" | custom-call | tf_op jit(solution)/shard_map/pallas_call | solution.py:47
  29.3 2.1 %shard_map.85 = bf16[32,160,128]{2,1,0:T(8,128)(2,1)} custom-call(s32[4]{0:T(128)S(1)} %pad_add_fusion.at, bf16[128,512]{1,0:T(8,128)(2,1)S(1)} %get-tuple-element.16.s0, bf16[128,512]{1,0:T(8,128)(2,1)S(1)} %collective-permute-done.s1, bf16[128,512]{1,0:T(8,128)(2,1)S(1)} %collective-permute-done.2.s2, bf16[128,512]{1,0:T(8,128)(2,1)S(1)} %collective-permute-done.3.s3, ...), custom_call_target="tpu_custom_call" | custom-call | tf_op jit(solution)/shard_map/pallas_call | solution.py:47
  31.4 7.9 %all-to-all-start = ((bf16[32,160,128]{2,1,0:T(8,128)(2,1)}), bf16[32,160,128]{2,1,0:T(8,128)(2,1)S(1)}, u32[]{:S(2)}, u32[]{:S(2)}) async-start(bf16[32,160,128]{2,1,0:T(8,128)(2,1)} %shard_map.85), calls=%async_computation | async-start | bytes 2621440 | tf_op jit(solution)/shard_map/all_to_all | solution.py:323
  39.4 1.1 collective-permute-start.8
  40.5 19.3 %collective-permute-done.8.packed = bf16[128,1152]{1,0:T(8,128)(2,1)S(1)} collective-permute-done((bf16[128,1152]{1,0:T(8,128)(2,1)S(1)}, bf16[128,1152]{1,0:T(8,128)(2,1)S(1)}, u32[]{:S(2)}, u32[]{:S(2)}) %collective-permute-start.8) | collective-permute-done | bytes 294944 | tf_op jit(solution)/shard_map/ppermute | solution.py:25
  59.8 0.8 collective-permute-start.9
  60.6 3.1 %collective-permute-start.6 = (bf16[128,512]{1,0:T(8,128)(2,1)S(1)}, bf16[128,512]{1,0:T(8,128)(2,1)S(1)}, u32[]{:S(2)}, u32[]{:S(2)}) collective-permute-start(bf16[128,512]{1,0:T(8,128)(2,1)S(1)} %get-tuple-element.26), channel_id=1, source_target_pairs={{0,128},{128,0},{1,129},{129,1},{2,130},{130,2},{3,131},{131,3},{4... | collective-permute-start | bytes 393224 | tf_op jit(solution)/shard_map/ppermute | solution.py:25
  63.7 6.7 %collective-permute-done.6.s0 = bf16[128,512]{1,0:T(8,128)(2,1)S(1)} collective-permute-done((bf16[128,512]{1,0:T(8,128)(2,1)S(1)}, bf16[128,512]{1,0:T(8,128)(2,1)S(1)}, u32[]{:S(2)}, u32[]{:S(2)}) %collective-permute-start.6) | collective-permute-done | bytes 131104 | tf_op jit(solution)/shard_map/ppermute | solution.py:25
  71.0 1.0 collective-permute-done.7.s1
  72.0 2.2 %shard_map.87 = bf16[32,160,128]{2,1,0:T(8,128)(2,1)} custom-call(s32[4]{0:T(128)S(1)} %pad_add_fusion.at, bf16[128,512]{1,0:T(8,128)(2,1)S(1)} %collective-permute-done.6.s0, bf16[128,512]{1,0:T(8,128)(2,1)S(1)} %collective-permute-done.7.s1, bf16[128,1152]{1,0:T(8,128)(2,1)S(1)} %collective-permute-done.8.packed, ...), custom_call_target="tpu_custom_call" | custom-call | tf_op jit(solution)/shard_map/pallas_call | solution.py:47
  74.1 7.1 %all-to-all-start.1 = ((bf16[32,160,128]{2,1,0:T(8,128)(2,1)}), bf16[32,160,128]{2,1,0:T(8,128)(2,1)S(1)}, u32[]{:S(2)}, u32[]{:S(2)}) async-start(bf16[32,160,128]{2,1,0:T(8,128)(2,1)} %shard_map.87), calls=%async_computation.1 | async-start | bytes 2621440 | tf_op jit(solution)/shard_map/all_to_all | solution.py:329
  81.3 1.6 %shard_map.86.own_far = bf16[160,32,128]{2,1,0:T(8,128)(2,1)S(1)} custom-call(bf16[32,160,128]{2,1,0:T(8,128)(2,1)S(1)} %all-to-all-done.got), custom_call_target="tpu_custom_call" | custom-call | tf_op jit(solution)/shard_map/pallas_call | solution.py:47
  82.9 1.1 copy-done
  83.9 14.9 %all-to-all-done.1.other = bf16[32,160,128]{2,1,0:T(8,128)(2,1)S(1)} async-done(((bf16[32,160,128]{2,1,0:T(8,128)(2,1)}), bf16[32,160,128]{2,1,0:T(8,128)(2,1)S(1)}, u32[]{:S(2)}, u32[]{:S(2)}) %all-to-all-start.1) | async-done | bytes 1310752 | tf_op jit(solution)/shard_map/all_to_all | solution.py:329
  98.8 4.1 %shard_map.88 = f32[256,128]{1,0:T(8,128)S(1)} custom-call(s32[4]{0:T(128)S(1)} %pad_add_fusion.at, bf16[160,32,128]{2,1,0:T(8,128)(2,1)} %copy-done, bf16[32,160,128]{2,1,0:T(8,128)(2,1)S(1)} %all-to-all-done.1.other), custom_call_target="tpu_custom_call" | custom-call | tf_op jit(solution)/shard_map/pallas_call | solution.py:47
  102.9 24.7 %all_to_all.15 = f32[256,1,128]{2,1,0:T(1,128)S(1)} all-to-all(f32[256,1,128]{2,1,0:T(1,128)S(1)} %bitcast.10), channel_id=1, replica_groups=mesh['zb'=2,'za'=2,'x'=4,'y'=4,'h'=2,'c'=2] {'zb','za','x','y','h','c'}, dimensions={0} | all-to-all | bytes 262144 | tf_op jit(solution)/shard_map/all_to_all | solution.py:340
  127.5 1.2 shard_map.89
  (16 shorter events, 1.1 us)
Async XLA Ops:
  0.0 10.7 %collective-permute-start.2 = (bf16[128,512]{1,0:T(8,128)(2,1)}, bf16[128,512]{1,0:T(8,128)(2,1)S(1)}, u32[]{:S(2)}, u32[]{:S(2)}) collective-permute-start(bf16[128,512]{1,0:T(8,128)(2,1)} %bitcast.12), channel_id=1, source_target_pairs={{0,2},{2,0},{1,3},{3,1},{4,6},{6,4},{5,7},{7,5},{8,10},{10,8},{9,1... | collective-permute-start | bytes 393224 | tf_op jit(solution)/shard_map/ppermute | solution.py:25
  7.7 8.1 %collective-permute-start.4 = (bf16[128,512]{1,0:T(8,128)(2,1)}, bf16[128,512]{1,0:T(8,128)(2,1)S(1)}, u32[]{:S(2)}, u32[]{:S(2)}) collective-permute-start(bf16[128,512]{1,0:T(8,128)(2,1)} %bitcast.15), channel_id=1, source_target_pairs={{0,2},{2,0},{1,3},{3,1},{4,6},{6,4},{5,7},{7,5},{8,10},{10,8},{9,1... | collective-permute-start | bytes 393224 | tf_op jit(solution)/shard_map/ppermute | solution.py:25
  7.7 12.7 %collective-permute-start = (bf16[128,512]{1,0:T(8,128)(2,1)}, bf16[128,512]{1,0:T(8,128)(2,1)S(1)}, u32[]{:S(2)}, u32[]{:S(2)}) collective-permute-start(bf16[128,512]{1,0:T(8,128)(2,1)} %bitcast.13), channel_id=1, source_target_pairs={{0,1},{1,0},{2,3},{3,2},{4,5},{5,4},{6,7},{7,6},{8,9},{9,8},{10,11... | collective-permute-start | bytes 393224 | tf_op jit(solution)/shard_map/ppermute | solution.py:25
  9.1 11.4 %collective-permute-start.1 = (bf16[128,512]{1,0:T(8,128)(2,1)}, bf16[128,512]{1,0:T(8,128)(2,1)S(1)}, u32[]{:S(2)}, u32[]{:S(2)}) collective-permute-start(bf16[128,512]{1,0:T(8,128)(2,1)} %bitcast.16), channel_id=1, source_target_pairs={{0,1},{1,0},{2,3},{3,2},{4,5},{5,4},{6,7},{7,6},{8,9},{9,8},{10,11... | collective-permute-start | bytes 393224 | tf_op jit(solution)/shard_map/ppermute | solution.py:25
  10.7 13.8 %collective-permute-start.3 = (bf16[128,512]{1,0:T(8,128)(2,1)S(1)}, bf16[128,512]{1,0:T(8,128)(2,1)S(1)}, u32[]{:S(2)}, u32[]{:S(2)}) collective-permute-start(bf16[128,512]{1,0:T(8,128)(2,1)S(1)} %collective-permute-done.2.s2), channel_id=1, source_target_pairs={{0,1},{1,0},{2,3},{3,2},{4,5},{5,4},{6,7},{7,6},{8,9},{9,8},{10,11... | collective-permute-start | bytes 393224 | tf_op jit(solution)/shard_map/ppermute | solution.py:25
  15.8 12.2 %collective-permute-start.5 = (bf16[128,512]{1,0:T(8,128)(2,1)S(1)}, bf16[128,512]{1,0:T(8,128)(2,1)S(1)}, u32[]{:S(2)}, u32[]{:S(2)}) collective-permute-start(bf16[128,512]{1,0:T(8,128)(2,1)S(1)} %collective-permute-done.4.c2), channel_id=1, source_target_pairs={{0,1},{1,0},{2,3},{3,2},{4,5},{5,4},{6,7},{7,6},{8,9},{9,8},{10,11... | collective-permute-start | bytes 393224 | tf_op jit(solution)/shard_map/ppermute | solution.py:25
  20.5 4.0 %copy-start.1 = (f32[128,128]{1,0:T(8,128)S(1)}, f32[128,128]{1,0:T(8,128)}, u32[]{:S(2)}) copy-start(f32[128,128]{1,0:T(8,128)} %constant.33.clone.cos_ref) | copy-start | bytes 196612
  20.5 4.0 %copy-start.2 = (f32[128,128]{1,0:T(8,128)S(1)}, f32[128,128]{1,0:T(8,128)}, u32[]{:S(2)}) copy-start(f32[128,128]{1,0:T(8,128)} %constant.34.clone.sine_ref) | copy-start | bytes 196612
  31.4 42.7 %all-to-all-start = ((bf16[32,160,128]{2,1,0:T(8,128)(2,1)}), bf16[32,160,128]{2,1,0:T(8,128)(2,1)S(1)}, u32[]{:S(2)}, u32[]{:S(2)}) async-start(bf16[32,160,128]{2,1,0:T(8,128)(2,1)} %shard_map.85), calls=%async_computation | async-start | bytes 2621440 | tf_op jit(solution)/shard_map/all_to_all | solution.py:323
  39.4 20.4 %collective-permute-start.8 = (bf16[128,1152]{1,0:T(8,128)(2,1)S(1)}, bf16[128,1152]{1,0:T(8,128)(2,1)S(1)}, u32[]{:S(2)}, u32[]{:S(2)}) collective-permute-start(bf16[128,1152]{1,0:T(8,128)(2,1)S(1)} %shard_map.84.packed), channel_id=1, source_target_pairs={{0,128},{128,0},{1,129},{129,1},{2,130},{130,2},{3,131},{131,3},{4... | collective-permute-start | bytes 884744 | tf_op jit(solution)/shard_map/ppermute | solution.py:25
  59.8 12.2 %collective-permute-start.9 = (bf16[128,1152]{1,0:T(8,128)(2,1)S(1)}, bf16[128,1152]{1,0:T(8,128)(2,1)S(1)}, u32[]{:S(2)}, u32[]{:S(2)}) collective-permute-start(bf16[128,1152]{1,0:T(8,128)(2,1)S(1)} %collective-permute-done.8.packed), channel_id=1, source_target_pairs={{0,1},{1,0},{2,3},{3,2},{4,5},{5,4},{6,7},{7,6},{8,9},{9,8},{10,11... | collective-permute-start | bytes 884744 | tf_op jit(solution)/shard_map/ppermute | solution.py:25
  60.6 9.8 %collective-permute-start.6 = (bf16[128,512]{1,0:T(8,128)(2,1)S(1)}, bf16[128,512]{1,0:T(8,128)(2,1)S(1)}, u32[]{:S(2)}, u32[]{:S(2)}) collective-permute-start(bf16[128,512]{1,0:T(8,128)(2,1)S(1)} %get-tuple-element.26), channel_id=1, source_target_pairs={{0,128},{128,0},{1,129},{129,1},{2,130},{130,2},{3,131},{131,3},{4... | collective-permute-start | bytes 393224 | tf_op jit(solution)/shard_map/ppermute | solution.py:25
  70.4 1.6 %collective-permute-start.7 = (bf16[128,512]{1,0:T(8,128)(2,1)S(1)}, bf16[128,512]{1,0:T(8,128)(2,1)S(1)}, u32[]{:S(2)}, u32[]{:S(2)}) collective-permute-start(bf16[128,512]{1,0:T(8,128)(2,1)S(1)} %collective-permute-done.6.s0), channel_id=1, source_target_pairs={{0,1},{1,0},{2,3},{3,2},{4,5},{5,4},{6,7},{7,6},{8,9},{9,8},{10,11... | collective-permute-start | bytes 393224 | tf_op jit(solution)/shard_map/ppermute | solution.py:25
  74.1 24.7 %all-to-all-start.1 = ((bf16[32,160,128]{2,1,0:T(8,128)(2,1)}), bf16[32,160,128]{2,1,0:T(8,128)(2,1)S(1)}, u32[]{:S(2)}, u32[]{:S(2)}) async-start(bf16[32,160,128]{2,1,0:T(8,128)(2,1)} %shard_map.87), calls=%async_computation.1 | async-start | bytes 2621440 | tf_op jit(solution)/shard_map/all_to_all | solution.py:329
  82.9 1.1 copy-start
